TPU v7x, 32 devices: a whole 2x2x4 slice. The times are simulated.
32 devices in a mesh: dp: 2 (over x), seq: 4 (over z), tensor: 4 (over y, core).
Axes of the slice: x: 2, y: 2, z: 4, core: 2. Of those that a mesh axis runs over, the one named last changes fastest.
Arguments:
- tokens: bfloat16 [2, 2, 2048, 512], P(None, 'dp', 'seq'), may hold values from -6 to 6
- document_index: int32 [2, 2, 2048], P(None, 'dp', 'seq'), may hold values from 0 to 2, never falling along the last dimension, each value on 1 to 1280 neighbouring positions
- filters: bfloat16 [24, 2048], P('tensor'), may hold values from -1.1 to 1.1
- stu_gain: float32 [512], replicated, may hold values from 0.5 to 1.5
- filter_proj: bfloat16 [24, 512, 512], P('tensor'), may hold values from -0.0546875 to 0.0546875
- lag_proj: bfloat16 [3, 512, 512], P(None, 'tensor'), may hold values from -0.15625 to 0.15625
- attention_gain: float32 [512], replicated, may hold values from 0.5 to 1.5
- query_weight: bfloat16 [512, 512], P(None, 'tensor'), may hold values from -0.25 to 0.25
- key_weight: bfloat16 [512, 512], P(None, 'tensor'), may hold values from -0.25 to 0.25
- value_weight: bfloat16 [512, 512], P(None, 'tensor'), may hold values from -0.25 to 0.25
- output_weight: bfloat16 [512, 512], P('tensor'), may hold values from -3 to 3
- feed_gain: float32 [512], replicated, may hold values from 0.5 to 1.5
- gate_weight: bfloat16 [512, 2048], P(None, 'tensor'), may hold values from -0.25 to 0.25
- up_weight: bfloat16 [512, 2048], P(None, 'tensor'), may hold values from -0.25 to 0.25
- down_weight: bfloat16 [2048, 512], P('tensor'), may hold values from -0.125 to 0.125
- cotangent: bfloat16 [2, 2, 2048, 512], P(None, 'dp', 'seq'), may hold values from -6 to 6
Outputs:
- layer_output: bfloat16 [2, 2, 2048, 512], P(None, 'dp', 'seq')
- input_gradient: bfloat16 [2, 2, 2048, 512], P(None, 'dp', 'seq')
- stu_gain_grad: float32 [512], P('seq')
- filter_proj_grad: float32 [24, 512, 512], P('tensor', 'seq')
- lag_proj_grad: float32 [3, 512, 512], P(None, 'tensor', 'seq')
- attention_gain_grad: float32 [512], P('seq')
- query_grad: float32 [512, 512], P('seq', 'tensor')
- key_grad: float32 [512, 512], P('seq', 'tensor')
- value_grad: float32 [512, 512], P('seq', 'tensor')
- output_grad: float32 [512, 512], P('tensor', 'seq')
- feed_gain_grad: float32 [512], P('seq')
- gate_grad: float32 [512, 2048], P('seq', 'tensor')
- up_grad: float32 [512, 2048], P('seq', 'tensor')
- down_grad: float32 [2048, 512], P('tensor', 'seq')
Inputs may be any that keep to these rules, and one draw needn't show every extreme that they name: `document_index`: along each row of 2048 tokens the ids never fall; each id marks one contiguous document.
All inputs are finite; a program needn't handle non-finite values.
Results may differ from a plain program's by a relative error of at most 0.017.
Values may be sent and summed in bfloat16 or wider, within the bound.
A program may use at most 384 MiB of HBM per device.

v0:
```python
import jax
import jax.numpy as jnp
from jax import lax
from jax.sharding import PartitionSpec as P

HD = 64
WINDOW = 1024


EPSILON = 1e-05


def shifted(block, axis, distance):
    devices = range(lax.axis_size(axis))
    route = [(i - distance, i) for i in devices if i - distance in devices]
    return lax.ppermute(block, axis, route)


def rms_scale(values, gain_vec):
    inverse = lax.rsqrt(jnp.mean(values * values, axis=-1, keepdims=True) + EPSILON)
    return values * inverse * gain_vec


def norm_back(values, gain_vec, grad_out):
    final_output, backward_function = jax.vjp(rms_scale, values, gain_vec)
    return backward_function(grad_out)


def gated_unit(gate_pre, up_pre):
    return jax.nn.gelu(gate_pre, approximate=True) * up_pre


def tensor_total(partial_value):
    return lax.psum(partial_value, "tensor")


def skew_tiles(filters, block_rows, block_count):
    filter_rows = filters.shape[0]
    padded = jnp.concatenate([jnp.zeros((filter_rows, block_rows), filters.dtype), filters], axis=1)
    lower_half = padded[:, : block_count * block_rows].reshape(filter_rows, block_count, block_rows)
    upper_half = padded[:, block_rows : block_rows + block_count * block_rows].reshape(
        filter_rows, block_count, block_rows
    )
    strip = jnp.concatenate([lower_half, upper_half], axis=2)
    reordered = jnp.concatenate(
        [
            jnp.flip(strip[:, :, : block_rows + 1], axis=2),
            jnp.flip(strip[:, :, block_rows + 1 :], axis=2),
        ],
        axis=2,
    )
    repeated = jnp.tile(reordered, (1, 1, block_rows))
    skewed = repeated[:, :, : block_rows * (2 * block_rows - 1)].reshape(
        filter_rows, block_count, block_rows, 2 * block_rows - 1
    )
    return skewed[:, :, :, :block_rows]


def local(
    tokens,
    document_index,
    filters,
    stu_gain,
    filter_proj,
    lag_proj,
    attention_gain,
    query_weight,
    key_weight,
    value_weight,
    output_weight,
    feed_gain,
    gate_weight,
    up_weight,
    down_weight,
    cotangent,
):
    micro_count = tokens.shape[0]
    local_len = tokens.shape[2]
    model_width = tokens.shape[3]
    seq_count = lax.axis_size("seq")
    seq_place = lax.axis_index("seq")
    row_len = local_len * seq_count
    filter_count = filters.shape[0]
    lag_order = lag_proj.shape[0]
    chan_width = lag_proj.shape[1]
    chan_start = lax.axis_index("tensor") * chan_width
    local_heads = query_weight.shape[1] // HD
    hop_count = WINDOW // local_len
    score_scale = HD ** (-0.5)
    positions = seq_place * local_len + jnp.arange(local_len, dtype=jnp.int32)
    shard_tiles = skew_tiles(filters, local_len, seq_count)
    shard_table = jnp.concatenate(
        [
            jnp.flip(shard_tiles, axis=1),
            jnp.zeros((filter_count, seq_count - 1, local_len, local_len), filters.dtype),
        ],
        axis=1,
    )
    filter_acc = jnp.zeros(filter_proj.shape, jnp.float32)
    lag_acc = jnp.zeros(lag_proj.shape, jnp.float32)
    query_acc = jnp.zeros(query_weight.shape, jnp.float32)
    key_acc = jnp.zeros(key_weight.shape, jnp.float32)
    value_acc = jnp.zeros(value_weight.shape, jnp.float32)
    output_acc = jnp.zeros(output_weight.shape, jnp.float32)
    gate_acc = jnp.zeros(gate_weight.shape, jnp.float32)
    up_acc = jnp.zeros(up_weight.shape, jnp.float32)
    down_acc = jnp.zeros(down_weight.shape, jnp.float32)
    stu_gain_acc = jnp.zeros(stu_gain.shape, jnp.float32)
    attn_gain_acc = jnp.zeros(stu_gain.shape, jnp.float32)
    feed_gain_acc = jnp.zeros(stu_gain.shape, jnp.float32)
    out_rows = []
    grad_rows = []
    for mb_index in range(micro_count):
        row_tokens = tokens[mb_index, 0].astype(jnp.float32)
        row_ids = document_index[mb_index, 0]
        inputs = rms_scale(row_tokens, stu_gain).astype(jnp.bfloat16)
        id_table = jnp.zeros((row_len,), jnp.int32)
        source_rows = lax.all_gather(inputs, "seq", axis=0, tiled=True)
        source_ids = lax.all_gather(row_ids, "seq", axis=0, tiled=True)
        shard_span = source_rows.shape[0] // local_len
        table_start = seq_count - 1 - seq_place
        tiles = lax.dynamic_slice_in_dim(shard_table, table_start, shard_span, 1)
        add_matches = row_ids[None, :, None] == source_ids.reshape(shard_span, 1, local_len)
        coeffs = jnp.where(add_matches[None], tiles, jnp.zeros((), tiles.dtype))
        running_sum = jnp.einsum(
            "kqij,qjd->kid",
            coeffs,
            source_rows.reshape(shard_span, local_len, model_width),
            preferred_element_type=jnp.float32,
        )
        id_table = lax.dynamic_update_slice_in_dim(id_table, source_ids, jnp.int32(0), 0)
        conv_out = running_sum.astype(jnp.bfloat16)
        own_chan = lax.dynamic_slice_in_dim(inputs, chan_start, chan_width, 1)
        tail_vals, tail_ids = shifted(
            (own_chan[local_len - lag_order :], row_ids[local_len - lag_order :]), "seq", 1
        )
        ext_vals = jnp.concatenate([tail_vals, own_chan], axis=0)
        ext_ids = jnp.concatenate([tail_ids, row_ids], axis=0)
        lag_masks = []
        lagged_list = []
        for lag_step in range(1, lag_order + 1):
            low_edge = lag_order - lag_step
            matches = ext_ids[low_edge : low_edge + local_len] == row_ids
            lag_masks.append(matches)
            lagged_list.append(
                jnp.where(
                    matches[:, None],
                    ext_vals[low_edge : low_edge + local_len],
                    jnp.zeros((), jnp.bfloat16),
                )
            )
        lag_stack = jnp.stack(lagged_list)
        mixed_sum = jnp.einsum(
            "ktd,kde->te", conv_out, filter_proj, preferred_element_type=jnp.float32
        )
        mixed_sum = mixed_sum + jnp.einsum(
            "itc,ice->te", lag_stack, lag_proj, preferred_element_type=jnp.float32
        )
        hidden_one = row_tokens + tensor_total(mixed_sum)
        attn_in = rms_scale(hidden_one, attention_gain).astype(jnp.bfloat16)
        queries = jnp.dot(attn_in, query_weight, preferred_element_type=jnp.float32).astype(
            jnp.bfloat16
        )
        key_rows = jnp.dot(attn_in, key_weight, preferred_element_type=jnp.float32).astype(
            jnp.bfloat16
        )
        value_rows = jnp.dot(attn_in, value_weight, preferred_element_type=jnp.float32).astype(
            jnp.bfloat16
        )
        key_parts = []
        value_parts = []
        id_parts = []
        pos_parts = []
        for hop_step in range(hop_count, 0, -1):
            moved_keys, moved_values, moved_ids = shifted(
                (key_rows, value_rows, row_ids), "seq", hop_step
            )
            key_parts.append(moved_keys)
            value_parts.append(moved_values)
            id_parts.append(moved_ids)
            pos_parts.append(positions - hop_step * local_len)
        key_parts.append(key_rows)
        value_parts.append(value_rows)
        id_parts.append(row_ids)
        pos_parts.append(positions)
        key_ids = jnp.concatenate(id_parts)
        key_pos = jnp.concatenate(pos_parts)
        allowed = (
            (key_ids[None, :] == row_ids[:, None])
            & (key_pos[None, :] <= positions[:, None])
            & (positions[:, None] - key_pos[None, :] < WINDOW)
            & (key_pos[None, :] >= 0)
        )
        query_heads = queries.reshape(local_len, local_heads, HD)
        key_heads = jnp.concatenate(key_parts).reshape(-1, local_heads, HD)
        value_heads = jnp.concatenate(value_parts).reshape(-1, local_heads, HD)
        scores = (
            jnp.einsum("qhd,khd->hqk", query_heads, key_heads, preferred_element_type=jnp.float32)
            * score_scale
        )
        scores = jnp.where(allowed[None], scores, -1e30)
        row_peak = jnp.max(scores, axis=-1, keepdims=True)
        exp_scores = jnp.exp(scores - row_peak)
        denominator = jnp.sum(exp_scores, axis=-1, keepdims=True)
        log_total = row_peak + jnp.log(denominator)
        prob_low = (exp_scores / denominator).astype(jnp.bfloat16)
        attended = jnp.einsum(
            "hqk,khd->qhd", prob_low, value_heads, preferred_element_type=jnp.float32
        )
        attended = attended.reshape(local_len, local_heads * HD).astype(jnp.bfloat16)
        hidden_two = hidden_one + tensor_total(
            jnp.dot(attended, output_weight, preferred_element_type=jnp.float32)
        )
        feed_in = rms_scale(hidden_two, feed_gain).astype(jnp.bfloat16)
        gate_pre = jnp.dot(feed_in, gate_weight, preferred_element_type=jnp.float32)
        up_pre = jnp.dot(feed_in, up_weight, preferred_element_type=jnp.float32)
        inner_act = gated_unit(gate_pre, up_pre).astype(jnp.bfloat16)
        layer_rows = hidden_two + tensor_total(
            jnp.dot(inner_act, down_weight, preferred_element_type=jnp.float32)
        )
        out_rows.append(layer_rows.astype(jnp.bfloat16))
        grad_out = cotangent[mb_index, 0].astype(jnp.float32)
        grad_three = cotangent[mb_index, 0]
        down_acc = down_acc + jnp.einsum(
            "tf,te->fe", inner_act, grad_three, preferred_element_type=jnp.float32
        )
        grad_inner = jnp.einsum(
            "te,fe->tf", grad_three, down_weight, preferred_element_type=jnp.float32
        )
        unit_out, unit_pull = jax.vjp(gated_unit, gate_pre, up_pre)
        grad_gate, grad_up = unit_pull(grad_inner)
        grad_gate = grad_gate.astype(jnp.bfloat16)
        grad_up = grad_up.astype(jnp.bfloat16)
        gate_acc = gate_acc + jnp.einsum(
            "td,tf->df", feed_in, grad_gate, preferred_element_type=jnp.float32
        )
        up_acc = up_acc + jnp.einsum(
            "td,tf->df", feed_in, grad_up, preferred_element_type=jnp.float32
        )
        grad_feed = tensor_total(
            jnp.einsum("tf,df->td", grad_gate, gate_weight, preferred_element_type=jnp.float32)
            + jnp.einsum("tf,df->td", grad_up, up_weight, preferred_element_type=jnp.float32)
        )
        grad_two_in, gain_grad = norm_back(hidden_two, feed_gain, grad_feed)
        feed_gain_acc = feed_gain_acc + gain_grad
        grad_two = grad_out + grad_two_in
        grad_att_out = grad_two.astype(jnp.bfloat16)
        output_acc = output_acc + jnp.einsum(
            "tc,te->ce", attended, grad_att_out, preferred_element_type=jnp.float32
        )
        grad_attended = jnp.einsum(
            "te,ce->tc", grad_att_out, output_weight, preferred_element_type=jnp.float32
        ).astype(jnp.bfloat16)
        grad_heads = grad_attended.reshape(local_len, local_heads, HD)
        scores = (
            jnp.einsum("qhd,khd->hqk", query_heads, key_heads, preferred_element_type=jnp.float32)
            * score_scale
        )
        prob_full = jnp.where(allowed[None], jnp.exp(scores - log_total), 0.0)
        prob_low = prob_full.astype(jnp.bfloat16)
        grad_prob = jnp.einsum(
            "qhd,khd->hqk", grad_heads, value_heads, preferred_element_type=jnp.float32
        )
        grad_scores = prob_full * (
            grad_prob - jnp.sum(prob_full * grad_prob, axis=-1, keepdims=True)
        )
        grad_scores = grad_scores.astype(jnp.bfloat16)
        grad_queries = (
            jnp.einsum("hqk,khd->qhd", grad_scores, key_heads, preferred_element_type=jnp.float32)
            * score_scale
        )
        grad_queries = grad_queries.reshape(local_len, local_heads * HD).astype(jnp.bfloat16)
        grad_key_all = (
            jnp.einsum("hqk,qhd->khd", grad_scores, query_heads, preferred_element_type=jnp.float32)
            * score_scale
        )
        grad_value_all = jnp.einsum(
            "hqk,qhd->khd", prob_low, grad_heads, preferred_element_type=jnp.float32
        )
        grad_key_all = grad_key_all.reshape(-1, local_heads * HD)
        grad_value_all = grad_value_all.reshape(-1, local_heads * HD)
        grad_keys = grad_key_all[hop_count * local_len :]
        grad_values = grad_value_all[hop_count * local_len :]
        for hop_step in range(hop_count, 0, -1):
            slot_start = (hop_count - hop_step) * local_len
            back_keys, back_values = shifted(
                (
                    grad_key_all[slot_start : slot_start + local_len],
                    grad_value_all[slot_start : slot_start + local_len],
                ),
                "seq",
                -hop_step,
            )
            grad_keys = grad_keys + back_keys
            grad_values = grad_values + back_values
        grad_keys = grad_keys.astype(jnp.bfloat16)
        grad_values = grad_values.astype(jnp.bfloat16)
        query_acc = query_acc + jnp.einsum(
            "td,tc->dc", attn_in, grad_queries, preferred_element_type=jnp.float32
        )
        key_acc = key_acc + jnp.einsum(
            "td,tc->dc", attn_in, grad_keys, preferred_element_type=jnp.float32
        )
        value_acc = value_acc + jnp.einsum(
            "td,tc->dc", attn_in, grad_values, preferred_element_type=jnp.float32
        )
        grad_attn_in = tensor_total(
            jnp.einsum("tc,dc->td", grad_queries, query_weight, preferred_element_type=jnp.float32)
            + jnp.einsum("tc,dc->td", grad_keys, key_weight, preferred_element_type=jnp.float32)
            + jnp.einsum("tc,dc->td", grad_values, value_weight, preferred_element_type=jnp.float32)
        )
        grad_one_in, gain_grad = norm_back(hidden_one, attention_gain, grad_attn_in)
        attn_gain_acc = attn_gain_acc + gain_grad
        grad_one = grad_two + grad_one_in
        grad_stu = grad_one.astype(jnp.bfloat16)
        filter_acc = filter_acc + jnp.einsum(
            "ktd,te->kde", conv_out, grad_stu, preferred_element_type=jnp.float32
        )
        lag_acc = lag_acc + jnp.einsum(
            "itc,te->ice", lag_stack, grad_stu, preferred_element_type=jnp.float32
        )
        grad_conv = jnp.einsum(
            "te,kde->ktd", grad_stu, filter_proj, preferred_element_type=jnp.float32
        ).astype(jnp.bfloat16)
        grad_lagged = jnp.einsum(
            "te,ice->itc", grad_stu, lag_proj, preferred_element_type=jnp.float32
        )
        source_shard_span = local_len * lax.axis_size("seq") // local_len
        source_table_start = seq_count - 1 - seq_place
        source_tiles = lax.dynamic_slice_in_dim(
            shard_table, source_table_start, source_shard_span, 1
        )
        source_matches = row_ids[None, :, None] == id_table.reshape(source_shard_span, 1, local_len)
        source_coeffs = jnp.where(
            source_matches[None], source_tiles, jnp.zeros((), source_tiles.dtype)
        )
        terms = jnp.einsum(
            "kqij,kid->qjd", source_coeffs, grad_conv, preferred_element_type=jnp.float32
        )
        grad_inputs = lax.psum_scatter(
            terms.reshape(local_len * lax.axis_size("seq"), model_width).astype(jnp.bfloat16),
            "seq",
            scatter_dimension=0,
            tiled=True,
        ).astype(jnp.float32)
        ext_grad = jnp.zeros((lag_order + local_len, chan_width), jnp.float32)
        for lag_step in range(1, lag_order + 1):
            low_edge = lag_order - lag_step
            masked_grad = jnp.where(
                lag_masks[lag_step - 1][:, None], grad_lagged[lag_step - 1], 0.0
            )
            ext_grad = ext_grad.at[low_edge : low_edge + local_len].add(masked_grad)
        tail_grad = shifted(ext_grad[:lag_order], "seq", -1)
        own_grad = ext_grad[lag_order:].at[local_len - lag_order :].add(tail_grad)
        chan_grad = lax.dynamic_slice_in_dim(grad_inputs, chan_start, chan_width, 1) + own_grad
        grad_inputs = lax.dynamic_update_slice_in_dim(grad_inputs, chan_grad, chan_start, 1)
        grad_norm_in = tensor_total(grad_inputs)
        grad_zero_in, gain_grad = norm_back(row_tokens, stu_gain, grad_norm_in)
        stu_gain_acc = stu_gain_acc + gain_grad
        grad_rows.append((grad_one + grad_zero_in).astype(jnp.bfloat16))
    scattered = (
        lax.psum_scatter(filter_acc, "seq", scatter_dimension=1, tiled=True),
        lax.psum_scatter(lag_acc, "seq", scatter_dimension=2, tiled=True),
        lax.psum_scatter(query_acc, "seq", scatter_dimension=0, tiled=True),
        lax.psum_scatter(key_acc, "seq", scatter_dimension=0, tiled=True),
        lax.psum_scatter(value_acc, "seq", scatter_dimension=0, tiled=True),
        lax.psum_scatter(output_acc, "seq", scatter_dimension=1, tiled=True),
        lax.psum_scatter(gate_acc, "seq", scatter_dimension=0, tiled=True),
        lax.psum_scatter(up_acc, "seq", scatter_dimension=0, tiled=True),
        lax.psum_scatter(down_acc, "seq", scatter_dimension=1, tiled=True),
        lax.psum_scatter(stu_gain_acc, "seq", scatter_dimension=0, tiled=True),
        lax.psum_scatter(attn_gain_acc, "seq", scatter_dimension=0, tiled=True),
        lax.psum_scatter(feed_gain_acc, "seq", scatter_dimension=0, tiled=True),
    )
    summed = lax.psum(
        (
            scattered[0],
            scattered[1],
            scattered[2],
            scattered[3],
            scattered[4],
            scattered[5],
            scattered[6],
            scattered[7],
            scattered[8],
            scattered[9],
            scattered[10],
            scattered[11],
        ),
        "dp",
    )
    layer_output = jnp.stack(out_rows)[:, None]
    input_gradient = jnp.stack(grad_rows)[:, None]
    return (
        layer_output,
        input_gradient,
        summed[9],
        summed[0],
        summed[1],
        summed[10],
        summed[2],
        summed[3],
        summed[4],
        summed[5],
        summed[11],
        summed[6],
        summed[7],
        summed[8],
    )


def solution(mesh):
    return jax.shard_map(
        local,
        mesh=mesh,
        in_specs=(
            P(None, "dp", "seq", None),
            P(None, "dp", "seq"),
            P("tensor", None),
            P(),
            P("tensor", None, None),
            P(None, "tensor", None),
            P(),
            P(None, "tensor"),
            P(None, "tensor"),
            P(None, "tensor"),
            P("tensor", None),
            P(),
            P(None, "tensor"),
            P(None, "tensor"),
            P("tensor", None),
            P(None, "dp", "seq", None),
        ),
        out_specs=(
            P(None, "dp", "seq", None),
            P(None, "dp", "seq", None),
            P("seq"),
            P("tensor", "seq", None),
            P(None, "tensor", "seq"),
            P("seq"),
            P("seq", "tensor"),
            P("seq", "tensor"),
            P("seq", "tensor"),
            P("tensor", "seq"),
            P("seq"),
            P("seq", "tensor"),
            P("seq", "tensor"),
            P("tensor", "seq"),
        ),
        check_vma=False,
    )
```

profile of v0, /device:TPU:0, one launch (start us, length us, event | category | flops | bytes accessed | tf_op | source)
XLA Modules:
  0.0 1232.3 jit_solution(9163998885472126408)
XLA Ops:
  13.3 6.5 collective-permute-start.4
  19.8 4.1 collective-permute-start.5
  30.9 12.5 %all-gather = s32[1,1,2048]{2,1,0:T(1,128)S(1)} all-gather(s32[1,1,512]{2,1,0:T(1,128)S(1)} %get-tuple-element.249), channel_id=2, replica_groups=mesh['dp'=2,'seq'=4,'tensor'=4] {'seq'}, dimensions={2}, use_global_device_ids=true | all-gather | bytes 10240 | tf_op jit(solution)/shard_map/all_gather | solution.py:119
  49.3 12.3 all-gather.1
  66.4 8.5 tile.4
  74.9 24.9 %tile.10 = bf16[6,4,524288]{2,1,0:T(4,128)(2,1)} reshape(bf16[6,4,512,1024]{3,2,1,0:T(8,128)(2,1)} %tile.4) | data formatting | bytes 50331648 | tf_op jit(solution)/shard_map/tile | solution.py:52
  99.8 17.2 %slice.413 = bf16[6,4,523776]{2,1,0:T(4,128)(2,1)} slice(bf16[6,4,524288]{2,1,0:T(4,128)(2,1)} %tile.10), slice={[0:6], [0:4], [0:523776]} | slice | bytes 50282496 | tf_op jit(solution)/shard_map/slice | solution.py:53
  117.0 47.1 %reshape.672 = bf16[6,4,512,1023]{3,2,1,0:T(8,128)(2,1)} reshape(bf16[6,4,523776]{2,1,0:T(4,128)(2,1)} %slice.413) | data formatting | bytes 50282496 | tf_op jit(solution)/shard_map/reshape | solution.py:53
  164.1 10.4 slice.414
  174.5 10.6 rev.14
  190.2 4.2 collective-permute-start.1
  195.6 4.2 collective-permute-start.9
  202.1 9.2 bitcast_convert_fusion.1
  215.8 9.1 bitcast_convert_fusion
  233.3 3.2 fusion.22
  236.5 49.0 %all-reduce.30.cloned.1.call-done = (f32[512,512]{1,0:T(8,128)}, f32[512,512]{1,0:T(8,128)}) async-done(((f32[512,512]{1,0:T(8,128)}, f32[512,512]{1,0:T(8,128)}), (f32[512,512]{1,0:T(8,128)}, f32[512,512]{1,0:T(8,128)})) %all-reduce.30.cloned.1.call-update) | async-done | bytes 2097168 | tf_op jit(solution)/shard_map/psum | solution.py:34
  290.0 4.3 collective-permute-start.6
  294.3 3.4 collective-permute-start.7
  300.6 12.4 %collective-permute-start.3 = (bf16[512,128]{1,0:T(8,128)(2,1)}, bf16[512,128]{1,0:T(8,128)(2,1)}, u32[]{:S(2)}, u32[]{:S(2)}) collective-permute-start(bf16[512,128]{1,0:T(8,128)(2,1)} %convolution_convert_fusion.7), channel_id=1, source_target_pairs={{0,4},{4,8},{8,12},{1,5},{5,9},{9,13},{2,6},{6,10},{10,14},{3,7},{... | collective-permute-start | bytes 393224 | tf_op jit(solution)/shard_map/ppermute | solution.py:16
  354.8 48.8 %all-reduce.28.cloned.1.call-done = (f32[512,512]{1,0:T(8,128)}, f32[512,512]{1,0:T(8,128)}) async-done(((f32[512,512]{1,0:T(8,128)}, f32[512,512]{1,0:T(8,128)}), (f32[512,512]{1,0:T(8,128)}, f32[512,512]{1,0:T(8,128)})) %all-reduce.28.cloned.1.call-update) | async-done | bytes 2097168 | tf_op jit(solution)/shard_map/psum | solution.py:34
  420.8 49.9 %all-reduce.26.cloned.1.call-done = (f32[512,512]{1,0:T(8,128)}, f32[512,512]{1,0:T(8,128)}) async-done(((f32[512,512]{1,0:T(8,128)}, f32[512,512]{1,0:T(8,128)}), (f32[512,512]{1,0:T(8,128)}, f32[512,512]{1,0:T(8,128)})) %all-reduce.26.cloned.1.call-update) | async-done | bytes 2097168 | tf_op jit(solution)/shard_map/psum | solution.py:34
  470.8 3.5 multiply_reduce_fusion.3
  475.7 3.2 fusion.72
  506.3 38.0 %collective-permute-done.16 = f32[512,128]{0,1:T(8,128)S(1)} collective-permute-done((f32[512,128]{0,1:T(8,128)S(1)}, f32[512,128]{0,1:T(8,128)S(1)}, u32[]{:S(2)}, u32[]{:S(2)}) %collective-permute-start.16) | collective-permute-done | bytes 262176 | tf_op jit(solution)/shard_map/ppermute | solution.py:16
  548.6 3.9 collective-permute-done.19
  553.9 12.8 %collective-permute-done.21 = f32[512,128]{0,1:T(8,128)S(1)} collective-permute-done((f32[512,128]{0,1:T(8,128)S(1)}, f32[512,128]{0,1:T(8,128)S(1)}, u32[]{:S(2)}, u32[]{:S(2)}) %collective-permute-start.21) | collective-permute-done | bytes 262176 | tf_op jit(solution)/shard_map/ppermute | solution.py:16
  569.8 53.4 %all-reduce.24.cloned.1.call-done = (f32[512,512]{1,0:T(8,128)}, f32[512,512]{1,0:T(8,128)}) async-done(((f32[512,512]{1,0:T(8,128)}, f32[512,512]{1,0:T(8,128)}), (f32[512,512]{1,0:T(8,128)}, f32[512,512]{1,0:T(8,128)})) %all-reduce.24.cloned.1.call-update) | async-done | bytes 2097168 | tf_op jit(solution)/shard_map/psum | solution.py:34
  623.1 3.4 multiply_reduce_fusion.5
  626.5 5.0 fusion.178
  631.5 12.6 %bitcast_convert_fusion.3 = bf16[4,512,512]{2,1,0:T(8,128)(2,1)} fusion(bf16[6,512,512]{2,1,0:T(8,128)(2,1)S(1)} %copy-done, pred[4,512,512]{2,1,0:T(8,128)(4,1)} %broadcast_compare_fusion.1, bf16[512,512]{1,0:T(8,128)(2,1)} %get-tuple-element.195, s32[]{:T(128)S(6)} %select_n.74, bf16[6,4,512,512]{3,2,1,0:T(8,128)(2,1)} %rev.14), kind=kOutput, calls=%fused_computation.28 | convolution fusion | flops 8061976576 | bytes 19398660 | tf_op jit(solution)/shard_map/kqij,kid->qjd/dot_general | solution.py:337
  644.4 12.6 %bitcast_convert_fusion.2 = bf16[4,512,512]{2,1,0:T(8,128)(2,1)} fusion(bf16[6,512,512]{2,1,0:T(8,128)(2,1)S(1)} %copy-done, pred[4,512,512]{2,1,0:T(8,128)(4,1)} %broadcast_compare_fusion, bf16[512,512]{1,0:T(8,128)(2,1)} %get-tuple-element.251, s32[]{:T(128)S(6)} %select_n.74, bf16[6,4,512,512]{3,2,1,0:T(8,128)(2,1)} %rev.14), kind=kOutput, calls=%fused_computation.27 | convolution fusion | flops 8061976576 | bytes 19398660 | tf_op jit(solution)/shard_map/kqij,kid->qjd/dot_general | solution.py:337
  689.5 4.0 fusion.98
  693.5 4.4 convolution_add_fusion
  726.7 3.5 collective-permute-done.25
  741.6 15.7 %reduce-scatter.26.cloned.1.call-done = f32[128,128]{1,0:T(8,128)} async-done(((f32[128,512]{1,0:T(8,128)}), f32[128,128]{1,0:T(8,128)}) %reduce-scatter.26.cloned.1.call-update) | async-done | bytes 65552 | tf_op jit(solution)/shard_map/reduce_scatter | solution.py:367
  757.4 20.9 %reduce-scatter.20.cloned.1.call-done = f32[128,128]{1,0:T(8,128)} async-done(((f32[512,128]{1,0:T(8,128)}), f32[128,128]{1,0:T(8,128)}) %reduce-scatter.20.cloned.1.call-update) | async-done | bytes 65552 | tf_op jit(solution)/shard_map/reduce_scatter | solution.py:364
  778.3 20.5 %reduce-scatter.24.cloned.1.call-done = f32[128,128]{1,0:T(8,128)} async-done(((f32[512,128]{1,0:T(8,128)}), f32[128,128]{1,0:T(8,128)}) %reduce-scatter.24.cloned.1.call-update) | async-done | bytes 65552 | tf_op jit(solution)/shard_map/reduce_scatter | solution.py:366
  798.8 20.4 %reduce-scatter.22.cloned.1.call-done = f32[128,128]{1,0:T(8,128)} async-done(((f32[512,128]{1,0:T(8,128)}), f32[128,128]{1,0:T(8,128)}) %reduce-scatter.22.cloned.1.call-update) | async-done | bytes 65552 | tf_op jit(solution)/shard_map/reduce_scatter | solution.py:365
  819.2 27.8 %reduce-scatter.32.cloned.1.call-done = f32[512,128]{1,0:T(8,128)} async-done(((f32[512,512]{1,0:T(8,128)}), f32[512,128]{1,0:T(8,128)}) %reduce-scatter.32.cloned.1.call-update) | async-done | bytes 262160 | tf_op jit(solution)/shard_map/reduce_scatter | solution.py:370
  847.0 28.0 %reduce-scatter.30.cloned.1.call-done = f32[128,512]{1,0:T(8,128)} async-done(((f32[512,512]{1,0:T(8,128)}), f32[128,512]{1,0:T(8,128)}) %reduce-scatter.30.cloned.1.call-update) | async-done | bytes 262160 | tf_op jit(solution)/shard_map/reduce_scatter | solution.py:369
  874.9 27.9 %reduce-scatter.28.cloned.1.call-done = f32[128,512]{1,0:T(8,128)} async-done(((f32[512,512]{1,0:T(8,128)}), f32[128,512]{1,0:T(8,128)}) %reduce-scatter.28.cloned.1.call-update) | async-done | bytes 262160 | tf_op jit(solution)/shard_map/reduce_scatter | solution.py:368
  902.9 23.9 %reduce-scatter.18.cloned.1.call-done = f32[3,128,128]{2,1,0:T(8,128)} async-done(((f32[3,128,512]{2,1,0:T(8,128)}), f32[3,128,128]{2,1,0:T(8,128)}) %reduce-scatter.18.cloned.1.call-update) | async-done | bytes 196624 | tf_op jit(solution)/shard_map/reduce_scatter | solution.py:363
  926.8 112.4 %reduce-scatter.16.cloned.1.call-done = f32[6,128,512]{2,1,0:T(8,128)} async-done(((f32[6,512,512]{2,1,0:T(8,128)}), f32[6,128,512]{2,1,0:T(8,128)}) %reduce-scatter.16.cloned.1.call-update) | async-done | bytes 1572880 | tf_op jit(solution)/shard_map/reduce_scatter | solution.py:362
  1040.6 87.7 %all-reduce.22.cloned.1.call-done = (f32[512,512]{1,0:T(8,128)}, f32[512,512]{1,0:T(8,128)}, f32[512,512]{1,0:T(8,128)}, f32[512,512]{1,0:T(8,128)}) async-done(((f32[512,512]{1,0:T(8,128)}, f32[512,512]{1,0:T(8,128)}, f32[512,512]{1,0:T(8,128)}, f32[512,512]{1,0:T(8,128)}), (f32[512,512]{1,0:T(8,128)}, f32[512,512]{1,0:T(8,128)}, f32[512,512]{1,0:T(8,128)}, ...) | async-done | bytes 4194320 | tf_op jit(solution)/shard_map/psum | solution.py:34
  1131.1 11.8 all-reduce.12
  1143.1 5.6 all-reduce.13
  1148.8 3.2 fusion.87
  1154.7 55.4 %all-reduce.32.cloned.1.call-done = (f32[6,128,512]{2,1,0:T(8,128)}, f32[3,128,128]{2,1,0:T(8,128)}, f32[128,128]{1,0:T(8,128)}, f32[128,128]{1,0:T(8,128)}, f32...) async-done(((f32[6,128,512]{2,1,0:T(8,128)}, f32[3,128,128]{2,1,0:T(8,128)}, f32[128,128]{1,0:T(8,128)}, ...) | async-done | bytes 2818064 | tf_op jit(solution)/shard_map/psum | solution.py:375
  (499 shorter events, 241.9 us)
Async XLA Ops:
  7.2 194.9 %all-gather.5.cloned.1.call-start = ((), (), s32[]{:S(2)}) async-start(), calls=%async_computation.11 | async-start | bytes 2621440 | tf_op jit(solution)/shard_map/all_gather | solution.py:118
  12.5 203.3 %all-gather.7.cloned.1.call-start = ((), (), s32[]{:S(2)}) async-start(), calls=%async_computation.12 | async-start | bytes 2621440 | tf_op jit(solution)/shard_map/all_gather | solution.py:118
  13.3 218.6 %collective-permute-start.4 = (s32[512]{0:T(512)S(1)}, s32[512]{0:T(512)}, u32[]{:S(2)}, u32[]{:S(2)}) collective-permute-start(s32[512]{0:T(512)S(1)} %bitcast.386), channel_id=1, source_target_pairs={{0,8},{4,12},{1,9},{5,13},{2,10},{6,14},{3,11},{7,15},{16,24},{20,... | collective-permute-start | bytes 6152 | tf_op jit(solution)/shard_map/ppermute | solution.py:16
  19.8 212.1 %collective-permute-start.5 = (s32[512]{0:T(512)S(1)}, s32[512]{0:T(512)}, u32[]{:S(2)}, u32[]{:S(2)}) collective-permute-start(s32[512]{0:T(512)S(1)} %bitcast.387), channel_id=1, source_target_pairs={{0,4},{4,8},{8,12},{1,5},{5,9},{9,13},{2,6},{6,10},{10,14},{3,7},{... | collective-permute-start | bytes 6152 | tf_op jit(solution)/shard_map/ppermute | solution.py:16
  23.8 208.8 %collective-permute-start.12 = (s32[512]{0:T(512)S(1)}, s32[512]{0:T(512)}, u32[]{:S(2)}, u32[]{:S(2)}) collective-permute-start(s32[512]{0:T(512)S(1)} %bitcast.393), channel_id=1, source_target_pairs={{0,8},{4,12},{1,9},{5,13},{2,10},{6,14},{3,11},{7,15},{16,24},{20,... | collective-permute-start | bytes 6152 | tf_op jit(solution)/shard_map/ppermute | solution.py:16
  25.7 206.9 %collective-permute-start.13 = (s32[512]{0:T(512)S(1)}, s32[512]{0:T(512)}, u32[]{:S(2)}, u32[]{:S(2)}) collective-permute-start(s32[512]{0:T(512)S(1)} %bitcast.394), channel_id=1, source_target_pairs={{0,4},{4,8},{8,12},{1,5},{5,9},{9,13},{2,6},{6,10},{10,14},{3,7},{... | collective-permute-start | bytes 6152 | tf_op jit(solution)/shard_map/ppermute | solution.py:16
  28.9 158.5 %collective-permute-start = (s32[3]{0:T(128)}, s32[3]{0:T(128)}, u32[]{:S(2)}, u32[]{:S(2)}) collective-permute-start(s32[3]{0:T(128)} %get-tuple-element.247), channel_id=1, source_target_pairs={{0,4},{4,8},{8,12},{1,5},{5,9},{9,13},{2,6},{6,10},{10,14},{3,7},{... | collective-permute-start | bytes 44 | tf_op jit(solution)/shard_map/ppermute | solution.py:16
  30.8 254.7 %all-reduce.30.cloned.1.call-start = ((), (), s32[]{:S(2)}) async-start(), calls=%async_computation.28 | async-start | bytes 4194304 | tf_op jit(solution)/shard_map/psum | solution.py:34
  187.4 2.8 collective-permute-start.8
  190.2 5.5 collective-permute-start.1
  195.6 5.5 collective-permute-start.9
  230.5 173.1 %all-reduce.28.cloned.1.call-start = ((), (), s32[]{:S(2)}) async-start(), calls=%async_computation.27 | async-start | bytes 4194304 | tf_op jit(solution)/shard_map/psum | solution.py:34
  290.0 28.9 %collective-permute-start.6 = (bf16[512,128]{1,0:T(8,128)(2,1)S(1)}, bf16[512,128]{1,0:T(8,128)(2,1)S(1)}, u32[]{:S(2)}, u32[]{:S(2)}) collective-permute-start(bf16[512,128]{1,0:T(8,128)(2,1)S(1)} %convolution_convert_fusion.5), channel_id=1, source_target_pairs={{0,8},{4,12},{1,9},{5,13},{2,10},{6,14},{3,11},{7,15},{16,24},{20,... | collective-permute-start | bytes 393224 | tf_op jit(solution)/shard_map/ppermute | solution.py:16
  294.3 26.7 %collective-permute-start.7 = (bf16[512,128]{1,0:T(8,128)(2,1)S(1)}, bf16[512,128]{1,0:T(8,128)(2,1)S(1)}, u32[]{:S(2)}, u32[]{:S(2)}) collective-permute-start(bf16[512,128]{1,0:T(8,128)(2,1)S(1)} %convolution_convert_fusion.5), channel_id=1, source_target_pairs={{0,4},{4,8},{8,12},{1,5},{5,9},{9,13},{2,6},{6,10},{10,14},{3,7},{... | collective-permute-start | bytes 393224 | tf_op jit(solution)/shard_map/ppermute | solution.py:16
  298.7 27.1 %collective-permute-start.2 = (bf16[512,128]{1,0:T(8,128)(2,1)}, bf16[512,128]{1,0:T(8,128)(2,1)}, u32[]{:S(2)}, u32[]{:S(2)}) collective-permute-start(bf16[512,128]{1,0:T(8,128)(2,1)} %convolution_convert_fusion.7), channel_id=1, source_target_pairs={{0,8},{4,12},{1,9},{5,13},{2,10},{6,14},{3,11},{7,15},{16,24},{20,... | collective-permute-start | bytes 393224 | tf_op jit(solution)/shard_map/ppermute | solution.py:16
  300.6 27.1 %collective-permute-start.3 = (bf16[512,128]{1,0:T(8,128)(2,1)}, bf16[512,128]{1,0:T(8,128)(2,1)}, u32[]{:S(2)}, u32[]{:S(2)}) collective-permute-start(bf16[512,128]{1,0:T(8,128)(2,1)} %convolution_convert_fusion.7), channel_id=1, source_target_pairs={{0,4},{4,8},{8,12},{1,5},{5,9},{9,13},{2,6},{6,10},{10,14},{3,7},{... | collective-permute-start | bytes 393224 | tf_op jit(solution)/shard_map/ppermute | solution.py:16
  316.0 15.5 %collective-permute-start.14 = (bf16[512,128]{1,0:T(8,128)(2,1)}, bf16[512,128]{1,0:T(8,128)(2,1)}, u32[]{:S(2)}, u32[]{:S(2)}) collective-permute-start(bf16[512,128]{1,0:T(8,128)(2,1)} %convolution_convert_fusion.2), channel_id=1, source_target_pairs={{0,8},{4,12},{1,9},{5,13},{2,10},{6,14},{3,11},{7,15},{16,24},{20,... | collective-permute-start | bytes 393224 | tf_op jit(solution)/shard_map/ppermute | solution.py:16
  318.9 12.6 %collective-permute-start.15 = (bf16[512,128]{1,0:T(8,128)(2,1)}, bf16[512,128]{1,0:T(8,128)(2,1)}, u32[]{:S(2)}, u32[]{:S(2)}) collective-permute-start(bf16[512,128]{1,0:T(8,128)(2,1)} %convolution_convert_fusion.2), channel_id=1, source_target_pairs={{0,4},{4,8},{8,12},{1,5},{5,9},{9,13},{2,6},{6,10},{10,14},{3,7},{... | collective-permute-start | bytes 393224 | tf_op jit(solution)/shard_map/ppermute | solution.py:16
  321.0 14.2 %collective-permute-start.10 = (bf16[512,128]{1,0:T(8,128)(2,1)}, bf16[512,128]{1,0:T(8,128)(2,1)}, u32[]{:S(2)}, u32[]{:S(2)}) collective-permute-start(bf16[512,128]{1,0:T(8,128)(2,1)} %convolution_convert_fusion.4), channel_id=1, source_target_pairs={{0,8},{4,12},{1,9},{5,13},{2,10},{6,14},{3,11},{7,15},{16,24},{20,... | collective-permute-start | bytes 393224 | tf_op jit(solution)/shard_map/ppermute | solution.py:16
  325.7 9.5 collective-permute-start.11
  354.7 116.0 %all-reduce.26.cloned.1.call-start = ((), (), s32[]{:S(2)}) async-start(), calls=%async_computation.26 | async-start | bytes 4194304 | tf_op jit(solution)/shard_map/psum | solution.py:34
  419.1 204.0 %all-reduce.24.cloned.1.call-start = ((), (), s32[]{:S(2)}) async-start(), calls=%async_computation.25 | async-start | bytes 4194304 | tf_op jit(solution)/shard_map/psum | solution.py:34
  498.8 68.4 %collective-permute-start.23 = (f32[512,128]{0,1:T(8,128)S(1)}, f32[512,128]{0,1:T(8,128)S(1)}, u32[]{:S(2)}, u32[]{:S(2)}) collective-permute-start(f32[512,128]{0,1:T(8,128)S(1)} %bitcast.378), channel_id=1, source_target_pairs={{8,0},{12,4},{9,1},{13,5},{10,2},{14,6},{11,3},{15,7},{24,16},{28,... | collective-permute-start | bytes 786440 | tf_op jit(solution)/shard_map/ppermute | solution.py:16
  500.2 67.0 %collective-permute-start.24 = (f32[512,128]{0,1:T(8,128)S(1)}, f32[512,128]{0,1:T(8,128)S(1)}, u32[]{:S(2)}, u32[]{:S(2)}) collective-permute-start(f32[512,128]{0,1:T(8,128)S(1)} %bitcast.377), channel_id=1, source_target_pairs={{4,0},{8,4},{12,8},{5,1},{9,5},{13,9},{6,2},{10,6},{14,10},{7,3},{... | collective-permute-start | bytes 786440 | tf_op jit(solution)/shard_map/ppermute | solution.py:16
  501.6 45.7 %collective-permute-start.18 = (f32[512,128]{0,1:T(8,128)S(1)}, f32[512,128]{0,1:T(8,128)S(1)}, u32[]{:S(2)}, u32[]{:S(2)}) collective-permute-start(f32[512,128]{0,1:T(8,128)S(1)} %bitcast.380), channel_id=1, source_target_pairs={{8,0},{12,4},{9,1},{13,5},{10,2},{14,6},{11,3},{15,7},{24,16},{28,... | collective-permute-start | bytes 786440 | tf_op jit(solution)/shard_map/ppermute | solution.py:16
  502.9 41.3 %collective-permute-start.16 = (f32[512,128]{0,1:T(8,128)S(1)}, f32[512,128]{0,1:T(8,128)S(1)}, u32[]{:S(2)}, u32[]{:S(2)}) collective-permute-start(f32[512,128]{0,1:T(8,128)S(1)} %bitcast.384), channel_id=1, source_target_pairs={{8,0},{12,4},{9,1},{13,5},{10,2},{14,6},{11,3},{15,7},{24,16},{28,... | collective-permute-start | bytes 786440 | tf_op jit(solution)/shard_map/ppermute | solution.py:16
  504.2 41.3 %collective-permute-start.17 = (f32[512,128]{0,1:T(8,128)S(1)}, f32[512,128]{0,1:T(8,128)S(1)}, u32[]{:S(2)}, u32[]{:S(2)}) collective-permute-start(f32[512,128]{0,1:T(8,128)S(1)} %bitcast.383), channel_id=1, source_target_pairs={{4,0},{8,4},{12,8},{5,1},{9,5},{13,9},{6,2},{10,6},{14,10},{7,3},{... | collective-permute-start | bytes 786440 | tf_op jit(solution)/shard_map/ppermute | solution.py:16
  544.3 8.3 collective-permute-start.19
  545.6 21.2 %collective-permute-start.21 = (f32[512,128]{0,1:T(8,128)S(1)}, f32[512,128]{0,1:T(8,128)S(1)}, u32[]{:S(2)}, u32[]{:S(2)}) collective-permute-start(f32[512,128]{0,1:T(8,128)S(1)} %bitcast.382), channel_id=1, source_target_pairs={{8,0},{12,4},{9,1},{13,5},{10,2},{14,6},{11,3},{15,7},{24,16},{28,... | collective-permute-start | bytes 786440 | tf_op jit(solution)/shard_map/ppermute | solution.py:16
  547.3 19.5 %collective-permute-start.22 = (f32[512,128]{0,1:T(8,128)S(1)}, f32[512,128]{0,1:T(8,128)S(1)}, u32[]{:S(2)}, u32[]{:S(2)}) collective-permute-start(f32[512,128]{0,1:T(8,128)S(1)} %bitcast.381), channel_id=1, source_target_pairs={{4,0},{8,4},{12,8},{5,1},{9,5},{13,9},{6,2},{10,6},{14,10},{7,3},{... | collective-permute-start | bytes 786440 | tf_op jit(solution)/shard_map/ppermute | solution.py:16
  569.6 162.0 %reduce-scatter.12.cloned.1.call-start = ((), (), s32[]{:S(2)}) async-start(), calls=%async_computation.13 | async-start | bytes 2621440 | tf_op jit(solution)/shard_map/reduce_scatter | solution.py:340
  644.1 91.7 %reduce-scatter.14.cloned.1.call-start = ((), (), s32[]{:S(2)}) async-start(), calls=%async_computation.14 | async-start | bytes 2621440 | tf_op jit(solution)/shard_map/reduce_scatter | solution.py:340
  657.0 100.3 %reduce-scatter.26.cloned.1.call-start = ((), (), s32[]{:S(2)}) async-start(), calls=%async_computation.20 | async-start | bytes 327680 | tf_op jit(solution)/shard_map/reduce_scatter | solution.py:367
  660.9 117.4 %reduce-scatter.20.cloned.1.call-start = ((), (), s32[]{:S(2)}) async-start(), calls=%async_computation.17 | async-start | bytes 327680 | tf_op jit(solution)/shard_map/reduce_scatter | solution.py:364
  664.5 134.3 %reduce-scatter.24.cloned.1.call-start = ((), (), s32[]{:S(2)}) async-start(), calls=%async_computation.19 | async-start | bytes 327680 | tf_op jit(solution)/shard_map/reduce_scatter | solution.py:366
  668.1 151.1 %reduce-scatter.22.cloned.1.call-start = ((), (), s32[]{:S(2)}) async-start(), calls=%async_computation.18 | async-start | bytes 327680 | tf_op jit(solution)/shard_map/reduce_scatter | solution.py:365
  671.7 175.3 %reduce-scatter.32.cloned.1.call-start = ((), (), s32[]{:S(2)}) async-start(), calls=%async_computation.23 | async-start | bytes 1310720 | tf_op jit(solution)/shard_map/reduce_scatter | solution.py:370
  676.1 198.9 %reduce-scatter.30.cloned.1.call-start = ((), (), s32[]{:S(2)}) async-start(), calls=%async_computation.22 | async-start | bytes 1310720 | tf_op jit(solution)/shard_map/reduce_scatter | solution.py:369
  680.5 222.4 %reduce-scatter.28.cloned.1.call-start = ((), (), s32[]{:S(2)}) async-start(), calls=%async_computation.21 | async-start | bytes 1310720 | tf_op jit(solution)/shard_map/reduce_scatter | solution.py:368
  685.1 241.6 %reduce-scatter.18.cloned.1.call-start = ((), (), s32[]{:S(2)}) async-start(), calls=%async_computation.16 | async-start | bytes 983040 | tf_op jit(solution)/shard_map/reduce_scatter | solution.py:363
  689.4 349.8 %reduce-scatter.16.cloned.1.call-start = ((), (), s32[]{:S(2)}) async-start(), calls=%async_computation.15 | async-start | bytes 7864320 | tf_op jit(solution)/shard_map/reduce_scatter | solution.py:362
  698.0 430.3 %all-reduce.22.cloned.1.call-start = ((), (), s32[]{:S(2)}) async-start(), calls=%async_computation.24 | async-start | bytes 8388608 | tf_op jit(solution)/shard_map/psum | solution.py:34
  710.9 13.8 %collective-permute-start.20 = (f32[3,128]{1,0:T(4,128)S(1)}, f32[3,128]{1,0:T(4,128)S(1)}, u32[]{:S(2)}, u32[]{:S(2)}) collective-permute-start(f32[3,128]{1,0:T(4,128)S(1)} %slice.435), channel_id=1, source_target_pairs={{4,0},{8,4},{12,8},{5,1},{9,5},{13,9},{6,2},{10,6},{14,10},{7,3},{... | collective-permute-start | bytes 4616 | tf_op jit(solution)/shard_map/ppermute | solution.py:16
  722.5 405.8 %copy-start.73 = (f32[512]{0:T(512)S(1)}, f32[512]{0:T(512)}, u32[]{:S(2)}) copy-start(f32[512]{0:T(512)} %copy-done.72) | copy-start | bytes 6148
  722.5 7.7 collective-permute-start.25
  738.0 410.8 %copy-start.83 = (f32[512]{0:T(512)S(1)}, f32[512]{0:T(512)}, u32[]{:S(2)}) copy-start(f32[512]{0:T(512)} %copy-done.82) | copy-start | bytes 6148
  738.0 410.8 %copy-start.85 = (f32[512]{0:T(512)S(1)}, f32[512]{0:T(512)}, u32[]{:S(2)}) copy-start(f32[512]{0:T(512)} %copy-done.84) | copy-start | bytes 6148
  741.6 468.5 %all-reduce.32.cloned.1.call-start = ((), (), s32[]{:S(2)}) async-start(), calls=%async_computation.29 | async-start | bytes 5636096 | tf_op jit(solution)/shard_map/psum | solution.py:375
  (113 other events, 3601.1 us)
Sparse Core Ops, SparseCore 0:
  12.6 48.6 all-gather.4
  62.8 44.4 all-gather.6
  230.6 54.8 all-reduce.29
  354.8 48.6 all-reduce.27
  419.3 51.4 all-reduce.25
  569.7 53.4 all-reduce.23
  644.3 46.3 reduce-scatter.11
  692.9 42.8 reduce-scatter.13
  738.1 19.1 reduce-scatter.25
  760.0 18.2 reduce-scatter.19
  780.5 18.2 reduce-scatter.23
  800.9 18.2 reduce-scatter.21
  821.5 25.4 reduce-scatter.31
  849.1 25.7 reduce-scatter.29
  877.1 25.7 reduce-scatter.27
  905.1 21.6 reduce-scatter.17
  928.9 110.2 reduce-scatter.15
  1042.2 86.0 all-reduce.21
  1131.1 78.9 all-reduce.31
where the time goes:
time: 1240 us; the launch traced here: 1230 us
  waiting for transfers between devices  704 us (57%)
  local copies, waits for them, and re-layouts  173 us (14%)
  matrix products  143 us (12%)
  other arithmetic  81.9 us (7%)
  starting transfers between devices  71 us (6%)
  blocking collectives  42.2 us (3%)
  between operations  17 us (1%)
    psum x5, waiting for transfers between devices, tensor_total(): return lax.psum(partial_value, 'tensor')  289 us
    reduce_scatter x1, waiting for transfers between devices, local(): lax.psum_scatter(filter_acc, 'seq', scatter_dimension=1, tiled=True)  112 us
    ppermute x26, starting transfers between devices, shifted(): return lax.ppermute(block, axis, route)  69.3 us
    ppermute x26, waiting for transfers between devices, shifted(): return lax.ppermute(block, axis, route)  60.2 us
    psum x1, waiting for transfers between devices, local(): lax.psum((scattered[0], scattered[1], scattered[2], scattered[3], scatter...  55.4 us
    reshape x1, local copies, waits for them, and re-layouts, skew_tiles(): repeated[:, :, :block_rows * (2 * block_rows - 1)]  47.1 us
    another operation x2, local copies, waits for them, and re-layouts, skew_tiles(): repeated = jnp.tile(reordered, (1, 1, block_rows))  33.4 us
    reduce_scatter x1, waiting for transfers between devices, local(): lax.psum_scatter(up_acc, 'seq', scatter_dimension=0, tiled=True)  28 us
  transfers between devices with their start and end apart: 45, of which 23 were waited for; matrix products, arithmetic and copies ran while one was open for 23% of the time, Pallas kernels for 0%

commit v1 on v0

v1 whole, which is shorter than its diff:
```python
import functools

import jax
import jax.numpy as jnp
from jax import lax
from jax.experimental import pallas as pl
from jax.experimental.pallas import tpu as pltpu
from jax.sharding import PartitionSpec as P

HD = 64
WINDOW = 1024
EPSILON = 1e-05
LANES = 128
NEGATIVE = -1e30
MESH = pl.DeviceIdType.MESH
BF = jnp.bfloat16
F32 = jnp.float32
VMEM_LIMIT = 60 * 1024 * 1024


def place():
    s = lax.axis_index("seq")
    t = lax.axis_index("tensor")
    y = t // 2
    c = t - 2 * y
    return s, t, y, c, t + 1 - 2 * c, t + 2 - 4 * y


def when(condition, action):
    if condition is True:
        action()
    else:
        pl.when(condition)(action)


def remote(src, dst, send_sem, recv_sem, device):
    return pltpu.make_async_remote_copy(
        src_ref=src, dst_ref=dst, send_sem=send_sem, recv_sem=recv_sem, device_id=device, device_id_type=MESH
    )


def greet(seq_count, hops):
    s, t, y, c, core, far = place()
    barrier = pltpu.get_barrier_semaphore()
    for peer in (core, far):
        pl.semaphore_signal(barrier, inc=1, device_id={"tensor": peer}, device_id_type=MESH)
    for h in range(1, hops + 1):
        for there, peer in ((s - h >= 0, s - h), (s + h < seq_count, s + h)):

            @pl.when(there)
            def _():
                pl.semaphore_signal(barrier, inc=1, device_id={"seq": peer}, device_id_type=MESH)

    peers = 2 + jnp.minimum(s, hops) + jnp.minimum(seq_count - 1 - s, hops)
    pl.semaphore_wait(barrier, peers)


class ReduceScatter:
    def __init__(self, seq_count, hops, streams, part, scratch):
        self.seq_count, self.hops, self.streams, self.part = seq_count, hops, streams, part
        self.near, self.half, self.over, self.hop_out, self.hop_in, self.sem = scratch

    @staticmethod
    def scratch(hops, streams, rows, width):
        quarter = (hops + 1, streams, rows, width)
        return [
            pltpu.VMEM((hops + 1, streams, 2, rows, width), BF),
            pltpu.VMEM(quarter, BF),
            pltpu.VMEM(quarter, BF),
            pltpu.VMEM(quarter, BF),
            pltpu.VMEM(quarter, BF),
            pltpu.SemaphoreType.DMA((6, hops + 1, streams)),
        ]

    def to_core(self, h, m):
        s, t, y, c, core, far = place()
        return remote(
            self.part(h, m).at[:, 1 - c], self.near.at[h, m], self.sem.at[0, h, m], self.sem.at[1, h, m], {"tensor": core}
        )

    def to_far(self, h, m):
        s, t, y, c, core, far = place()
        return remote(self.half.at[h, m], self.over.at[h, m], self.sem.at[2, h, m], self.sem.at[3, h, m], {"tensor": far})

    def to_hop(self, h, m, peer):
        return remote(
            self.hop_out.at[h, m], self.hop_in.at[h, m], self.sem.at[4, h, m], self.sem.at[5, h, m], {"seq": peer}
        )

    def there(self, h):
        return True if h == 0 else lax.axis_index("seq") - h >= 0

    def order(self):
        return [(h, m) for h in range(self.hops, -1, -1) for m in range(self.streams)]

    def start(self, h, m):
        when(self.there(h), lambda: self.to_core(h, m).start())

    def middle(self, h, m):
        s, t, y, c, core, far = place()

        def act():
            self.to_core(h, m).wait_recv()
            mine = self.part(h, m)[1 - y, c].astype(F32) + self.near[h, m, 1 - y].astype(F32)
            self.half[h, m] = mine.astype(BF)
            self.to_far(h, m).start()

        when(self.there(h), act)

    def own(self, h, m):
        s, t, y, c, core, far = place()
        self.to_far(h, m).wait_recv()
        return (
            self.part(h, m)[y, c].astype(F32) + self.near[h, m, y].astype(F32) + self.over[h, m].astype(F32)
        )

    def hop(self, h, m):
        def act():
            self.hop_out[h, m] = self.own(h, m).astype(BF)
            self.to_hop(h, m, lax.axis_index("seq") - h).start()

        when(self.there(h), act)

    def total(self, m, acc):
        acc[...] = self.own(0, m)
        for h in range(1, self.hops + 1):
            s = lax.axis_index("seq")

            @pl.when(s + h < self.seq_count)
            def _():
                self.to_hop(h, m, s + h).wait_recv()
                acc[...] += self.hop_in[h, m].astype(F32)

    def drain(self):
        for h, m in self.order():

            def act():
                self.to_core(h, m).wait_send()
                self.to_far(h, m).wait_send()
                if h:
                    self.to_hop(h, m, lax.axis_index("seq") - h).wait_send()

            when(self.there(h), act)


class AllGather:
    def __init__(self, seq_count, hops, streams, out, sem, first=0):
        self.seq_count, self.hops, self.streams, self.out, self.sem, self.first = seq_count, hops, streams, out, sem, first

    @staticmethod
    def scratch(hops, streams):
        return [pltpu.SemaphoreType.DMA((8, hops + 1, streams))]

    def there(self, h):
        return True if h == 0 else lax.axis_index("seq") - h >= 0

    def copy(self, kind, h, m, quarter, device, to=None):
        source = self.out.at[0 if kind == 0 else h, m, quarter]
        return remote(source, self.out.at[h, m, quarter], self.sem.at[2 * kind, h, m], self.sem.at[2 * kind + 1, h, m], device)

    def to_hop(self, h, m, peer):
        return self.copy(0, h, m, place()[1], {"seq": peer})

    def spread(self, h, m):
        s, t, y, c, core, far = place()
        self.copy(1, h, m, t, {"tensor": far}).start()
        self.copy(2, h, m, t, {"tensor": core}).start()

    def start(self, m):
        s, t, y, c, core, far = place()
        for h in range(1, self.hops + 1):

            @pl.when(s + h < self.seq_count)
            def _():
                self.to_hop(h, m, s + h).start()

        if self.first == 0:
            self.spread(0, m)

    def arrive(self, h, m):
        @pl.when(self.there(h))
        def _():
            self.to_hop(h, m, lax.axis_index("seq") - h).wait_recv()
            self.spread(h, m)

    def pass_on(self, h, m):
        s, t, y, c, core, far = place()

        def act():
            self.copy(1, h, m, far, {"tensor": far}).wait_recv()
            self.copy(3, h, m, far, {"tensor": core}).start()

        when(self.there(h), act)

    def finish(self, h, m):
        s, t, y, c, core, far = place()

        def act():
            self.copy(2, h, m, core, {"tensor": core}).wait_recv()
            self.copy(3, h, m, 3 - t, {"tensor": core}).wait_recv()

        when(self.there(h), act)

    def clear(self, h, m):
        @pl.when(lax.axis_index("seq") - h < 0)
        def _():
            self.out[h, m] = jnp.zeros(self.out.shape[2:], self.out.dtype)

    def drain(self):
        s, t, y, c, core, far = place()
        for m in range(self.streams):
            for h in range(1, self.hops + 1):

                @pl.when(s + h < self.seq_count)
                def _():
                    self.to_hop(h, m, s + h).wait_send()

            for h in range(self.first, self.hops + 1):

                def act():
                    self.copy(1, h, m, t, {"tensor": far}).wait_send()
                    self.copy(2, h, m, t, {"tensor": core}).wait_send()
                    self.copy(3, h, m, far, {"tensor": core}).wait_send()

                when(self.there(h), act)


def params(cid=None):
    if cid is None:
        return pltpu.CompilerParams(vmem_limit_bytes=VMEM_LIMIT)
    return pltpu.CompilerParams(vmem_limit_bytes=VMEM_LIMIT, collective_id=cid, has_side_effects=True)


def in_vmem(count):
    return [pl.BlockSpec(memory_space=pltpu.VMEM)] * count


def gather_rows(inputs, ids, seq_count):
    streams, quarters, rows, width = inputs.shape
    hops = seq_count - 1

    def kernel(x_ref, id_ref, out, out_ids, sem, id_sem):
        s, t, y, c, core, far = place()
        greet(seq_count, hops)
        out[0] = x_ref[...]
        out_ids[0] = id_ref[...]
        ag = AllGather(seq_count, hops, streams, out, sem, first=1)

        def id_copy(h, peer):
            return remote(id_ref, out_ids.at[h], id_sem.at[0, h], id_sem.at[1, h], {"seq": peer})

        for h in range(1, hops + 1):

            @pl.when(s + h < seq_count)
            def _():
                id_copy(h, s + h).start()

        ag.to_hop = lambda h, m, peer: remote(
            x_ref.at[m, t], out.at[h, m, t], sem.at[0, h, m], sem.at[1, h, m], {"seq": peer}
        )
        for m in range(streams):
            ag.start(m)
        for h in range(1, hops + 1):
            for m in range(streams):
                ag.clear(h, m)

            @pl.when(s - h < 0)
            def _():
                out_ids[h] = jnp.full(out_ids.shape[1:], -1, jnp.int32)

        for h in range(1, hops + 1):
            for m in range(streams):
                ag.arrive(h, m)
        for h in range(1, hops + 1):
            for m in range(streams):
                ag.pass_on(h, m)
        for h in range(1, hops + 1):
            for m in range(streams):
                ag.finish(h, m)

            @pl.when(s - h >= 0)
            def _():
                id_copy(h, s - h).wait_recv()

            @pl.when(s + h < seq_count)
            def _():
                id_copy(h, s + h).wait_send()

        ag.drain()

    return pl.pallas_call(
        kernel,
        name="gather_rows",
        out_shape=(
            jax.ShapeDtypeStruct((seq_count,) + inputs.shape, inputs.dtype),
            jax.ShapeDtypeStruct((seq_count,) + ids.shape, jnp.int32),
        ),
        in_specs=in_vmem(2),
        out_specs=tuple(in_vmem(2)),
        scratch_shapes=AllGather.scratch(hops, streams) + [pltpu.SemaphoreType.DMA((2, seq_count))],
        compiler_params=params(1),
    )(inputs, ids)


def exchange(name, cid, seq_count, parts, others, reduce_hops, gather_hops, finish, extra):
    per_part = parts[0].shape[1]
    rows, width = parts[0].shape[4:]
    streams = per_part * len(parts)
    hops = max(reduce_hops, gather_hops)

    def kernel(*refs):
        refs = list(refs)
        part_refs = [refs.pop(0) for _ in parts]
        other_refs = [refs.pop(0) for _ in others]
        out = refs.pop(0)
        extra_refs = [refs.pop(0) for _ in extra]
        acc = refs.pop(0)
        gather_sem = refs.pop(0)
        s, t, y, c, core, far = place()
        greet(seq_count, hops)
        rs = ReduceScatter(
            seq_count, reduce_hops, streams, lambda h, m: part_refs[m // per_part].at[h, m % per_part], refs
        )
        ag = AllGather(seq_count, gather_hops, streams, out, gather_sem)
        for h, m in rs.order():
            rs.start(h, m)
        for h in range(1, gather_hops + 1):
            for m in range(streams):
                ag.clear(h, m)
        for h, m in rs.order():
            rs.middle(h, m)
        for h, m in rs.order():
            if h:
                rs.hop(h, m)
        for m in range(streams):
            rs.total(m, acc)
            out[0, m, t] = finish(m, acc[...], other_refs, extra_refs)
            ag.start(m)
        for h in range(gather_hops + 1):
            for m in range(streams):
                if h:
                    ag.arrive(h, m)
            for m in range(streams):
                ag.pass_on(h, m)
        for h in range(gather_hops + 1):
            for m in range(streams):
                ag.finish(h, m)
        rs.drain()
        ag.drain()

    return pl.pallas_call(
        kernel,
        name=name,
        out_shape=(jax.ShapeDtypeStruct((gather_hops + 1, streams, 4, rows, width), BF),) + tuple(extra),
        in_specs=in_vmem(len(parts) + len(others)),
        out_specs=tuple(in_vmem(1 + len(extra))),
        scratch_shapes=[pltpu.VMEM((rows, width), F32)]
        + AllGather.scratch(gather_hops, streams)
        + ReduceScatter.scratch(reduce_hops, streams, rows, width),
        compiler_params=params(cid),
    )(*parts, *others)


def norm_of(values, gain_row):
    inverse = lax.rsqrt(jnp.mean(values * values, axis=-1, keepdims=True) + EPSILON)
    return values * inverse * gain_row


def norm_back(values, gain_row, grad_out):
    inverse = lax.rsqrt(jnp.mean(values * values, axis=-1, keepdims=True) + EPSILON)
    scaled = grad_out * gain_row
    dot = jnp.mean(scaled * values, axis=-1, keepdims=True)
    grad_in = inverse * scaled - values * (inverse * inverse * inverse) * dot
    return grad_in, jnp.sum(grad_out * values * inverse, axis=0, keepdims=True)


def strips(base_ref, strip):
    @pl.loop(0, base_ref.shape[0])
    def _(k):
        row = jnp.broadcast_to(base_ref[k], strip.shape[1:])
        strip[k] = pltpu.roll(row, 0, 1, stride=1, stride_axis=0).astype(BF)


def convolve(rows, row_ids, col_ids, base, seq_count):
    _, streams, length, width = rows.shape
    count, _, wide = base.shape
    blocks = length // LANES

    def kernel(x_ref, row_ref, col_ref, base_ref, out_ref, strip, mask, acc):
        strips(base_ref, strip)
        s = lax.axis_index("seq")

        @pl.loop(0, streams)
        def _(m):
            acc[...] = jnp.zeros_like(acc)

            @pl.loop(0, s + 1)
            def _(h):
                mask[...] = jnp.where(col_ref[m] == row_ref[h, m], 1.0, 0.0).astype(BF)

                @pl.loop(0, count)
                def _(k):
                    pieces = []
                    for a in range(blocks):
                        start = pl.multiple_of(LANES * (blocks * (seq_count - h) - 1 - a), LANES)
                        pieces.append(strip[k, :, pl.ds(start, length)] * mask[a * LANES : (a + 1) * LANES])
                    acc[k] += jnp.dot(jnp.concatenate(pieces, axis=0), x_ref[h, m], preferred_element_type=F32)

            @pl.loop(0, count)
            def _(k):
                out_ref[k, m] = acc[k].astype(BF)

    return pl.pallas_call(
        kernel,
        name="convolve",
        out_shape=jax.ShapeDtypeStruct((count, streams, length, width), BF),
        in_specs=in_vmem(4),
        out_specs=in_vmem(1)[0],
        scratch_shapes=[
            pltpu.VMEM((count, LANES, wide), BF),
            pltpu.VMEM((length, length), BF),
            pltpu.VMEM((count, length, width), F32),
        ],
        compiler_params=params(),
    )(rows, row_ids, col_ids, base)


def convolve_back(grads, row_ids, col_ids, base, own_lag, tail_lag, seq_count):
    count, streams, length, width = grads.shape
    wide = base.shape[2]
    blocks = length // LANES
    channels = own_lag.shape[2]
    tail_rows = tail_lag.shape[1]

    def kernel(g_ref, row_ref, col_ref, base_ref, own_ref, tail_ref, out_ref, strip, mask, acc):
        strips(base_ref, strip)
        s = lax.axis_index("seq")
        mine = pl.ds(pl.multiple_of(lax.axis_index("tensor") * channels, LANES), channels)

        @pl.loop(0, s + 1)
        def _(h):
            @pl.loop(0, streams)
            def _(m):
                mask[...] = jnp.where(col_ref[h, m] == row_ref[m], 1.0, 0.0).astype(BF)
                acc[...] = jnp.zeros_like(acc)

                @pl.when(h == 0)
                def _():
                    acc[:, mine] = own_ref[m]

                @pl.when(h == 1)
                def _():
                    acc[length - tail_rows :, mine] = tail_ref[m]

                @pl.loop(0, count)
                def _(k):
                    pieces = []
                    for a in range(blocks):
                        start = pl.multiple_of(LANES * (blocks * h + blocks - 1 - a), LANES)
                        pieces.append(strip[k, :, pl.ds(start, length)] * mask[a * LANES : (a + 1) * LANES])
                    acc[...] += jnp.dot(jnp.concatenate(pieces, axis=0), g_ref[k, m], preferred_element_type=F32)

                out_ref[h, m] = acc[...].astype(BF)

    return pl.pallas_call(
        kernel,
        name="convolve_back",
        out_shape=jax.ShapeDtypeStruct((seq_count, streams, length, width), BF),
        in_specs=in_vmem(6),
        out_specs=in_vmem(1)[0],
        scratch_shapes=[
            pltpu.VMEM((count, LANES, wide), BF),
            pltpu.VMEM((length, length), BF),
            pltpu.VMEM((length, width), F32),
        ],
        compiler_params=params(),
    )(grads, row_ids, col_ids, base, own_lag, tail_lag)


def dot_nn(a, b):
    return jnp.dot(a, b, preferred_element_type=F32)


def dot_nt(a, b):
    return lax.dot_general(a, b, (((1,), (1,)), ((), ())), preferred_element_type=F32)


def dot_tn(a, b):
    return lax.dot_general(a, b, (((0,), (0,)), ((), ())), preferred_element_type=F32)


def allowed_keys(query_ids, key_ids, first_row, distance):
    shape = (query_ids.shape[0], key_ids.shape[1])
    offset = lax.broadcasted_iota(jnp.int32, shape, 0) - lax.broadcasted_iota(jnp.int32, shape, 1) + (first_row + distance)
    return (query_ids == key_ids) & (offset >= 0) & (offset < WINDOW)


def one_head(block, head):
    lane = lax.broadcasted_iota(jnp.int32, block.shape, 1)
    return jnp.where((lane >= head * HD) & (lane < (head + 1) * HD), block, jnp.zeros_like(block))


def attend(rows, row_ids, col_ids, wq, wk, wv, wo):
    spans, streams, length, width = rows.shape
    cols = wq.shape[1]
    heads = cols // HD
    tile = min(256, length)
    scale = HD ** (-0.5)

    def kernel(x_ref, row_ref, col_ref, wq_ref, wk_ref, wv_ref, wo_ref, q_ref, k_ref, v_ref, a_ref, lse_ref, p_ref):
        @pl.loop(0, streams)
        def _(m):
            q_ref[m] = dot_nn(x_ref[0, m], wq_ref[...]).astype(BF)
            for h in range(spans):
                k_ref[h, m] = dot_nn(x_ref[h, m], wk_ref[...]).astype(BF)
                v_ref[h, m] = dot_nn(x_ref[h, m], wv_ref[...]).astype(BF)

            @pl.loop(0, length // tile)
            def _(i):
                first = pl.multiple_of(i * tile, tile)
                here = pl.ds(first, tile)
                masks = [allowed_keys(col_ref[m, here], row_ref[h, m], first, h * length) for h in range(spans)]
                block = q_ref[m, here]
                result = jnp.zeros((tile, cols), F32)
                for head in range(heads):
                    query = one_head(block, head)
                    scores = [
                        jnp.where(masks[h], dot_nt(query, k_ref[h, m]) * scale, NEGATIVE) for h in range(spans)
                    ]
                    peak = functools.reduce(jnp.maximum, [jnp.max(v, axis=-1, keepdims=True) for v in scores])
                    raised = [jnp.exp(v - peak) for v in scores]
                    total = sum([jnp.sum(v, axis=-1, keepdims=True) for v in raised])
                    inverse = 1.0 / total
                    mixed = sum([dot_nn((raised[h] * inverse).astype(BF), v_ref[h, m]) for h in range(spans)])
                    result = result + one_head(mixed, head)
                    lse_ref[m, head, here] = jnp.broadcast_to(peak + jnp.log(total), (tile, LANES))
                a_ref[m, here] = result.astype(BF)

            p_ref[m] = dot_nn(a_ref[m], wo_ref[...]).astype(BF)

    part = jax.ShapeDtypeStruct((streams, length, cols), BF)
    span = jax.ShapeDtypeStruct((spans, streams, length, cols), BF)
    return pl.pallas_call(
        kernel,
        name="attend",
        out_shape=(
            part,
            span,
            span,
            part,
            jax.ShapeDtypeStruct((streams, heads, length, LANES), F32),
            jax.ShapeDtypeStruct((streams, length, width), BF),
        ),
        in_specs=in_vmem(7),
        out_specs=tuple(in_vmem(6)),
        compiler_params=params(),
    )(rows, row_ids, col_ids, wq, wk, wv, wo)


def attend_back(q, k, v, lse, grad_out, row_ids, col_ids, wq, wk, wv, wo):
    spans, streams, length, cols = k.shape
    width = grad_out.shape[2]
    heads = cols // HD
    tile = min(256, length)
    scale = HD ** (-0.5)

    def kernel(
        q_ref, k_ref, v_ref, lse_ref, go_ref, row_ref, col_ref, wq_ref, wk_ref, wv_ref, wo_ref,
        dq_ref, dk_ref, dv_ref, p_ref, ga_ref, dk_acc, dv_acc,
    ):
        @pl.loop(0, streams)
        def _(m):
            ga_ref[...] = dot_nt(go_ref[m], wo_ref[...]).astype(BF)
            dk_acc[...] = jnp.zeros_like(dk_acc)
            dv_acc[...] = jnp.zeros_like(dv_acc)

            @pl.loop(0, length // tile)
            def _(i):
                first = pl.multiple_of(i * tile, tile)
                here = pl.ds(first, tile)
                masks = [allowed_keys(col_ref[m, here], row_ref[h, m], first, h * length) for h in range(spans)]
                block = q_ref[m, here]
                grad_block = ga_ref[here]
                result = jnp.zeros((tile, cols), F32)
                for head in range(heads):
                    query = one_head(block, head)
                    grad = one_head(grad_block, head)
                    level = lse_ref[m, head, here][:, :1]
                    prob = [
                        jnp.where(masks[h], jnp.exp(dot_nt(query, k_ref[h, m]) * scale - level), 0.0)
                        for h in range(spans)
                    ]
                    grad_prob = [dot_nt(grad, v_ref[h, m]) for h in range(spans)]
                    mean = sum([jnp.sum(p * g, axis=-1, keepdims=True) for p, g in zip(prob, grad_prob)])
                    grad_scores = [(p * (g - mean)).astype(BF) for p, g in zip(prob, grad_prob)]
                    for h in range(spans):
                        dv_acc[h] += dot_tn(prob[h].astype(BF), grad)
                        dk_acc[h] += dot_tn(grad_scores[h], query)
                    mixed = sum([dot_nn(grad_scores[h], k_ref[h, m]) for h in range(spans)])
                    result = result + one_head(mixed, head)
                dq_ref[m, here] = (result * scale).astype(BF)

            for h in range(spans):
                dk_ref[h, m] = (dk_acc[h] * scale).astype(BF)
                dv_ref[h, m] = dv_acc[h].astype(BF)
                back = dot_nt(dk_ref[h, m], wk_ref[...]) + dot_nt(dv_ref[h, m], wv_ref[...])
                if h == 0:
                    back = back + dot_nt(dq_ref[m], wq_ref[...])
                p_ref[h, m] = back.astype(BF)

    span = jax.ShapeDtypeStruct((spans, streams, length, cols), BF)
    return pl.pallas_call(
        kernel,
        name="attend_back",
        out_shape=(
            jax.ShapeDtypeStruct((streams, length, cols), BF),
            span,
            span,
            jax.ShapeDtypeStruct((spans, streams, length, width), BF),
        ),
        in_specs=in_vmem(11),
        out_specs=tuple(in_vmem(4)),
        scratch_shapes=[
            pltpu.VMEM((length, cols), BF),
            pltpu.VMEM((spans, length, cols), F32),
            pltpu.VMEM((spans, length, cols), F32),
        ],
        compiler_params=params(),
    )(q, k, v, lse, grad_out, row_ids, col_ids, wq, wk, wv, wo)


def gated_unit(gate_pre, up_pre):
    return jax.nn.gelu(gate_pre, approximate=True) * up_pre


def local(
    seq_count,
    tokens,
    document_index,
    filters,
    stu_gain,
    filter_proj,
    lag_proj,
    attention_gain,
    query_weight,
    key_weight,
    value_weight,
    output_weight,
    feed_gain,
    gate_weight,
    up_weight,
    down_weight,
    cotangent,
):
    streams, _, length, width = tokens.shape
    row_len = length * seq_count
    quarter = length // 4
    lag_order, channels = lag_proj.shape[:2]
    count = filters.shape[0]
    hops = WINDOW // length
    tensor_place = lax.axis_index("tensor")
    chan_start = tensor_place * channels

    def split(a):
        return a.reshape(a.shape[:-2] + (2, 2, quarter, width))

    def quarters(a):
        return a.reshape(a.shape[:-2] + (4, quarter, width))

    def whole(a):
        return a.reshape(a.shape[:-3] + (length, width))

    def row(gain):
        return gain.reshape(1, width)

    x = tokens[:, 0]
    grad_three = cotangent[:, 0]
    ids = document_index[:, 0]
    inputs = norm_of(x.astype(F32), stu_gain).astype(BF)
    id_tile = ids.reshape(streams * length // LANES, LANES)
    rows_ext, id_ext = gather_rows(quarters(inputs), id_tile, seq_count)
    rows_ext = whole(rows_ext)
    id_ext = id_ext.reshape(seq_count, streams, length)
    id_rows = id_ext[:, :, None, :]
    id_cols = id_ext[:, :, :, None]

    pad = jnp.zeros((count, 4 * LANES), filters.dtype)
    ahead = row_len - LANES
    base = jnp.concatenate(
        [
            jnp.flip(filters[:, : ahead + 1], axis=1),
            pad[:, : 4 * LANES],
            jnp.flip(filters[:, ahead + 1 :], axis=1),
        ],
        axis=1,
    ).astype(F32)[:, None]
    base_back = jnp.concatenate(
        [pad[:, : length - LANES], filters, pad[:, :LANES]], axis=1
    ).astype(F32)[:, None]
    conv = convolve(rows_ext, id_rows, id_cols[0], base, seq_count)

    chan_rows = lax.dynamic_slice_in_dim(rows_ext[:2], chan_start, channels, 3)
    joined = jnp.concatenate([chan_rows[1][:, length - lag_order :], chan_rows[0]], axis=1)
    joined_ids = jnp.concatenate([id_ext[1][:, length - lag_order :], ids], axis=1)
    masks = []
    lagged = []
    for step in range(1, lag_order + 1):
        low = lag_order - step
        masks.append((joined_ids[:, low : low + length] == ids)[:, :, None])
        lagged.append(jnp.where(masks[-1], joined[:, low : low + length], jnp.zeros((), BF)))
    lag_stack = jnp.stack(lagged)

    mixed = jnp.einsum("kmtd,kde->mte", conv, filter_proj, preferred_element_type=F32)
    mixed = mixed + jnp.einsum("imtc,ice->mte", lag_stack, lag_proj, preferred_element_type=F32)

    state = jax.ShapeDtypeStruct((streams, quarter, width), F32)
    gain_state = jax.ShapeDtypeStruct((1, width), F32)

    def finish_one(m, total, others, extra):
        x_ref, gain_ref = others
        hidden = x_ref[m, place()[1]].astype(F32) + total
        extra[0][m] = hidden
        return norm_of(hidden, gain_ref[...]).astype(BF)

    attn_ext, hidden_one = exchange(
        "exchange_one", 2, seq_count, [split(mixed.astype(BF))[None]], [quarters(x), row(attention_gain)], 0, hops,
        finish_one, [state],
    )
    attn_ext = whole(attn_ext)

    q, k, v, attended, lse, out_part = attend(
        attn_ext, id_rows[: hops + 1], id_cols[0], query_weight, key_weight, value_weight, output_weight
    )

    def finish_two(m, total, others, extra):
        hidden_ref, gain_ref = others
        hidden = hidden_ref[m] + total
        extra[0][m] = hidden
        return norm_of(hidden, gain_ref[...]).astype(BF)

    feed_in, hidden_two = exchange(
        "exchange_two", 3, seq_count, [split(out_part)[None]], [hidden_one, row(feed_gain)], 0, 0, finish_two, [state]
    )
    feed_in = whole(feed_in)[0].reshape(streams * length, width)
    flat_three = grad_three.reshape(streams * length, width)

    gate_pre = dot_nn(feed_in, gate_weight)
    up_pre = dot_nn(feed_in, up_weight)
    grad_inner = dot_nt(flat_three, down_weight)
    unit, pull = jax.vjp(gated_unit, gate_pre, up_pre)
    inner = unit.astype(BF)
    grad_gate, grad_up = pull(grad_inner)
    grad_gate = grad_gate.astype(BF)
    grad_up = grad_up.astype(BF)
    layer_part = dot_nn(inner, down_weight).astype(BF)
    feed_part = (dot_nt(grad_gate, gate_weight) + dot_nt(grad_up, up_weight)).astype(BF)

    def finish_three(m, total, others, extra):
        hidden_ref, gain_ref, cot_ref = others
        if m >= streams:
            return (hidden_ref[m - streams] + total).astype(BF)
        grad_in, gain_grad = norm_back(hidden_ref[m], gain_ref[...], total)
        grad_two = cot_ref[m, place()[1]].astype(F32) + grad_in
        extra[0][m] = grad_two
        extra[1][...] = gain_grad if m == 0 else extra[1][...] + gain_grad
        return grad_two.astype(BF)

    shape = (1, streams, length, width)
    both, grad_two, feed_gain_grad = exchange(
        "exchange_three", 4, seq_count, [split(feed_part.reshape(shape)), split(layer_part.reshape(shape))],
        [hidden_two, row(feed_gain), quarters(grad_three)], 0, 0, finish_three, [state, gain_state],
    )
    both = whole(both)[0]
    grad_att_out = both[:streams]
    layer_output = both[streams:]

    dq, dk, dv, attn_part = attend_back(
        q, k, v, lse, grad_att_out, id_rows[: hops + 1], id_cols[0], query_weight, key_weight, value_weight, output_weight
    )

    def finish_four(m, total, others, extra):
        hidden_ref, gain_ref, grad_ref = others
        grad_in, gain_grad = norm_back(hidden_ref[m], gain_ref[...], total)
        grad_one = grad_ref[m] + grad_in
        extra[0][m] = grad_one
        extra[1][...] = gain_grad if m == 0 else extra[1][...] + gain_grad
        return grad_one.astype(BF)

    grad_stu, grad_one, attn_gain_grad = exchange(
        "exchange_four", 5, seq_count, [split(attn_part)], [hidden_one, row(attention_gain), grad_two], hops, 0,
        finish_four, [state, gain_state],
    )
    grad_stu = whole(grad_stu)[0]

    grad_conv = jnp.einsum("mte,kde->kmtd", grad_stu, filter_proj, preferred_element_type=F32).astype(BF)
    grad_lagged = jnp.einsum("mte,ice->imtc", grad_stu, lag_proj, preferred_element_type=F32)
    ext_grad = jnp.zeros((streams, 8 + length, channels), F32)
    for step in range(1, lag_order + 1):
        term = jnp.where(masks[step - 1], grad_lagged[step - 1], 0.0)
        ext_grad = ext_grad + jnp.pad(term, ((0, 0), (8 - step, step), (0, 0)))
    terms = convolve_back(
        grad_conv, id_rows[0], id_cols, base_back, ext_grad[:, 8:], ext_grad[:, :8], seq_count
    )

    def finish_five(m, total, others, extra):
        x_ref, gain_ref, grad_ref = others
        grad_in, gain_grad = norm_back(x_ref[m, place()[1]].astype(F32), gain_ref[...], total)
        extra[0][...] = gain_grad if m == 0 else extra[0][...] + gain_grad
        return (grad_ref[m] + grad_in).astype(BF)

    input_gradient, stu_gain_grad = exchange(
        "exchange_five", 6, seq_count, [split(terms)], [quarters(x), row(stu_gain), grad_one], seq_count - 1, 0,
        finish_five, [gain_state],
    )
    input_gradient = whole(input_gradient)[0]

    tokens_flat = streams * length
    go = grad_att_out.reshape(tokens_flat, width)
    first = jnp.concatenate(
        [
            dot_tn(feed_in, grad_gate).astype(BF),
            dot_tn(feed_in, grad_up).astype(BF),
            dot_tn(flat_three, inner).astype(BF),
            dot_tn(attn_ext[0].reshape(tokens_flat, width), dq.reshape(tokens_flat, -1)).astype(BF),
            dot_tn(attn_ext.reshape(-1, width), dk.reshape(-1, dk.shape[-1])).astype(BF),
            dot_tn(attn_ext.reshape(-1, width), dv.reshape(-1, dv.shape[-1])).astype(BF),
            dot_tn(go, attended.reshape(tokens_flat, -1)).astype(BF),
        ],
        axis=1,
    )
    stu = grad_stu.reshape(tokens_flat, width)
    second = jnp.concatenate(
        [
            jnp.einsum("kmtd,mte->kde", conv, grad_stu, preferred_element_type=F32).astype(BF),
            jnp.concatenate(
                [dot_tn(stu, lag_stack[i].reshape(tokens_flat, channels)).astype(BF) for i in range(lag_order)]
                + [jnp.zeros((width, width - lag_order * channels), BF)],
                axis=1,
            )[None],
        ],
        axis=0,
    )
    first = lax.psum(lax.psum_scatter(first, "seq", scatter_dimension=0, tiled=True), "dp").astype(F32)
    second = lax.psum(lax.psum_scatter(second, "seq", scatter_dimension=1, tiled=True), "dp").astype(F32)
    gains = jnp.concatenate([stu_gain_grad, attn_gain_grad, feed_gain_grad], axis=0)
    gains = lax.psum(gains, ("dp", "seq", "tensor"))
    gain_width = width // seq_count
    gains = lax.dynamic_slice_in_dim(gains, lax.axis_index("seq") * gain_width, gain_width, 1)

    hidden_units = gate_weight.shape[1]
    cols = query_weight.shape[1]
    cuts = [hidden_units, 2 * hidden_units, 3 * hidden_units]
    cuts += [cuts[-1] + cols, cuts[-1] + 2 * cols, cuts[-1] + 3 * cols]
    gate_grad, up_grad, down_grad, query_grad, key_grad, value_grad, output_grad = jnp.split(first, cuts, axis=1)
    lag_grad = second[count][:, : lag_order * channels].T.reshape(lag_order, channels, -1)
    return (
        layer_output[:, None],
        input_gradient[:, None],
        gains[0],
        second[:count],
        lag_grad,
        gains[1],
        query_grad,
        key_grad,
        value_grad,
        output_grad.T,
        gains[2],
        gate_grad,
        up_grad,
        down_grad.T,
    )


def solution(mesh):
    return jax.shard_map(
        functools.partial(local, mesh.shape["seq"]),
        mesh=mesh,
        in_specs=(
            P(None, "dp", "seq", None),
            P(None, "dp", "seq"),
            P("tensor", None),
            P(),
            P("tensor", None, None),
            P(None, "tensor", None),
            P(),
            P(None, "tensor"),
            P(None, "tensor"),
            P(None, "tensor"),
            P("tensor", None),
            P(),
            P(None, "tensor"),
            P(None, "tensor"),
            P("tensor", None),
            P(None, "dp", "seq", None),
        ),
        out_specs=(
            P(None, "dp", "seq", None),
            P(None, "dp", "seq", None),
            P("seq"),
            P("tensor", "seq", None),
            P(None, "tensor", "seq"),
            P("seq"),
            P("seq", "tensor"),
            P("seq", "tensor"),
            P("seq", "tensor"),
            P("tensor", "seq"),
            P("seq"),
            P("seq", "tensor"),
            P("seq", "tensor"),
            P("tensor", "seq"),
        ),
        check_vma=False,
    )
```

time: 1240 us -> 554 us (0.45)
  waiting for transfers between devices: 704 us -> 74.8 us
  Pallas kernels: 0 us -> 307 us
  local copies, waits for them, and re-layouts: 173 us -> 42.6 us
  matrix products: 143 us -> 51.8 us
  starting transfers between devices: 71 us -> 0.12 us
  other arithmetic: 81.9 us -> 16.3 us
    psum x6 -> x1, waiting for transfers between devices: 344 us -> 0.01 us  [local(): lax.psum(lax.psum_scatter(second, 'seq', scatter_dimension=1, tiled=True)...]
    pallas_call x0 -> x10, Pallas kernels: none -> 307 us  [the longest x5 219 us: exchange(): pl.pallas_call(kernel, name=name, out_shape=(jax.ShapeDtypeStruct((gather...]
    reduce_scatter x11 -> x1, waiting for transfers between devices: 300 us -> 74.8 us  [local(): lax.psum_scatter(second, 'seq', scatter_dimension=1, tiled=True)]
    dot_general x68 -> x21, matrix products: 143 us -> 51.8 us  [the longest x10 16.9 us: dot_tn(): lax.dot_general(a, b, (((0,), (0,)), ((), ())), preferred_element_type=F32)]
    ppermute x26 -> x0, starting transfers between devices: 69.3 us -> none  [shifted(): return lax.ppermute(block, axis, route)]
    ppermute x26 -> x0, waiting for transfers between devices: 60.2 us -> none  [shifted(): return lax.ppermute(block, axis, route)]
    reshape x3 -> x0, local copies, waits for them, and re-layouts: 47.9 us -> none  [the longest x1 47.1 us: skew_tiles(): repeated[:, :, :block_rows * (2 * block_rows - 1)]]
    psum x1, blocking collectives: 5.63 us -> 45.2 us  [local(): gains = lax.psum(gains, ('dp', 'seq', 'tensor'))]
  transfers between devices with their start and end apart: 45 -> 3, of which waited for: 23 -> 1; matrix products, arithmetic and copies ran while one was open for 23% -> 6% of each run, Pallas kernels for 0% -> 24%
where the time goes in v1:
time: 554 us; the launch traced here: 553 us
  Pallas kernels  307 us (55%)
  waiting for transfers between devices  74.8 us (14%)
  matrix products  51.8 us (9%)
  blocking collectives  45.2 us (8%)
  local copies, waits for them, and re-layouts  42.6 us (8%)
  other arithmetic  16.3 us (3%)
  between operations  14.3 us (3%)
    pallas_call x5, Pallas kernels, exchange(): pl.pallas_call(kernel, name=name, out_shape=(jax.ShapeDtypeStruct((gather...  219 us
    reduce_scatter x1, waiting for transfers between devices, local(): lax.psum_scatter(second, 'seq', scatter_dimension=1, tiled=True)  74.8 us
    psum x1, blocking collectives, local(): gains = lax.psum(gains, ('dp', 'seq', 'tensor'))  45.2 us
    pallas_call x1, Pallas kernels, gather_rows(): pl.pallas_call(kernel, name='gather_rows', out_shape=(jax.ShapeDtypeStruc...  26.2 us
    pallas_call x1, Pallas kernels, attend_back(): pl.pallas_call(kernel, name='attend_back', out_shape=(jax.ShapeDtypeStruc...  20.3 us
    unnamed x70, local copies, waits for them, and re-layouts  17.5 us
    dot_general x10, matrix products, dot_tn(): lax.dot_general(a, b, (((0,), (0,)), ((), ())), preferred_element_type=F32)  16.9 us
    pallas_call x1, Pallas kernels, attend(): pl.pallas_call(kernel, name='attend', out_shape=(part, span, span, part,...  15.6 us
  transfers between devices with their start and end apart: 3, of which 1 were waited for; matrix products, arithmetic and copies ran while one was open for 6% of the time, Pallas kernels for 24%

profile of v1, /device:TPU:0, one launch (start us, length us, event | category | flops | bytes accessed | tf_op | source)
XLA Modules:
  0.0 552.6 jit_solution(9307785264138029953)
XLA Ops:
  7.2 1.7 multiply_reduce_fusion
  9.6 2.5 multiply_convert_fusion.2.x_ref
  12.1 26.2 %gather_rows.1 = (bf16[4,2,4,128,512]{4,3,2,1,0:T(8,128)(2,1)}, s32[4,8,128]{2,1,0:T(8,128)}) custom-call(bf16[2,4,128,512]{3,2,1,0:T(8,128)(2,1)} %multiply_convert_fusion.2.x_ref, s32[8,128]{1,0:T(8,128)} %bitcast.201), custom_call_target="tpu_custom_call" | custom-call | tf_op jit(solution)/shard_map/gather_rows/pallas_call | solution.py:291
  39.0 1.3 slice.130
  40.3 3.1 slice.120
  46.4 1.3 reverse
  50.3 3.3 fusion.21
  53.6 13.6 %convolve.1 = bf16[6,2,512,512]{3,2,1,0:T(8,128)(2,1)} custom-call(bf16[4,2,512,512]{3,2,1,0:T(8,128)(2,1)} %bitcast.167, s32[4,2,1,512]{3,2,1,0:T(1,128)} %bitcast.196, s32[2,512,1]{2,1,0:T(8,128)} %squeeze.58.col_ref, f32[6,1,2560]{2,1,0:T(1,128)} %convert_element_type.105.base_ref), custom_call_target="tpu_custom_call" | custom-call | tf_op jit(solution)/shard_map/convolve/pallas_call | solution.py:413
  67.2 7.5 %fusion.10 = bf16[2,512,512]{2,1,0:T(8,128)(2,1)} fusion(f32[2,512,512,1]{2,1,0,3:T(8,128)} %fusion.21, bf16[6,2,512,512]{3,2,1,0:T(8,128)(2,1)} %convolve.1, bf16[6,512,512]{2,1,0:T(8,128)(2,1)S(1)} %copy-done), kind=kOutput, calls=%fused_computation.16 | convolution fusion | flops 3222274048 | bytes 12582912 | tf_op jit(solution)/shard_map/kmtd,kde->mte/dot_general | solution.py:713
  74.7 48.9 %exchange_one.1 = (bf16[3,2,4,128,512]{4,3,2,1,0:T(8,128)(2,1)}, f32[2,128,512]{2,1,0:T(8,128)}) custom-call(bf16[1,2,2,2,128,512]{5,4,3,2,1,0:T(8,128)(2,1)} %bitcast.184, bf16[2,4,128,512]{3,2,1,0:T(8,128)(2,1)} %bitcast.164, f32[1,512]{1,0:T(1,128)} %bitcast.205), custom_call_target="tpu_custom_call" | custom-call | tf_op jit(solution)/shard_map/exchange_one/pallas_call | solution.py:351
  123.6 15.6 %attend.1 = (bf16[2,512,128]{2,1,0:T(8,128)(2,1)}, bf16[3,2,512,128]{3,2,1,0:T(8,128)(2,1)}, bf16[3,2,512,128]{3,2,1,0:T(8,128)(2,1)}, bf16[2,512,128]{2,1,0:T(8...) custom-call(bf16[3,2,512,512]{3,2,1,0:T(8,128)(2,1)} %bitcast.168, s32[3,2,1,512]{3,2,1,0:T(1,128)} %bitcast.198, ...), custom_call_target="tpu_custom_call" | custom-call | tf_op jit(solution)/shard_map/attend/pallas_call | solution.py:543
  139.2 19.5 %exchange_two.1 = (bf16[1,2,4,128,512]{4,3,2,1,0:T(8,128)(2,1)}, f32[2,128,512]{2,1,0:T(8,128)}) custom-call(bf16[1,2,2,2,128,512]{5,4,3,2,1,0:T(8,128)(2,1)} %bitcast.185, f32[2,128,512]{2,1,0:T(8,128)} %get-tuple-element.42.refs_1_, f32[1,512]{1,0:T(1,128)} %bitcast.203), custom_call_target="tpu_custom_call" | custom-call | tf_op jit(solution)/shard_map/exchange_two/pallas_call | solution.py:351
  158.7 2.0 fusion.48
  162.1 2.1 multiply_convert_fusion
  164.3 1.6 fusion.14
  166.6 2.3 slice.147
  168.9 1.7 convolution_convert_fusion
  170.5 1.6 fusion.13
  172.1 1.6 fusion.16
  173.7 1.7 add_convert_fusion
  175.4 31.9 %exchange_three.1 = (bf16[1,4,4,128,512]{4,3,2,1,0:T(8,128)(2,1)}, f32[2,128,512]{2,1,0:T(8,128)}, f32[1,512]{1,0:T(1,128)}) custom-call(bf16[1,2,2,2,128,512]{5,4,3,2,1,0:T(8,128)(2,1)} %bitcast.174, bf16[1,2,2,2,128,512]{5,4,3,2,1,0:T(8,128)(2,1)} %bitcast.183, f32[2,128,512]{2,1,0:T(8,128)} %get-tuple-element.44.refs_2_, f32[1,512]{1,0:T(1,128)} %bitcast.204, ...), custom_call_target="tpu_custom_call" | custom-call | tf_op jit(solution)/shard_map/exchange_three/pallas_call | solution.py:351
  207.3 3.0 fusion.43
  210.3 20.3 %attend_back.1 = (bf16[2,512,128]{2,1,0:T(8,128)(2,1)}, bf16[3,2,512,128]{3,2,1,0:T(8,128)(2,1)}, bf16[3,2,512,128]{3,2,1,0:T(8,128)(2,1)}, bf16[3,2,512,512]{3,2,1,0:T(8,128)(2,1)}) custom-call(bf16[2,512,128]{2,1,0:T(8,128)(2,1)} %get-tuple-element.46.q_ref, bf16[3,2,512,128]{3,2,1,0:T(8,128)(2,1)} %get-tuple-element.47.k_ref, ...), custom_call_target="tpu_custom_call" | custom-call | tf_op jit(solution)/shard_map/attend_back/pallas_call | solution.py:612
  230.6 2.3 fusion.18
  232.9 3.5 fusion.20
  236.5 1.3 fusion.19
  238.8 4.0 copy.99
  242.9 64.3 %exchange_four.1 = (bf16[1,2,4,128,512]{4,3,2,1,0:T(8,128)(2,1)}, f32[2,128,512]{2,1,0:T(8,128)}, f32[1,512]{1,0:T(1,128)}) custom-call(bf16[3,2,2,2,128,512]{5,4,3,2,1,0:T(8,128)(2,1)} %bitcast.178, f32[2,128,512]{2,1,0:T(8,128)} %get-tuple-element.42.refs_1_, f32[1,512]{1,0:T(1,128)} %bitcast.206, f32[2,128,512]{2,1,0:T(8,128)} %get-tuple-element.51.refs_3_), custom_call_target="tpu_custom_call" | custom-call | tf_op jit(solution)/shard_map/exchange_four/pallas_call | solution.py:351
  307.2 1.8 convolution_convert_fusion.6
  309.1 1.7 convolution_convert_fusion.7
  311.4 6.6 %bitcast_convert_fusion = bf16[6,512,512]{2,1,0:T(8,128)(2,1)S(1)} fusion(bf16[6,2,512,512]{3,2,1,0:T(8,128)(2,1)} %convolve.1, bf16[2,512,512,1]{2,1,0,3:T(8,128)(2,1)S(1)} %bitcast.161), kind=kOutput, calls=%fused_computation | convolution fusion | flops 3222798336 | bytes 10485760 | tf_op jit(solution)/shard_map/kmtd,mte->kde/dot_general | solution.py:834
  318.0 2.2 pad_maximum_fusion
  321.2 3.2 convolution_bitcast_fusion
  324.4 5.3 convert_bitcast_fusion.g_ref
  329.7 2.0 copy.100
  331.8 74.8 %reduce-scatter.5.cloned.1.call-done = bf16[7,128,512]{2,1,0:T(8,128)(2,1)} async-done(((bf16[7,512,512]{2,1,0:T(8,128)(2,1)}), bf16[7,128,512]{2,1,0:T(8,128)(2,1)}) %reduce-scatter.5.cloned.1.call-update) | async-done | bytes 917520 | tf_op jit(solution)/shard_map/reduce_scatter | solution.py:844
  406.6 2.6 fusion.29
  409.2 3.3 broadcast_in_dim_reshape.16.col_ref
  412.5 1.6 pad_add_fusion
  416.4 12.7 %convolve_back.1 = bf16[4,2,512,512]{3,2,1,0:T(8,128)(2,1)} custom-call(bf16[6,2,512,512]{3,2,1,0:T(8,128)(2,1)} %convert_bitcast_fusion.g_ref, s32[2,1,512]{2,1,0:T(1,128)} %bitcast.200, s32[4,2,512,1]{3,2,1,0:T(8,128)} %broadcast_in_dim_reshape.16.col_ref, f32[6,1,2560]{2,1,0:T(1,128)} %maximum_convert_fusion.base_ref, f32[2,512,128]{2,1,0:T(8,128)} %slice.162.own_ref, ...), custom_call_target="tpu_custom_call" | custom-call | tf_op jit(solution)/shard_map/convolve_back/pallas_call | solution.py:465
  429.1 54.5 %exchange_five.1 = (bf16[1,2,4,128,512]{4,3,2,1,0:T(8,128)(2,1)}, f32[1,512]{1,0:T(1,128)}) custom-call(bf16[4,2,2,2,128,512]{5,4,3,2,1,0:T(8,128)(2,1)} %bitcast.166, bf16[2,4,128,512]{3,2,1,0:T(8,128)(2,1)} %bitcast.165, f32[1,512]{1,0:T(1,128)} %bitcast.207, f32[2,128,512]{2,1,0:T(8,128)} %get-tuple-element.53.refs_3_), custom_call_target="tpu_custom_call" | custom-call | tf_op jit(solution)/shard_map/exchange_five/pallas_call | solution.py:351
  484.3 45.2 %psum.21 = f32[3,512]{1,0:T(4,128)S(1)} all-reduce(f32[3,512]{1,0:T(4,128)S(1)} %pad_maximum_fusion.2), channel_id=1, replica_groups=mesh['dp'=2,'seq'=4,'tensor'=4] {'dp','seq','tensor'}, use_global_device_ids=true, to_apply=%region_1.2 | all-reduce | flops 1536 | bytes 12288 | tf_op jit(solution)/shard_map/psum | solution.py:846
  530.0 1.5 convert_element_type.119
  531.6 1.4 slice.163
  536.5 1.7 copy.82
  538.2 1.8 copy.88
  540.8 1.6 copy.85
  543.8 2.3 copy.113
  (114 shorter events, 20.9 us)
Async XLA Ops:
  7.2 60.0 %copy-start = (bf16[6,512,512]{2,1,0:T(8,128)(2,1)S(1)}, bf16[6,512,512]{2,1,0:T(8,128)(2,1)}, u32[]{:S(2)}) copy-start(bf16[6,512,512]{2,1,0:T(8,128)(2,1)} %param.20) | copy-start | bytes 9437188
  7.2 322.5 %reduce-scatter.7.cloned.1.call-start = ((), (), s32[]{:S(2)}) async-start(), calls=%async_computation.3 | async-start | bytes 2621440
  39.0 6.2 %copy-start.25 = (s32[1,8,128]{2,1,0:T(8,128)}, s32[1,8,128]{2,1,0:T(8,128)S(1)}, u32[]{:S(2)}) copy-start(s32[1,8,128]{2,1,0:T(8,128)S(1)} %get-tuple-element.124) | copy-start | bytes 12292
  40.3 6.0 %copy-start.23 = (bf16[6,2048]{1,0:T(8,128)(2,1)S(1)}, bf16[6,2048]{1,0:T(8,128)(2,1)}, u32[]{:S(2)}) copy-start(bf16[6,2048]{1,0:T(8,128)(2,1)} %param.18) | copy-start | bytes 73732
  50.2 3.3 copy-start.13
  50.3 3.3 copy-start.15
  50.3 3.3 copy-start.17
  123.6 35.1 %copy-start.11 = (bf16[512,512]{1,0:T(8,128)(2,1)S(1)}, bf16[512,512]{1,0:T(8,128)(2,1)}, u32[]{:S(2)}) copy-start(bf16[512,512]{1,0:T(8,128)(2,1)} %param.28) | copy-start | bytes 1572868
  158.7 2.1 copy-start.8
  158.7 2.1 copy-start.19
  160.8 1.2 copy-start.12
  160.8 1.3 copy-start.20
  232.9 3.6 copy-start.4
  232.9 3.6 copy-start.28
  236.4 1.3 copy-start.9
  236.4 1.3 copy-start.29
  242.8 163.7 %reduce-scatter.5.cloned.1.call-start = ((), (), s32[]{:S(2)}) async-start(), calls=%async_computation.2 | async-start | bytes 4587520 | tf_op jit(solution)/shard_map/reduce_scatter | solution.py:844
  242.8 64.4 %copy-start.18 = (bf16[2,512,128]{2,1,0:T(8,128)(2,1)S(1)}, bf16[2,512,128]{2,1,0:T(8,128)(2,1)}, u32[]{:S(2)}) copy-start(bf16[2,512,128]{2,1,0:T(8,128)(2,1)} %copy-done.17) | copy-start | bytes 786436
  242.9 66.2 %copy-start.16 = (bf16[2,512,128]{2,1,0:T(8,128)(2,1)S(1)}, bf16[2,512,128]{2,1,0:T(8,128)(2,1)}, u32[]{:S(2)}) copy-start(bf16[2,512,128]{2,1,0:T(8,128)(2,1)} %copy-done.15) | copy-start | bytes 786436
  307.2 3.6 copy-start.1
  307.2 3.6 copy-start.14
  320.2 1.0 copy-start.21
  320.2 209.8 %all-reduce.6.cloned.1.call-start = ((), (), s32[]{:S(2)}) async-start(), calls=%async_computation.4 | async-start | bytes 2883584 | tf_op jit(solution)/shard_map/psum | solution.py:844
  321.2 3.2 copy-start.2
  406.5 2.6 copy-start.22
  412.5 2.5 copy-start.24
  412.5 2.5 copy-start.5
  412.5 2.5 copy-start.6
  412.5 2.5 copy-start.7
  429.1 54.5 %copy-start.26 = (f32[1,512]{1,0:T(1,128)S(1)}, f32[1,512]{1,0:T(1,128)}, u32[]{:S(2)}) copy-start(f32[1,512]{1,0:T(1,128)} %get-tuple-element.57) | copy-start | bytes 6148
  429.1 54.5 %copy-start.27 = (f32[1,512]{1,0:T(1,128)S(1)}, f32[1,512]{1,0:T(1,128)}, u32[]{:S(2)}) copy-start(f32[1,512]{1,0:T(1,128)} %get-tuple-element.56) | copy-start | bytes 6148
  530.0 1.5 copy-start.3
  531.6 1.4 copy-start.10
Sparse Core Ops, SparseCore 0:
  242.9 75.3 reduce-scatter.6
  320.6 85.8 reduce-scatter.4
  408.9 48.9 all-reduce.5

commit v2 on v1

--- a/solution.py
+++ b/solution.py
@@ -39,19 +39,38 @@
     )
 
 
-def greet(seq_count, hops):
+def greet(seq_count, hops, wide=False, gains=False):
     s, t, y, c, core, far = place()
     barrier = pltpu.get_barrier_semaphore()
-    for peer in (core, far):
-        pl.semaphore_signal(barrier, inc=1, device_id={"tensor": peer}, device_id_type=MESH)
-    for h in range(1, hops + 1):
-        for there, peer in ((s - h >= 0, s - h), (s + h < seq_count, s + h)):
-
-            @pl.when(there)
+
+    def signal(device):
+        pl.semaphore_signal(barrier, inc=1, device_id=device, device_id_type=MESH)
+
+    signal({"tensor": core})
+    signal({"tensor": far})
+    if gains:
+        signal({"tensor": 3 - t})
+    if wide:
+        p = lax.axis_index("dp")
+        signal({"dp": 1 - p})
+        for j in range(seq_count):
+
+            @pl.when(s != j)
             def _():
-                pl.semaphore_signal(barrier, inc=1, device_id={"seq": peer}, device_id_type=MESH)
-
-    peers = 2 + jnp.minimum(s, hops) + jnp.minimum(seq_count - 1 - s, hops)
+                signal({"seq": j})
+                if gains:
+                    signal({"dp": 1 - p, "seq": j})
+
+        peers = 2 + gains + 1 + (seq_count - 1) * (1 + gains)
+    else:
+        for h in range(1, hops + 1):
+            for there, peer in ((s - h >= 0, s - h), (s + h < seq_count, s + h)):
+
+                @pl.when(there)
+                def _():
+                    signal({"seq": peer})
+
+        peers = 2 + jnp.minimum(s, hops) + jnp.minimum(seq_count - 1 - s, hops)
     pl.semaphore_wait(barrier, peers)
 
 
@@ -88,7 +107,7 @@
         )
 
     def there(self, h):
-        return True if h == 0 else lax.axis_index("seq") - h >= 0
+        return True if isinstance(h, int) and h == 0 else lax.axis_index("seq") - h >= 0
 
     def order(self):
         return [(h, m) for h in range(self.hops, -1, -1) for m in range(self.streams)]
@@ -223,6 +242,89 @@
                     self.copy(3, h, m, far, {"tensor": core}).wait_send()
 
                 when(self.there(h), act)
+
+
+class GradReduce:
+    def __init__(self, seq_count, source, result, scratch):
+        self.seq_count, self.source, self.result = seq_count, source, result
+        self.x_in, self.z_out, self.z_in, self.back_out, self.back_in, self.x_sem, self.z_sem, self.back_sem = scratch
+        self.half = self.x_in.shape[2]
+        self.rows = self.back_out.shape[1]
+
+    @staticmethod
+    def scratch(seq_count, chunks, depth, width):
+        rows, half = depth // seq_count, width // 2
+        return [
+            pltpu.VMEM((chunks, depth, half), BF),
+            pltpu.VMEM((chunks, depth, half), BF),
+            pltpu.VMEM((chunks, seq_count, rows, half), BF),
+            pltpu.VMEM((chunks, rows, half), BF),
+            pltpu.VMEM((chunks, rows, half), BF),
+            pltpu.SemaphoreType.DMA((2, chunks)),
+            pltpu.SemaphoreType.DMA((2, chunks, seq_count)),
+            pltpu.SemaphoreType.DMA((2, chunks)),
+        ]
+
+    def columns(self, p):
+        return pl.ds(pl.multiple_of(p * self.half, LANES), self.half)
+
+    def block(self, j):
+        return pl.ds(pl.multiple_of(j * self.rows, 16), self.rows)
+
+    def over(self, c):
+        p = lax.axis_index("dp")
+        return remote(
+            self.source(c).at[:, self.columns(1 - p)], self.x_in.at[c], self.x_sem.at[0, c], self.x_sem.at[1, c], {"dp": 1 - p}
+        )
+
+    def row_copy(self, c, j, slot):
+        return remote(
+            self.z_out.at[c, self.block(j)], self.z_in.at[c, slot], self.z_sem.at[0, c, j], self.z_sem.at[1, c, slot], {"seq": j}
+        )
+
+    def back(self, c):
+        p = lax.axis_index("dp")
+        return remote(
+            self.back_out.at[c], self.back_in.at[c], self.back_sem.at[0, c], self.back_sem.at[1, c], {"dp": 1 - p}
+        )
+
+    def others(self, action):
+        for j in range(self.seq_count):
+            pl.when(lax.axis_index("seq") != j)(functools.partial(action, j))
+
+    def start(self, c):
+        self.over(c).start()
+
+    def spread(self, c):
+        s, p = lax.axis_index("seq"), lax.axis_index("dp")
+        self.over(c).wait_recv()
+        mine = self.source(c)[:, self.columns(p)].astype(F32) + self.x_in[c].astype(F32)
+        self.z_out[c] = mine.astype(BF)
+        self.others(lambda j: self.row_copy(c, j, s).start())
+
+    def collect(self, c, acc):
+        s, p = lax.axis_index("seq"), lax.axis_index("dp")
+        here = self.block(s)
+        acc[...] = self.source(c)[here, self.columns(p)].astype(F32) + self.x_in[c, here].astype(F32)
+
+        def add(j):
+            self.row_copy(c, j, j).wait_recv()
+            acc[...] += self.z_in[c, j].astype(F32)
+
+        self.others(add)
+        self.back_out[c] = acc[...].astype(BF)
+        self.back(c).start()
+
+    def finish(self, c):
+        p = lax.axis_index("dp")
+        self.back(c).wait_recv()
+        self.result(c)[:, self.columns(p)] = self.back_out[c].astype(F32)
+        self.result(c)[:, self.columns(1 - p)] = self.back_in[c].astype(F32)
+
+    def drain(self, c):
+        self.over(c).wait_send()
+        self.others(lambda j: self.row_copy(c, j, lax.axis_index("seq")).wait_send())
+        self.back(c).wait_send()
 
 
 def params(cid=None):
@@ -302,28 +404,43 @@
     )(inputs, ids)
 
 
-def exchange(name, cid, seq_count, parts, others, reduce_hops, gather_hops, finish, extra):
+def exchange(name, cid, seq_count, parts, others, reduce_hops, gather_hops, finish, extra, grads=None):
     per_part = parts[0].shape[1]
     rows, width = parts[0].shape[4:]
     streams = per_part * len(parts)
     hops = max(reduce_hops, gather_hops)
+    given = [] if grads is None else [grads]
+    chunks = 0 if grads is None else grads.shape[0]
+    sums, tools = [], []
+    if chunks:
+        depth, wide = grads.shape[1:]
+        sums = [jax.ShapeDtypeStruct((chunks, depth // seq_count, wide), F32)]
+        tools = [pltpu.VMEM((depth // seq_count, wide // 2), F32)] + GradReduce.scratch(seq_count, chunks, depth, wide)
 
     def kernel(*refs):
         refs = list(refs)
         part_refs = [refs.pop(0) for _ in parts]
         other_refs = [refs.pop(0) for _ in others]
+        grad_ref = refs.pop(0) if chunks else None
         out = refs.pop(0)
         extra_refs = [refs.pop(0) for _ in extra]
+        sum_ref = refs.pop(0) if chunks else None
+        grad_tools = [refs.pop(0) for _ in tools]
         acc = refs.pop(0)
         gather_sem = refs.pop(0)
         s, t, y, c, core, far = place()
-        greet(seq_count, hops)
+        greet(seq_count, hops, wide=bool(chunks))
+        if chunks:
+            grad_acc = grad_tools.pop(0)
+            gr = GradReduce(seq_count, lambda c: grad_ref.at[c], lambda c: sum_ref.at[c], grad_tools)
         rs = ReduceScatter(
             seq_count, reduce_hops, streams, lambda h, m: part_refs[m // per_part].at[h, m % per_part], refs
         )
         ag = AllGather(seq_count, gather_hops, streams, out, gather_sem)
         for h, m in rs.order():
             rs.start(h, m)
+        for k in range(chunks):
+            gr.start(k)
         for h in range(1, gather_hops + 1):
             for m in range(streams):
                 ag.clear(h, m)
@@ -332,10 +449,14 @@
         for h, m in rs.order():
             if h:
                 rs.hop(h, m)
+        for k in range(chunks):
+            gr.spread(k)
         for m in range(streams):
             rs.total(m, acc)
             out[0, m, t] = finish(m, acc[...], other_refs, extra_refs)
             ag.start(m)
+        for k in range(chunks):
+            gr.collect(k, grad_acc)
         for h in range(gather_hops + 1):
             for m in range(streams):
                 if h:
@@ -345,20 +466,24 @@
         for h in range(gather_hops + 1):
             for m in range(streams):
                 ag.finish(h, m)
+        for k in range(chunks):
+            gr.finish(k)
+            gr.drain(k)
         rs.drain()
         ag.drain()
 
     return pl.pallas_call(
         kernel,
         name=name,
-        out_shape=(jax.ShapeDtypeStruct((gather_hops + 1, streams, 4, rows, width), BF),) + tuple(extra),
-        in_specs=in_vmem(len(parts) + len(others)),
-        out_specs=tuple(in_vmem(1 + len(extra))),
-        scratch_shapes=[pltpu.VMEM((rows, width), F32)]
+        out_shape=(jax.ShapeDtypeStruct((gather_hops + 1, streams, 4, rows, width), BF),) + tuple(extra) + tuple(sums),
+        in_specs=in_vmem(len(parts) + len(others) + len(given)),
+        out_specs=tuple(in_vmem(1 + len(extra) + len(sums))),
+        scratch_shapes=tools
+        + [pltpu.VMEM((rows, width), F32)]
         + AllGather.scratch(gather_hops, streams)
         + ReduceScatter.scratch(reduce_hops, streams, rows, width),
         compiler_params=params(cid),
-    )(*parts, *others)
+    )(*parts, *others, *given)
 
 
 def norm_of(values, gain_row):
@@ -627,6 +752,201 @@
         ],
         compiler_params=params(),
     )(q, k, v, lse, grad_out, row_ids, col_ids, wq, wk, wv, wo)
+
+
+def tail(
+    grad_stu, filter_proj, lag_proj, conv, lag_stack, lag_masks, row_ids, col_ids, base, x, gain, grad_one, gains, seq_count
+):
+    count, length_all, width = conv.shape
+    streams, _, quarter, _ = x.shape
+    length = length_all // streams
+    lag_order, channels = lag_proj.shape[:2]
+    wide = base.shape[2]
+    blocks = length // LANES
+    hops = seq_count - 1
+    chunks = count + 1
+    steps = seq_count * streams
+    rows = width // seq_count
+    gain_rows = 8
+
+    def kernel(
+        gs_ref, fp_ref, lp_ref, conv_ref, lag_ref, mask_ref, row_ref, col_ref, base_ref, x_ref, gain_ref, one_ref, gains_ref,
+        out, filter_out, lag_out, gain_out,
+        strip, mask, acc, terms, grad_conv, grads, lag_ext, total, grad_acc, gather_sem,
+        gain_own, gain_near, gain_sum, gain_far, near_sem, far_sem, *scratch,
+    ):
+        s, t, y, c, core, far = place()
+        p = lax.axis_index("dp")
+        rs_scratch, gr_scratch = scratch[:6], scratch[6:]
+        greet(seq_count, hops, wide=True, gains=True)
+
+        def source(k):
+            return grads.at[k]
+
+        def result(k):
+            return filter_out.at[k] if k < count else lag_out
+
+        gr = GradReduce(seq_count, source, result, gr_scratch)
+        rs = ReduceScatter(seq_count, hops, streams, lambda h, m: terms.at[h, m], rs_scratch)
+        ag = AllGather(seq_count, 0, streams, out, gather_sem)
+
+        @pl.loop(0, count)
+        def _(k):
+            grads[k] = dot_tn(conv_ref[k], gs_ref[...]).astype(BF)
+            gr.start(k)
+            grad_conv[k] = dot_nt(gs_ref[...], fp_ref[k]).astype(BF)
+
+        grads[count] = jnp.zeros_like(grads.at[count])
+        for i in range(lag_order):
+            grads[count, :, i * channels : (i + 1) * channels] = dot_tn(gs_ref[...], lag_ref[i]).astype(BF)
+        gr.start(count)
+        for m in range(streams):
+            lag_ext[m] = jnp.zeros_like(lag_ext.at[m])
+            for i in range(lag_order):
+                term = dot_nt(gs_ref[m * length : (m + 1) * length], lp_ref[i]) * mask_ref[i, m]
+                lag_ext[m, 7 - i : 7 - i + length] += term
+        strips(base_ref, strip)
+        mine = pl.ds(pl.multiple_of(t * channels, LANES), channels)
+
+        def step_of(i):
+            return seq_count - 1 - i // streams, i - i // streams * streams
+
+        @pl.loop(0, steps)
+        def _(i):
+            h, m = step_of(i)
+
+            @pl.when(h <= s)
+            def _():
+                mask[...] = jnp.where(col_ref[h, m] == row_ref[m], 1.0, 0.0).astype(BF)
+                acc[...] = jnp.zeros_like(acc)
+
+                @pl.when(h == 0)
+                def _():
+                    acc[:, mine] = lag_ext[m, 8:]
+
+                @pl.when(h == 1)
+                def _():
+                    acc[length - 8 :, mine] = lag_ext[m, :8]
+
+                @pl.loop(0, count)
+                def _(k):
+                    pieces = []
+                    for a in range(blocks):
+                        start = pl.multiple_of(LANES * (blocks * h + blocks - 1 - a), LANES)
+                        pieces.append(strip[k, :, pl.ds(start, length)] * mask[a * LANES : (a + 1) * LANES])
+                    block = grad_conv[k, pl.ds(pl.multiple_of(m * length, LANES), length)]
+                    acc[...] += jnp.dot(jnp.concatenate(pieces, axis=0), block, preferred_element_type=F32)
+
+                for quarter_y in range(2):
+                    for quarter_c in range(2):
+                        first = (2 * quarter_y + quarter_c) * quarter
+                        terms[h, m, quarter_y, quarter_c] = acc[first : first + quarter].astype(BF)
+                rs.start(h, m)
+
+            @pl.when(i >= 1)
+            def _():
+                rs.middle(*step_of(i - 1))
+
+            @pl.when((i >= 2) & (i < steps - streams + 2))
+            def _():
+                rs.hop(*step_of(i - 2))
+
+            @pl.when(i < chunks)
+            def _():
+                gr.spread(i)
+
+            @pl.when((i >= 3) & (i < chunks + 3))
+            def _():
+                gr.collect(i - 3, grad_acc)
+
+        rs.middle(0, streams - 1)
+        for k in range(steps, chunks):
+            gr.spread(k)
+        gain_own[...] = jnp.zeros_like(gain_own)
+        for m in range(streams):
+            rs.total(m, total)
+            grad_in, gain_grad = norm_back(x_ref[m, t].astype(F32), gain_ref[...], total[...])
+            out[0, m, t] = (one_ref[m] + grad_in).astype(BF)
+            ag.start(m)
+            gain_own[0:1] += gain_grad
+        gain_own[1:3] = gains_ref[...]
+        gain_near[t] = gain_own[...]
+
+        def near_copy(j, slot):
+            return remote(gain_own, gain_near.at[slot], near_sem.at[0, j], near_sem.at[1, slot], {"tensor": j})
+
+        for j in range(4):
+            pl.when(t != j)(lambda: near_copy(j, t).start())
+        for k in range(max(steps - 3, 0), chunks):
+            gr.collect(k, grad_acc)
+        for m in range(streams):
+            ag.pass_on(0, m)
+        for j in range(4):
+            pl.when(t != j)(lambda: near_copy(j, j).wait_recv())
+        gain_sum[...] = gain_near[0] + gain_near[1] + gain_near[2] + gain_near[3]
+        me = p * seq_count + s
+
+        def far_copy(j, slot):
+            d, q = j // seq_count, j % seq_count
+            return remote(
+                gain_sum.at[:, q * rows : (q + 1) * rows], gain_far.at[slot], far_sem.at[0, j], far_sem.at[1, slot],
+                {"dp": d, "seq": q},
+            )
+
+        gain_far[me] = gain_sum[:, pl.ds(pl.multiple_of(s * rows, LANES), rows)]
+        for j in range(2 * seq_count):
+            pl.when(me != j)(lambda: far_copy(j, me).start())
+        for m in range(streams):
+            ag.finish(0, m)
+        for k in range(chunks):
+            gr.finish(k)
+        for j in range(2 * seq_count):
+            pl.when(me != j)(lambda: far_copy(j, j).wait_recv())
+        gain_out[...] = functools.reduce(jnp.add, [gain_far[j] for j in range(2 * seq_count)])
+        for j in range(4):
+            pl.when(t != j)(lambda: near_copy(j, t).wait_send())
+        for j in range(2 * seq_count):
+            pl.when(me != j)(lambda: far_copy(j, me).wait_send())
+        for k in range(chunks):
+            gr.drain(k)
+        rs.drain()
+        ag.drain()
+
+    return pl.pallas_call(
+        kernel,
+        name="tail",
+        out_shape=(
+            jax.ShapeDtypeStruct((1, streams, 4, quarter, width), BF),
+            jax.ShapeDtypeStruct((count, rows, width), F32),
+            jax.ShapeDtypeStruct((rows, width), F32),
+            jax.ShapeDtypeStruct((gain_rows, rows), F32),
+        ),
+        in_specs=in_vmem(13),
+        out_specs=tuple(in_vmem(4)),
+        scratch_shapes=[
+            pltpu.VMEM((count, LANES, wide), BF),
+            pltpu.VMEM((length, length), BF),
+            pltpu.VMEM((length, width), F32),
+            pltpu.VMEM((seq_count, streams, 2, 2, quarter, width), BF),
+            pltpu.VMEM((count, length_all, width), BF),
+            pltpu.VMEM((chunks, width, width), BF),
+            pltpu.VMEM((streams, length + 8, channels), F32),
+            pltpu.VMEM((quarter, width), F32),
+            pltpu.VMEM((rows, width // 2), F32),
+            AllGather.scratch(0, streams)[0],
+            pltpu.VMEM((gain_rows, width), F32),
+            pltpu.VMEM((4, gain_rows, width), F32),
+            pltpu.VMEM((gain_rows, width), F32),
+            pltpu.VMEM((2 * seq_count, gain_rows, rows), F32),
+            pltpu.SemaphoreType.DMA((2, 4)),
+            pltpu.SemaphoreType.DMA((2, 2 * seq_count)),
+        ]
+        + ReduceScatter.scratch(hops, streams, quarter, width)
+        + GradReduce.scratch(seq_count, chunks, width, width),
+        compiler_params=params(7),
+    )(
+        grad_stu, filter_proj, lag_proj, conv, lag_stack, lag_masks, row_ids, col_ids, base, x, gain, grad_one, gains
+    )
 
 
 def gated_unit(gate_pre, up_pre):
@@ -778,42 +1098,6 @@
         q, k, v, lse, grad_att_out, id_rows[: hops + 1], id_cols[0], query_weight, key_weight, value_weight, output_weight
     )
 
-    def finish_four(m, total, others, extra):
-        hidden_ref, gain_ref, grad_ref = others
-        grad_in, gain_grad = norm_back(hidden_ref[m], gain_ref[...], total)
-        grad_one = grad_ref[m] + grad_in
-        extra[0][m] = grad_one
-        extra[1][...] = gain_grad if m == 0 else extra[1][...] + gain_grad
-        return grad_one.astype(BF)
-
-    grad_stu, grad_one, attn_gain_grad = exchange(
-        "exchange_four", 5, seq_count, [split(attn_part)], [hidden_one, row(attention_gain), grad_two], hops, 0,
-        finish_four, [state, gain_state],
-    )
-    grad_stu = whole(grad_stu)[0]
-
-    grad_conv = jnp.einsum("mte,kde->kmtd", grad_stu, filter_proj, preferred_element_type=F32).astype(BF)
-    grad_lagged = jnp.einsum("mte,ice->imtc", grad_stu, lag_proj, preferred_element_type=F32)
-    ext_grad = jnp.zeros((streams, 8 + length, channels), F32)
-    for step in range(1, lag_order + 1):
-        term = jnp.where(masks[step - 1], grad_lagged[step - 1], 0.0)
-        ext_grad = ext_grad + jnp.pad(term, ((0, 0), (8 - step, step), (0, 0)))
-    terms = convolve_back(
-        grad_conv, id_rows[0], id_cols, base_back, ext_grad[:, 8:], ext_grad[:, :8], seq_count
-    )
-
-    def finish_five(m, total, others, extra):
-        x_ref, gain_ref, grad_ref = others
-        grad_in, gain_grad = norm_back(x_ref[m, place()[1]].astype(F32), gain_ref[...], total)
-        extra[0][...] = gain_grad if m == 0 else extra[0][...] + gain_grad
-        return (grad_ref[m] + grad_in).astype(BF)
-
-    input_gradient, stu_gain_grad = exchange(
-        "exchange_five", 6, seq_count, [split(terms)], [quarters(x), row(stu_gain), grad_one], seq_count - 1, 0,
-        finish_five, [gain_state],
-    )
-    input_gradient = whole(input_gradient)[0]
-
     tokens_flat = streams * length
     go = grad_att_out.reshape(tokens_flat, width)
     first = jnp.concatenate(
@@ -828,36 +1112,79 @@
         ],
         axis=1,
     )
-    stu = grad_stu.reshape(tokens_flat, width)
-    second = jnp.concatenate(
-        [
-            jnp.einsum("kmtd,mte->kde", conv, grad_stu, preferred_element_type=F32).astype(BF),
-            jnp.concatenate(
-                [dot_tn(stu, lag_stack[i].reshape(tokens_flat, channels)).astype(BF) for i in range(lag_order)]
-                + [jnp.zeros((width, width - lag_order * channels), BF)],
-                axis=1,
-            )[None],
-        ],
-        axis=0,
+
+    def finish_four(m, total, others, extra):
+        hidden_ref, gain_ref, grad_ref = others
+        grad_in, gain_grad = norm_back(hidden_ref[m], gain_ref[...], total)
+        grad_one = grad_ref[m] + grad_in
+        extra[0][m] = grad_one
+        extra[1][...] = gain_grad if m == 0 else extra[1][...] + gain_grad
+        return grad_one.astype(BF)
+
+    fused = width // seq_count % LANES == 0
+    results = exchange(
+        "exchange_four", 5, seq_count, [split(attn_part)], [hidden_one, row(attention_gain), grad_two], hops, 0,
+        finish_four, [state, gain_state], first[None] if fused else None,
     )
-    first = lax.psum(lax.psum_scatter(first, "seq", scatter_dimension=0, tiled=True), "dp").astype(F32)
-    second = lax.psum(lax.psum_scatter(second, "seq", scatter_dimension=1, tiled=True), "dp").astype(F32)
-    gains = jnp.concatenate([stu_gain_grad, attn_gain_grad, feed_gain_grad], axis=0)
-    gains = lax.psum(gains, ("dp", "seq", "tensor"))
-    gain_width = width // seq_count
-    gains = lax.dynamic_slice_in_dim(gains, lax.axis_index("seq") * gain_width, gain_width, 1)
+    grad_stu, grad_one, attn_gain_grad = results[:3]
+    grad_stu = whole(grad_stu)[0]
+    lag_masks = jnp.stack(masks).astype(F32)
+    if fused:
+        first = results[3][0]
+        input_gradient, filter_grad, lag_grad, gains = tail(
+            grad_stu.reshape(tokens_flat, width), filter_proj, lag_proj, conv.reshape(count, tokens_flat, width),
+            lag_stack.reshape(lag_order, tokens_flat, channels), lag_masks, id_rows[0], id_cols, base_back,
+            quarters(x), row(stu_gain), grad_one, jnp.concatenate([attn_gain_grad, feed_gain_grad], axis=0), seq_count,
+        )
+        input_gradient = whole(input_gradient)[0]
+    else:
+        grad_conv = jnp.einsum("mte,kde->kmtd", grad_stu, filter_proj, preferred_element_type=F32).astype(BF)
+        grad_lagged = jnp.einsum("mte,ice->imtc", grad_stu, lag_proj, preferred_element_type=F32)
+        ext_grad = jnp.zeros((streams, 8 + length, channels), F32)
+        for step in range(1, lag_order + 1):
+            term = jnp.where(masks[step - 1], grad_lagged[step - 1], 0.0)
+            ext_grad = ext_grad + jnp.pad(term, ((0, 0), (8 - step, step), (0, 0)))
+        terms = convolve_back(
+            grad_conv, id_rows[0], id_cols, base_back, ext_grad[:, 8:], ext_grad[:, :8], seq_count
+        )
+
+        def finish_five(m, total, others, extra):
+            x_ref, gain_ref, grad_ref = others
+            grad_in, gain_grad = norm_back(x_ref[m, place()[1]].astype(F32), gain_ref[...], total)
+            extra[0][...] = gain_grad if m == 0 else extra[0][...] + gain_grad
+            return (grad_ref[m] + grad_in).astype(BF)
+
+        input_gradient, stu_gain_grad = exchange(
+            "exchange_five", 6, seq_count, [split(terms)], [quarters(x), row(stu_gain), grad_one], seq_count - 1, 0,
+            finish_five, [gain_state],
+        )
+        input_gradient = whole(input_gradient)[0]
+        stu = grad_stu.reshape(tokens_flat, width)
+        filter_part = jnp.einsum("kmtd,mte->kde", conv, grad_stu, preferred_element_type=F32).astype(BF)
+        lag_part = jnp.concatenate(
+            [dot_tn(stu, lag_stack[i].reshape(tokens_flat, channels)).astype(BF) for i in range(lag_order)], axis=1
+        )
+        first = lax.psum(lax.psum_scatter(first, "seq", scatter_dimension=0, tiled=True), "dp").astype(F32)
+        filter_grad = lax.psum(
+            lax.psum_scatter(filter_part, "seq", scatter_dimension=1, tiled=True), "dp"
+        ).astype(F32)
+        lag_grad = lax.psum(lax.psum_scatter(lag_part, "seq", scatter_dimension=0, tiled=True), "dp").astype(F32)
+        gains = jnp.concatenate([stu_gain_grad, attn_gain_grad, feed_gain_grad], axis=0)
+        gains = lax.psum(gains, ("dp", "seq", "tensor"))
+        gain_width = width // seq_count
+        gains = lax.dynamic_slice_in_dim(gains, lax.axis_index("seq") * gain_width, gain_width, 1)
 
     hidden_units = gate_weight.shape[1]
     cols = query_weight.shape[1]
     cuts = [hidden_units, 2 * hidden_units, 3 * hidden_units]
     cuts += [cuts[-1] + cols, cuts[-1] + 2 * cols, cuts[-1] + 3 * cols]
     gate_grad, up_grad, down_grad, query_grad, key_grad, value_grad, output_grad = jnp.split(first, cuts, axis=1)
-    lag_grad = second[count][:, : lag_order * channels].T.reshape(lag_order, channels, -1)
+    lag_grad = lag_grad[:, : lag_order * channels].T.reshape(lag_order, channels, -1)
     return (
         layer_output[:, None],
         input_gradient[:, None],
         gains[0],
-        second[:count],
+        filter_grad,
         lag_grad,
         gains[1],
         query_grad,

time: 554 us -> 421 us (0.76)
  waiting for transfers between devices: 74.8 us -> 0 us
  Pallas kernels: 307 us -> 355 us
  blocking collectives: 45.2 us -> 0 us
  matrix products: 51.8 us -> 26.6 us
  local copies, waits for them, and re-layouts: 42.6 us -> 26.5 us
  between operations: 14.3 us -> 1.05 us
    pallas_call x1, Pallas kernels: 12.7 us -> 100 us  [tail(): pl.pallas_call(kernel, name='tail', out_shape=(jax.ShapeDtypeStruct((1, s...]
    reduce_scatter x1 -> x0, waiting for transfers between devices: 74.8 us -> none  [local(): lax.psum_scatter(second, 'seq', scatter_dimension=1, tiled=True)]
    psum x1 -> x0, blocking collectives: 45.2 us -> none  [local(): gains = lax.psum(gains, ('dp', 'seq', 'tensor'))]
    pallas_call x5 -> x4, Pallas kernels: 219 us -> 179 us  [exchange(): pl.pallas_call(kernel, name=name, out_shape=(jax.ShapeDtypeStruct((gather...]
    dot_general x3 -> x0, matrix products: 15.1 us -> none  [the longest x1 6.58 us: local(): jnp.einsum('kmtd,mte->kde', conv, grad_stu, preferred_element_type=F32)]
    dot_general x10 -> x7, matrix products: 16.9 us -> 7.95 us  [dot_tn(): lax.dot_general(a, b, (((0,), (0,)), ((), ())), preferred_element_type=F32)]
    unnamed x70 -> x58, local copies, waits for them, and re-layouts: 17.5 us -> 9.58 us
  transfers between devices with their start and end apart: 3 -> 0, of which waited for: 1 -> 0; matrix products, arithmetic and copies ran while one was open for 6% -> 0% of each run, Pallas kernels for 24% -> 0%
where the time goes in v2:
time: 421 us; the launch traced here: 420 us
  Pallas kernels  355 us (84%)
  matrix products  26.6 us (6%)
  local copies, waits for them, and re-layouts  26.5 us (6%)
  other arithmetic  10.8 us (3%)
    pallas_call x4, Pallas kernels, exchange(): pl.pallas_call(kernel, name=name, out_shape=(jax.ShapeDtypeStruct((gather...  179 us
    pallas_call x1, Pallas kernels, tail(): pl.pallas_call(kernel, name='tail', out_shape=(jax.ShapeDtypeStruct((1, s...  100 us
    pallas_call x1, Pallas kernels, gather_rows(): pl.pallas_call(kernel, name='gather_rows', out_shape=(jax.ShapeDtypeStruc...  26.2 us
    pallas_call x1, Pallas kernels, attend_back(): pl.pallas_call(kernel, name='attend_back', out_shape=(jax.ShapeDtypeStruc...  20.5 us
    pallas_call x1, Pallas kernels, attend(): pl.pallas_call(kernel, name='attend', out_shape=(part, span, span, part,...  15.6 us
    pallas_call x1, Pallas kernels, convolve(): pl.pallas_call(kernel, name='convolve', out_shape=jax.ShapeDtypeStruct((c...  13.8 us
    unnamed x58, local copies, waits for them, and re-layouts  9.58 us

profile of v2, /device:TPU:0, one launch (start us, length us, event | category | flops | bytes accessed | tf_op | source)
XLA Modules:
  0.0 420.3 jit_solution(16634571007991735596)
XLA Ops:
  0.7 1.6 multiply_reduce_fusion
  2.3 2.5 multiply_convert_fusion.2.x_ref
  4.8 26.2 %gather_rows.1 = (bf16[4,2,4,128,512]{4,3,2,1,0:T(8,128)(2,1)}, s32[4,8,128]{2,1,0:T(8,128)}) custom-call(bf16[2,4,128,512]{3,2,1,0:T(8,128)(2,1)} %multiply_convert_fusion.2.x_ref, s32[8,128]{1,0:T(8,128)} %bitcast.171), custom_call_target="tpu_custom_call" | custom-call | tf_op jit(solution)/shard_map/gather_rows/pallas_call | solution.py:393
  31.0 1.8 slice.99
  32.9 0.8 dynamic-slice_bitcast_fusion.1
  33.9 1.7 fusion.30
  36.3 2.1 fusion.20
  38.4 1.1 squeeze.46.col_ref
  39.5 1.3 reverse
  41.3 0.7 convert_element_type.79.base_ref
  42.0 13.8 %convolve.1 = bf16[6,2,512,512]{3,2,1,0:T(8,128)(2,1)} custom-call(bf16[4,2,512,512]{3,2,1,0:T(8,128)(2,1)} %bitcast.128, s32[4,2,1,512]{3,2,1,0:T(1,128)} %bitcast.163, s32[2,512,1]{2,1,0:T(8,128)} %squeeze.46.col_ref, f32[6,1,2560]{2,1,0:T(1,128)} %convert_element_type.79.base_ref), custom_call_target="tpu_custom_call" | custom-call | tf_op jit(solution)/shard_map/convolve/pallas_call | solution.py:538
  55.7 7.5 %fusion.9 = bf16[2,512,512]{2,1,0:T(8,128)(2,1)} fusion(f32[2,512,512,1]{2,1,3,0:T(8,128)} %fusion.20, bf16[6,2,512,512]{3,2,1,0:T(8,128)(2,1)} %convolve.1, bf16[6,512,512]{2,1,0:T(8,128)(2,1)S(1)} %copy-done.4), kind=kOutput, calls=%fused_computation.12 | convolution fusion | flops 3222274048 | bytes 12582912 | tf_op jit(solution)/shard_map/kmtd,kde->mte/dot_general | solution.py:1033
  63.2 48.9 %exchange_one.1 = (bf16[3,2,4,128,512]{4,3,2,1,0:T(8,128)(2,1)}, f32[2,128,512]{2,1,0:T(8,128)}) custom-call(bf16[1,2,2,2,128,512]{5,4,3,2,1,0:T(8,128)(2,1)} %bitcast.154, bf16[2,4,128,512]{3,2,1,0:T(8,128)(2,1)} %bitcast.126, f32[1,512]{1,0:T(1,128)} %bitcast.175), custom_call_target="tpu_custom_call" | custom-call | tf_op jit(solution)/shard_map/exchange_one/pallas_call | solution.py:475
  112.8 15.6 %attend.1 = (bf16[2,512,128]{2,1,0:T(8,128)(2,1)}, bf16[3,2,512,128]{3,2,1,0:T(8,128)(2,1)}, bf16[3,2,512,128]{3,2,1,0:T(8,128)(2,1)}, bf16[2,512,128]{2,1,0:T(8...) custom-call(bf16[3,2,512,512]{3,2,1,0:T(8,128)(2,1)} %bitcast.131, s32[3,2,1,512]{3,2,1,0:T(1,128)} %bitcast.165, ...), custom_call_target="tpu_custom_call" | custom-call | tf_op jit(solution)/shard_map/attend/pallas_call | solution.py:668
  128.4 19.5 %exchange_two.1 = (bf16[1,2,4,128,512]{4,3,2,1,0:T(8,128)(2,1)}, f32[2,128,512]{2,1,0:T(8,128)}) custom-call(bf16[1,2,2,2,128,512]{5,4,3,2,1,0:T(8,128)(2,1)} %bitcast.157, f32[2,128,512]{2,1,0:T(8,128)} %get-tuple-element.45.refs_1_, f32[1,512]{1,0:T(1,128)} %bitcast.173), custom_call_target="tpu_custom_call" | custom-call | tf_op jit(solution)/shard_map/exchange_two/pallas_call | solution.py:475
  147.9 2.0 fusion.41
  149.9 0.7 fusion.40
  151.1 2.1 multiply_convert_fusion
  153.3 0.7 fusion.13
  154.0 0.7 fusion.12
  154.7 0.8 fusion.15
  155.5 1.3 copy-done.10
  156.8 0.7 fusion.42
  157.5 1.7 add_convert_fusion
  159.3 1.7 convolution_convert_fusion
  160.9 32.0 %exchange_three.1 = (bf16[1,4,4,128,512]{4,3,2,1,0:T(8,128)(2,1)}, f32[2,128,512]{2,1,0:T(8,128)}, f32[1,512]{1,0:T(1,128)}) custom-call(bf16[1,2,2,2,128,512]{5,4,3,2,1,0:T(8,128)(2,1)} %bitcast.137, bf16[1,2,2,2,128,512]{5,4,3,2,1,0:T(8,128)(2,1)} %bitcast.153, f32[2,128,512]{2,1,0:T(8,128)} %get-tuple-element.47.refs_2_, f32[1,512]{1,0:T(1,128)} %bitcast.174, ...), custom_call_target="tpu_custom_call" | custom-call | tf_op jit(solution)/shard_map/exchange_three/pallas_call | solution.py:475
  192.9 3.0 fusion.38
  196.0 20.5 %attend_back.1 = (bf16[2,512,128]{2,1,0:T(8,128)(2,1)}, bf16[3,2,512,128]{3,2,1,0:T(8,128)(2,1)}, bf16[3,2,512,128]{3,2,1,0:T(8,128)(2,1)}, bf16[3,2,512,512]{3,2,1,0:T(8,128)(2,1)}) custom-call(bf16[2,512,128]{2,1,0:T(8,128)(2,1)} %get-tuple-element.49.q_ref, bf16[3,2,512,128]{3,2,1,0:T(8,128)(2,1)} %get-tuple-element.50.k_ref, ...), custom_call_target="tpu_custom_call" | custom-call | tf_op jit(solution)/shard_map/attend_back/pallas_call | solution.py:737
  216.6 0.8 copy-done.17
  217.4 1.2 fusion.17
  218.6 1.7 fusion.19
  220.3 1.7 fusion.18
  222.0 1.2 fusion.16
  223.2 79.0 %exchange_four.1 = (bf16[1,2,4,128,512]{4,3,2,1,0:T(8,128)(2,1)}, f32[2,128,512]{2,1,0:T(8,128)}, f32[1,512]{1,0:T(1,128)}, f32[1,128,2048]{2,1,0:T(8,128)}) custom-call(bf16[3,2,2,2,128,512]{5,4,3,2,1,0:T(8,128)(2,1)} %bitcast.140, f32[2,128,512]{2,1,0:T(8,128)} %get-tuple-element.45.refs_1_, f32[1,512]{1,0:T(1,128)} %bitcast.176, ...), custom_call_target="tpu_custom_call" | custom-call | tf_op jit(solution)/shard_map/exchange_four/pallas_call | solution.py:475
  302.2 1.3 pad_maximum_fusion.2.gains_ref
  303.5 1.0 pad_maximum_fusion.lag_ref
  305.3 1.3 add_convert_fusion.1.mask_ref
  306.6 3.4 broadcast_in_dim_reshape.16.col_ref
  310.1 0.7 maximum_convert_fusion.base_ref
  310.7 100.0 %tail.1 = (bf16[1,2,4,128,512]{4,3,2,1,0:T(8,128)(2,1)}, f32[6,128,512]{2,1,0:T(8,128)}, f32[128,512]{1,0:T(8,128)}, f32[8,128]{1,0:T(8,128)}) custom-call(bf16[1024,512]{1,0:T(8,128)(2,1)} %bitcast.148, bf16[6,512,512]{2,1,0:T(8,128)(2,1)} %fp_ref.1, bf16[3,128,512]{2,1,0:T(8,128)(2,1)} %lp_ref.1, bf16[6,1024,512]{2,1,0:T(8,128)(2,1)} %bitcast.124, ...), custom_call_target="tpu_custom_call" | custom-call | tf_op jit(solution)/shard_map/tail/pallas_call | solution.py:915
  410.7 0.9 slice_bitcast_fusion.1
  411.7 0.8 copy.162
  412.5 1.3 slice_bitcast_fusion.3
  413.8 0.9 slice_bitcast_fusion
  414.7 0.8 copy.166
  416.2 0.7 copy.165
  416.9 2.3 copy.187
  419.2 1.1 copy.188
  (76 shorter events, 4.2 us)
Async XLA Ops:
  0.6 150.0 %copy-start = (bf16[512,512]{1,0:T(8,128)(2,1)S(1)}, bf16[512,512]{1,0:T(8,128)(2,1)}, u32[]{:S(2)}) copy-start(bf16[512,512]{1,0:T(8,128)(2,1)} %param.29) | copy-start | bytes 1572868
  31.0 2.7 copy-start.18
  31.0 2.8 copy-start.22
  32.8 3.4 copy-start.12
  33.7 4.7 %copy-start.21 = (s32[1,8,128]{2,1,0:T(8,128)}, s32[1,8,128]{2,1,0:T(8,128)S(1)}, u32[]{:S(2)}) copy-start(s32[1,8,128]{2,1,0:T(8,128)S(1)} %get-tuple-element.169) | copy-start | bytes 12292
  35.6 0.7 copy-start.5
  35.6 2.8 copy-start.7
  35.6 3.9 copy-start.20
  42.0 13.8 %copy-start.4 = (bf16[6,512,512]{2,1,0:T(8,128)(2,1)S(1)}, bf16[6,512,512]{2,1,0:T(8,128)(2,1)}, u32[]{:S(2)}) copy-start(bf16[6,512,512]{2,1,0:T(8,128)(2,1)} %fp_ref.1) | copy-start | bytes 9437188
  63.2 48.9 %copy-start.19 = (s32[4,8,128]{2,1,0:T(8,128)S(1)}, s32[4,8,128]{2,1,0:T(8,128)}, u32[]{:S(2)}) copy-start(s32[4,8,128]{2,1,0:T(8,128)} %get-tuple-element.42) | copy-start | bytes 49156
  112.8 35.1 %copy-start.9 = (bf16[512,512]{1,0:T(8,128)(2,1)S(1)}, bf16[512,512]{1,0:T(8,128)(2,1)}, u32[]{:S(2)}) copy-start(bf16[512,512]{1,0:T(8,128)(2,1)} %param.28) | copy-start | bytes 1572868
  147.8 2.1 copy-start.3
  147.8 2.1 copy-start.15
  149.9 1.2 copy-start.13
  155.5 1.3 copy-start.10
  196.0 20.5 %copy-start.2 = (bf16[3,2,4,128,512]{4,3,2,1,0:T(8,128)(2,1)S(1)}, bf16[3,2,4,128,512]{4,3,2,1,0:T(8,128)(2,1)}, u32[]{:S(2)}) copy-start(bf16[3,2,4,128,512]{4,3,2,1,0:T(8,128)(2,1)} %get-tuple-element.43) | copy-start | bytes 9437188
  216.5 0.9 copy-start.17
  216.5 2.1 copy-start.25
  218.6 1.7 copy-start.24
  220.3 1.7 copy-start.1
  220.3 1.7 copy-start.16
  223.2 79.0 %copy-start.23 = (f32[1,512]{1,0:T(1,128)S(1)}, f32[1,512]{1,0:T(1,128)}, u32[]{:S(2)}) copy-start(f32[1,512]{1,0:T(1,128)} %get-tuple-element.62) | copy-start | bytes 6148
  223.2 80.3 %copy-start.6 = (bf16[2,512,128]{2,1,0:T(8,128)(2,1)S(1)}, bf16[2,512,128]{2,1,0:T(8,128)(2,1)}, u32[]{:S(2)}) copy-start(bf16[2,512,128]{2,1,0:T(8,128)(2,1)} %copy-done.5) | copy-start | bytes 786436
  223.2 80.3 %copy-start.8 = (bf16[2,512,128]{2,1,0:T(8,128)(2,1)S(1)}, bf16[2,512,128]{2,1,0:T(8,128)(2,1)}, u32[]{:S(2)}) copy-start(bf16[2,512,128]{2,1,0:T(8,128)(2,1)} %copy-done.7) | copy-start | bytes 786436
  310.7 103.1 %copy-start.14 = (f32[1,128,2048]{2,1,0:T(8,128)S(1)}, f32[1,128,2048]{2,1,0:T(8,128)}, u32[]{:S(2)}) copy-start(f32[1,128,2048]{2,1,0:T(8,128)} %get-tuple-element.67) | copy-start | bytes 3145732
  413.8 5.4 %copy-start.11 = (f32[6,128,512]{2,1,0:T(8,128)S(1)}, f32[6,128,512]{2,1,0:T(8,128)}, u32[]{:S(2)}) copy-start(f32[6,128,512]{2,1,0:T(8,128)} %get-tuple-element.194) | copy-start | bytes 4718596

commit v3 on v2

--- a/solution.py
+++ b/solution.py
@@ -370,11 +370,11 @@
             def _():
                 out_ids[h] = jnp.full(out_ids.shape[1:], -1, jnp.int32)
 
-        for h in range(1, hops + 1):
-            for m in range(streams):
+        for m in range(streams):
+            for h in range(1, hops + 1):
                 ag.arrive(h, m)
-        for h in range(1, hops + 1):
-            for m in range(streams):
+        for m in range(streams):
+            for h in range(1, hops + 1):
                 ag.pass_on(h, m)
         for h in range(1, hops + 1):
             for m in range(streams):
@@ -457,11 +457,12 @@
             ag.start(m)
         for k in range(chunks):
             gr.collect(k, grad_acc)
-        for h in range(gather_hops + 1):
-            for m in range(streams):
-                if h:
-                    ag.arrive(h, m)
-            for m in range(streams):
+        for m in range(streams):
+            ag.pass_on(0, m)
+            for h in range(1, gather_hops + 1):
+                ag.arrive(h, m)
+        for m in range(streams):
+            for h in range(1, gather_hops + 1):
                 ag.pass_on(h, m)
         for h in range(gather_hops + 1):
             for m in range(streams):
@@ -510,6 +511,25 @@
     _, streams, length, width = rows.shape
     count, _, wide = base.shape
     blocks = length // LANES
+    at_once = seq_count <= 4
+
+    def whole_kernel(x_ref, row_ref, col_ref, base_ref, out_ref, strip, mask, left):
+        strips(base_ref, strip)
+
+        @pl.loop(0, streams)
+        def _(m):
+            for h in range(seq_count):
+                mask[:, h * length : (h + 1) * length] = jnp.where(col_ref[m] == row_ref[h, m], 1.0, 0.0).astype(BF)
+            right = jnp.concatenate([x_ref[h, m] for h in range(seq_count)], axis=0)
+
+            @pl.loop(0, count)
+            def _(k):
+                for a in range(blocks):
+                    for h in range(seq_count):
+                        start = LANES * (blocks * (seq_count - h) - 1 - a)
+                        down, across = slice(a * LANES, (a + 1) * LANES), slice(h * length, (h + 1) * length)
+                        left[down, across] = strip[k, :, start : start + length] * mask[down, across]
+                out_ref[k, m] = jnp.dot(left[...], right, preferred_element_type=F32).astype(BF)
 
     def kernel(x_ref, row_ref, col_ref, base_ref, out_ref, strip, mask, acc):
         strips(base_ref, strip)
@@ -535,16 +555,17 @@
             def _(k):
                 out_ref[k, m] = acc[k].astype(BF)
 
+    span = seq_count * length if at_once else length
     return pl.pallas_call(
-        kernel,
+        whole_kernel if at_once else kernel,
         name="convolve",
         out_shape=jax.ShapeDtypeStruct((count, streams, length, width), BF),
         in_specs=in_vmem(4),
         out_specs=in_vmem(1)[0],
         scratch_shapes=[
             pltpu.VMEM((count, LANES, wide), BF),
-            pltpu.VMEM((length, length), BF),
-            pltpu.VMEM((count, length, width), F32),
+            pltpu.VMEM((length, span), BF),
+            pltpu.VMEM((length, span), BF) if at_once else pltpu.VMEM((count, length, width), F32),
         ],
         compiler_params=params(),
     )(rows, row_ids, col_ids, base)
@@ -755,7 +776,7 @@
 
 
 def tail(
-    grad_stu, filter_proj, lag_proj, conv, lag_stack, lag_masks, row_ids, col_ids, base, x, gain, grad_one, gains, seq_count
+    grad_stu, filter_proj, lag_proj, conv, lag_stack, lag_masks, row_ids, ext_ids, base, x, gain, grad_one, gains, seq_count
 ):
     count, length_all, width = conv.shape
     streams, _, quarter, _ = x.shape
@@ -770,9 +791,9 @@
     gain_rows = 8
 
     def kernel(
-        gs_ref, fp_ref, lp_ref, conv_ref, lag_ref, mask_ref, row_ref, col_ref, base_ref, x_ref, gain_ref, one_ref, gains_ref,
+        gs_ref, fp_ref, lp_ref, conv_ref, lag_ref, mask_ref, row_ref, ext_ref, base_ref, x_ref, gain_ref, one_ref, gains_ref,
         out, filter_out, lag_out, gain_out,
-        strip, mask, acc, terms, grad_conv, grads, lag_ext, total, grad_acc, gather_sem,
+        strip, mask, cols, left, acc, terms, grad_conv, grads, lag_ext, total, grad_acc, gather_sem,
         gain_own, gain_near, gain_sum, gain_far, near_sem, far_sem, *scratch,
     ):
         s, t, y, c, core, far = place()
@@ -790,11 +811,20 @@
         rs = ReduceScatter(seq_count, hops, streams, lambda h, m: terms.at[h, m], rs_scratch)
         ag = AllGather(seq_count, 0, streams, out, gather_sem)
 
+        early = min(2, count)
+
         @pl.loop(0, count)
         def _(k):
             grads[k] = dot_tn(conv_ref[k], gs_ref[...]).astype(BF)
             gr.start(k)
-            grad_conv[k] = dot_nt(gs_ref[...], fp_ref[k]).astype(BF)
+            product = dot_nt(gs_ref[...], fp_ref[k]).astype(BF)
+            for m in range(streams):
+                here = pl.ds(pl.multiple_of(k * length, LANES), length)
+                grad_conv[m, here] = product[m * length : (m + 1) * length]
+
+            @pl.when(k >= count - early)
+            def _():
+                gr.spread(k - (count - early))
 
         grads[count] = jnp.zeros_like(grads.at[count])
         for i in range(lag_order):
@@ -806,7 +836,18 @@
                 term = dot_nt(gs_ref[m * length : (m + 1) * length], lp_ref[i]) * mask_ref[i, m]
                 lag_ext[m, 7 - i : 7 - i + length] += term
         strips(base_ref, strip)
+        turned = jnp.transpose(ext_ref[...].astype(F32))
+        for j in range(steps):
+            cols[j] = turned[:, j : j + 1]
         mine = pl.ds(pl.multiple_of(t * channels, LANES), channels)
+        spread_at = {}
+        collect_at = {}
+        for k in range(early, chunks):
+            if 2 * (k - early) < steps:
+                spread_at[2 * (k - early)] = k
+        for k in range(chunks):
+            if 2 * k + 3 < steps and k < early + len(spread_at):
+                collect_at[2 * k + 3] = k
 
         def step_of(i):
             return seq_count - 1 - i // streams, i - i // streams * streams
@@ -817,25 +858,21 @@
 
             @pl.when(h <= s)
             def _():
-                mask[...] = jnp.where(col_ref[h, m] == row_ref[m], 1.0, 0.0).astype(BF)
-                acc[...] = jnp.zeros_like(acc)
+                mask[...] = jnp.where(cols[h * streams + m] == row_ref[m].astype(F32), 1.0, 0.0).astype(BF)
+                for k in range(count):
+                    for a in range(blocks):
+                        start = pl.multiple_of(LANES * (blocks * h + blocks - 1 - a), LANES)
+                        down = slice(a * LANES, (a + 1) * LANES)
+                        left[down, k * length : (k + 1) * length] = strip[k, :, pl.ds(start, length)] * mask[down]
+                acc[...] = jnp.dot(left[...], grad_conv[m], preferred_element_type=F32)
 
                 @pl.when(h == 0)
                 def _():
-                    acc[:, mine] = lag_ext[m, 8:]
+                    acc[:, mine] += lag_ext[m, 8:]
 
                 @pl.when(h == 1)
                 def _():
-                    acc[length - 8 :, mine] = lag_ext[m, :8]
-
-                @pl.loop(0, count)
-                def _(k):
-                    pieces = []
-                    for a in range(blocks):
-                        start = pl.multiple_of(LANES * (blocks * h + blocks - 1 - a), LANES)
-                        pieces.append(strip[k, :, pl.ds(start, length)] * mask[a * LANES : (a + 1) * LANES])
-                    block = grad_conv[k, pl.ds(pl.multiple_of(m * length, LANES), length)]
-                    acc[...] += jnp.dot(jnp.concatenate(pieces, axis=0), block, preferred_element_type=F32)
+                    acc[length - 8 :, mine] += lag_ext[m, :8]
 
                 for quarter_y in range(2):
                     for quarter_c in range(2):
@@ -851,16 +888,13 @@
             def _():
                 rs.hop(*step_of(i - 2))
 
-            @pl.when(i < chunks)
-            def _():
-                gr.spread(i)
-
-            @pl.when((i >= 3) & (i < chunks + 3))
-            def _():
-                gr.collect(i - 3, grad_acc)
+            for step, k in spread_at.items():
+                pl.when(i == step)(functools.partial(gr.spread, k))
+            for step, k in collect_at.items():
+                pl.when(i == step)(functools.partial(gr.collect, k, grad_acc))
 
         rs.middle(0, streams - 1)
-        for k in range(steps, chunks):
+        for k in range(early + len(spread_at), chunks):
             gr.spread(k)
         gain_own[...] = jnp.zeros_like(gain_own)
         for m in range(streams):
@@ -877,10 +911,10 @@
 
         for j in range(4):
             pl.when(t != j)(lambda: near_copy(j, t).start())
-        for k in range(max(steps - 3, 0), chunks):
-            gr.collect(k, grad_acc)
         for m in range(streams):
             ag.pass_on(0, m)
+        for k in range(len(collect_at), chunks):
+            gr.collect(k, grad_acc)
         for j in range(4):
             pl.when(t != j)(lambda: near_copy(j, j).wait_recv())
         gain_sum[...] = gain_near[0] + gain_near[1] + gain_near[2] + gain_near[3]
@@ -926,9 +960,11 @@
         scratch_shapes=[
             pltpu.VMEM((count, LANES, wide), BF),
             pltpu.VMEM((length, length), BF),
+            pltpu.VMEM((steps, length, 1), F32),
+            pltpu.VMEM((length, count * length), BF),
             pltpu.VMEM((length, width), F32),
             pltpu.VMEM((seq_count, streams, 2, 2, quarter, width), BF),
-            pltpu.VMEM((count, length_all, width), BF),
+            pltpu.VMEM((streams, count * length, width), BF),
             pltpu.VMEM((chunks, width, width), BF),
             pltpu.VMEM((streams, length + 8, channels), F32),
             pltpu.VMEM((quarter, width), F32),
@@ -945,7 +981,7 @@
         + GradReduce.scratch(seq_count, chunks, width, width),
         compiler_params=params(7),
     )(
-        grad_stu, filter_proj, lag_proj, conv, lag_stack, lag_masks, row_ids, col_ids, base, x, gain, grad_one, gains
+        grad_stu, filter_proj, lag_proj, conv, lag_stack, lag_masks, row_ids, ext_ids, base, x, gain, grad_one, gains
     )
 
 
@@ -1085,26 +1121,35 @@
         extra[1][...] = gain_grad if m == 0 else extra[1][...] + gain_grad
         return grad_two.astype(BF)
 
-    shape = (1, streams, length, width)
-    both, grad_two, feed_gain_grad = exchange(
-        "exchange_three", 4, seq_count, [split(feed_part.reshape(shape)), split(layer_part.reshape(shape))],
-        [hidden_two, row(feed_gain), quarters(grad_three)], 0, 0, finish_three, [state, gain_state],
-    )
-    both = whole(both)[0]
-    grad_att_out = both[:streams]
-    layer_output = both[streams:]
-
-    dq, dk, dv, attn_part = attend_back(
-        q, k, v, lse, grad_att_out, id_rows[: hops + 1], id_cols[0], query_weight, key_weight, value_weight, output_weight
-    )
-
-    tokens_flat = streams * length
-    go = grad_att_out.reshape(tokens_flat, width)
-    first = jnp.concatenate(
+    fused = width // seq_count % LANES == 0
+    feed_grads = jnp.stack(
         [
             dot_tn(feed_in, grad_gate).astype(BF),
             dot_tn(feed_in, grad_up).astype(BF),
             dot_tn(flat_three, inner).astype(BF),
+        ]
+    )
+    shape = (1, streams, length, width)
+    results = exchange(
+        "exchange_three", 4, seq_count, [split(feed_part.reshape(shape)), split(layer_part.reshape(shape))],
+        [hidden_two, row(feed_gain), quarters(grad_three)], 0, 0, finish_three, [state, gain_state],
+        feed_grads if fused else None,
+    )
+    both, grad_two, feed_gain_grad = results[:3]
+    if fused:
+        feed_grads = results[3]
+    both = whole(both)[0]
+    grad_att_out = both[:streams]
+    layer_output = both[streams:]
+
+    dq, dk, dv, attn_part = attend_back(
+        q, k, v, lse, grad_att_out, id_rows[: hops + 1], id_cols[0], query_weight, key_weight, value_weight, output_weight
+    )
+
+    tokens_flat = streams * length
+    go = grad_att_out.reshape(tokens_flat, width)
+    attn_grads = jnp.concatenate(
+        [
             dot_tn(attn_ext[0].reshape(tokens_flat, width), dq.reshape(tokens_flat, -1)).astype(BF),
             dot_tn(attn_ext.reshape(-1, width), dk.reshape(-1, dk.shape[-1])).astype(BF),
             dot_tn(attn_ext.reshape(-1, width), dv.reshape(-1, dv.shape[-1])).astype(BF),
@@ -1121,19 +1166,19 @@
         extra[1][...] = gain_grad if m == 0 else extra[1][...] + gain_grad
         return grad_one.astype(BF)
 
-    fused = width // seq_count % LANES == 0
     results = exchange(
         "exchange_four", 5, seq_count, [split(attn_part)], [hidden_one, row(attention_gain), grad_two], hops, 0,
-        finish_four, [state, gain_state], first[None] if fused else None,
+        finish_four, [state, gain_state], attn_grads[None] if fused else None,
     )
     grad_stu, grad_one, attn_gain_grad = results[:3]
     grad_stu = whole(grad_stu)[0]
     lag_masks = jnp.stack(masks).astype(F32)
     if fused:
-        first = results[3][0]
+        attn_grads = results[3][0]
         input_gradient, filter_grad, lag_grad, gains = tail(
             grad_stu.reshape(tokens_flat, width), filter_proj, lag_proj, conv.reshape(count, tokens_flat, width),
-            lag_stack.reshape(lag_order, tokens_flat, channels), lag_masks, id_rows[0], id_cols, base_back,
+            lag_stack.reshape(lag_order, tokens_flat, channels), lag_masks, id_rows[0],
+            id_ext.reshape(seq_count * streams, length), base_back,
             quarters(x), row(stu_gain), grad_one, jnp.concatenate([attn_gain_grad, feed_gain_grad], axis=0), seq_count,
         )
         input_gradient = whole(input_gradient)[0]
@@ -1164,7 +1209,10 @@
         lag_part = jnp.concatenate(
             [dot_tn(stu, lag_stack[i].reshape(tokens_flat, channels)).astype(BF) for i in range(lag_order)], axis=1
         )
-        first = lax.psum(lax.psum_scatter(first, "seq", scatter_dimension=0, tiled=True), "dp").astype(F32)
+        feed_grads = lax.psum(
+            lax.psum_scatter(feed_grads, "seq", scatter_dimension=1, tiled=True), "dp"
+        ).astype(F32)
+        attn_grads = lax.psum(lax.psum_scatter(attn_grads, "seq", scatter_dimension=0, tiled=True), "dp").astype(F32)
         filter_grad = lax.psum(
             lax.psum_scatter(filter_part, "seq", scatter_dimension=1, tiled=True), "dp"
         ).astype(F32)
@@ -1174,11 +1222,9 @@
         gain_width = width // seq_count
         gains = lax.dynamic_slice_in_dim(gains, lax.axis_index("seq") * gain_width, gain_width, 1)
 
-    hidden_units = gate_weight.shape[1]
     cols = query_weight.shape[1]
-    cuts = [hidden_units, 2 * hidden_units, 3 * hidden_units]
-    cuts += [cuts[-1] + cols, cuts[-1] + 2 * cols, cuts[-1] + 3 * cols]
-    gate_grad, up_grad, down_grad, query_grad, key_grad, value_grad, output_grad = jnp.split(first, cuts, axis=1)
+    gate_grad, up_grad, down_grad = feed_grads
+    query_grad, key_grad, value_grad, output_grad = jnp.split(attn_grads, [cols, 2 * cols, 3 * cols], axis=1)
     lag_grad = lag_grad[:, : lag_order * channels].T.reshape(lag_order, channels, -1)
     return (
         layer_output[:, None],

time: 421 us -> 383 us (0.910)
  Pallas kernels: 355 us -> 323 us
    pallas_call x4, Pallas kernels: 179 us -> 150 us  [exchange(): pl.pallas_call(kernel, name=name, out_shape=(jax.ShapeDtypeStruct((gather...]
    pallas_call x1, Pallas kernels: 100 us -> 88 us  [tail(): pl.pallas_call(kernel, name='tail', out_shape=(jax.ShapeDtypeStruct((1, s...]
    pallas_call x1, Pallas kernels: 13.8 us -> 22.7 us  [convolve(): pl.pallas_call(whole_kernel if at_once else kernel, name='convolve', out_...]
    unnamed x58 -> x56, local copies, waits for them, and re-layouts: 9.58 us -> 7.88 us
where the time goes in v3:
time: 383 us; the launch traced here: 382 us
  Pallas kernels  323 us (84%)
  matrix products  23.9 us (6%)
  local copies, waits for them, and re-layouts  22.7 us (6%)
  other arithmetic  11.9 us (3%)
    pallas_call x4, Pallas kernels, exchange(): pl.pallas_call(kernel, name=name, out_shape=(jax.ShapeDtypeStruct((gather...  150 us
    pallas_call x1, Pallas kernels, tail(): pl.pallas_call(kernel, name='tail', out_shape=(jax.ShapeDtypeStruct((1, s...  88 us
    pallas_call x1, Pallas kernels, gather_rows(): pl.pallas_call(kernel, name='gather_rows', out_shape=(jax.ShapeDtypeStruc...  26.2 us
    pallas_call x1, Pallas kernels, convolve(): pl.pallas_call(whole_kernel if at_once else kernel, name='convolve', out_...  22.7 us
    pallas_call x1, Pallas kernels, attend_back(): pl.pallas_call(kernel, name='attend_back', out_shape=(jax.ShapeDtypeStruc...  20.5 us
    pallas_call x1, Pallas kernels, attend(): pl.pallas_call(kernel, name='attend', out_shape=(part, span, span, part,...  15.6 us
    unnamed x56, local copies, waits for them, and re-layouts  7.88 us

profile of v3, /device:TPU:0, one launch (start us, length us, event | category | flops | bytes accessed | tf_op | source)
XLA Modules:
  0.0 382.1 jit_solution(1303827201450801221)
XLA Ops:
  0.7 1.6 multiply_reduce_fusion
  2.3 2.5 multiply_convert_fusion.2.x_ref
  4.8 26.2 %gather_rows.1 = (bf16[4,2,4,128,512]{4,3,2,1,0:T(8,128)(2,1)}, s32[4,8,128]{2,1,0:T(8,128)}) custom-call(bf16[2,4,128,512]{3,2,1,0:T(8,128)(2,1)} %multiply_convert_fusion.2.x_ref, s32[8,128]{1,0:T(8,128)} %bitcast.180), custom_call_target="tpu_custom_call" | custom-call | tf_op jit(solution)/shard_map/gather_rows/pallas_call | solution.py:393
  31.0 1.8 slice.99
  33.1 0.7 copy.159
  34.5 0.7 copy-done.5
  35.2 2.1 fusion.15
  37.2 1.1 squeeze.46.col_ref
  38.4 1.3 reverse
  40.1 0.7 convert_element_type.79.base_ref
  40.8 22.7 %convolve.1 = bf16[6,2,512,512]{3,2,1,0:T(8,128)(2,1)} custom-call(bf16[4,2,512,512]{3,2,1,0:T(8,128)(2,1)} %bitcast.139, s32[4,2,1,512]{3,2,1,0:T(1,128)} %bitcast.172, s32[2,512,1]{2,1,0:T(8,128)} %squeeze.46.col_ref, f32[6,1,2560]{2,1,0:T(1,128)} %convert_element_type.79.base_ref), custom_call_target="tpu_custom_call" | custom-call | tf_op jit(solution)/shard_map/convolve/pallas_call | solution.py:559
  63.5 7.5 %fusion.9 = bf16[2,512,512]{2,1,0:T(8,128)(2,1)} fusion(f32[2,512,512,1]{2,1,3,0:T(8,128)} %fusion.15, bf16[6,2,512,512]{3,2,1,0:T(8,128)(2,1)} %convolve.1, bf16[6,512,512]{2,1,0:T(8,128)(2,1)S(1)} %copy-done.4), kind=kOutput, calls=%fused_computation.12 | convolution fusion | flops 3222274048 | bytes 12582912 | tf_op jit(solution)/shard_map/kmtd,kde->mte/dot_general | solution.py:1069
  71.0 34.6 %exchange_one.1 = (bf16[3,2,4,128,512]{4,3,2,1,0:T(8,128)(2,1)}, f32[2,128,512]{2,1,0:T(8,128)}) custom-call(bf16[1,2,2,2,128,512]{5,4,3,2,1,0:T(8,128)(2,1)} %bitcast.164, bf16[2,4,128,512]{3,2,1,0:T(8,128)(2,1)} %bitcast.137, f32[1,512]{1,0:T(1,128)} %bitcast.184), custom_call_target="tpu_custom_call" | custom-call | tf_op jit(solution)/shard_map/exchange_one/pallas_call | solution.py:476
  106.2 15.6 %attend.1 = (bf16[2,512,128]{2,1,0:T(8,128)(2,1)}, bf16[3,2,512,128]{3,2,1,0:T(8,128)(2,1)}, bf16[3,2,512,128]{3,2,1,0:T(8,128)(2,1)}, bf16[2,512,128]{2,1,0:T(8...) custom-call(bf16[3,2,512,512]{3,2,1,0:T(8,128)(2,1)} %bitcast.142, s32[3,2,1,512]{3,2,1,0:T(1,128)} %bitcast.174, ...), custom_call_target="tpu_custom_call" | custom-call | tf_op jit(solution)/shard_map/attend/pallas_call | solution.py:689
  121.8 19.5 %exchange_two.1 = (bf16[1,2,4,128,512]{4,3,2,1,0:T(8,128)(2,1)}, f32[2,128,512]{2,1,0:T(8,128)}) custom-call(bf16[1,2,2,2,128,512]{5,4,3,2,1,0:T(8,128)(2,1)} %bitcast.165, f32[2,128,512]{2,1,0:T(8,128)} %get-tuple-element.46.refs_1_, f32[1,512]{1,0:T(1,128)} %bitcast.182), custom_call_target="tpu_custom_call" | custom-call | tf_op jit(solution)/shard_map/exchange_two/pallas_call | solution.py:476
  141.3 2.0 fusion.36
  143.4 0.7 fusion.35
  144.6 2.1 multiply_convert_fusion
  146.7 0.7 fusion.12
  147.4 0.7 fusion.13
  148.2 0.8 fusion.14
  148.9 1.3 pad_maximum_fusion.refs_5_
  150.3 0.7 fusion.37
  151.0 1.7 add_convert_fusion
  152.7 1.7 convolution_convert_fusion
  154.4 56.3 %exchange_three.1 = (bf16[1,4,4,128,512]{4,3,2,1,0:T(8,128)(2,1)}, f32[2,128,512]{2,1,0:T(8,128)}, f32[1,512]{1,0:T(1,128)}, f32[3,128,512]{2,1,0:T(8,128)}) custom-call(bf16[1,2,2,2,128,512]{5,4,3,2,1,0:T(8,128)(2,1)} %bitcast.148, bf16[1,2,2,2,128,512]{5,4,3,2,1,0:T(8,128)(2,1)} %bitcast.163, f32[2,128,512]{2,1,0:T(8,128)} %get-tuple-element.48.refs_2_, ...), custom_call_target="tpu_custom_call" | custom-call | tf_op jit(solution)/shard_map/exchange_three/pallas_call | solution.py:476
  210.8 3.0 fusion.33
  213.8 20.5 %attend_back.1 = (bf16[2,512,128]{2,1,0:T(8,128)(2,1)}, bf16[3,2,512,128]{3,2,1,0:T(8,128)(2,1)}, bf16[3,2,512,128]{3,2,1,0:T(8,128)(2,1)}, bf16[3,2,512,512]{3,2,1,0:T(8,128)(2,1)}) custom-call(bf16[2,512,128]{2,1,0:T(8,128)(2,1)} %get-tuple-element.50.q_ref, bf16[3,2,512,128]{3,2,1,0:T(8,128)(2,1)} %get-tuple-element.51.k_ref, ...), custom_call_target="tpu_custom_call" | custom-call | tf_op jit(solution)/shard_map/attend_back/pallas_call | solution.py:758
  234.4 0.8 copy-done.17
  235.7 1.0 convolution_convert_fusion.7
  236.9 1.0 convolution_convert_fusion.6
  238.5 0.9 maximum_bitcast_fusion.refs_4_
  239.4 39.3 %exchange_four.1 = (bf16[1,2,4,128,512]{4,3,2,1,0:T(8,128)(2,1)}, f32[2,128,512]{2,1,0:T(8,128)}, f32[1,512]{1,0:T(1,128)}, f32[1,128,512]{2,1,0:T(8,128)}) custom-call(bf16[3,2,2,2,128,512]{5,4,3,2,1,0:T(8,128)(2,1)} %bitcast.151, f32[2,128,512]{2,1,0:T(8,128)} %get-tuple-element.46.refs_1_, f32[1,512]{1,0:T(1,128)} %bitcast.185, ...), custom_call_target="tpu_custom_call" | custom-call | tf_op jit(solution)/shard_map/exchange_four/pallas_call | solution.py:476
  278.7 1.3 pad_maximum_fusion.3.gains_ref
  280.0 1.0 pad_maximum_fusion.1.lag_ref
  281.8 1.3 add_convert_fusion.1.mask_ref
  283.1 0.6 reshape_reshape.16.ext_ref
  283.8 0.7 maximum_convert_fusion.base_ref
  284.5 88.0 %tail.1 = (bf16[1,2,4,128,512]{4,3,2,1,0:T(8,128)(2,1)}, f32[6,128,512]{2,1,0:T(8,128)}, f32[128,512]{1,0:T(8,128)}, f32[8,128]{1,0:T(8,128)}) custom-call(bf16[1024,512]{1,0:T(8,128)(2,1)} %bitcast.158, bf16[6,512,512]{2,1,0:T(8,128)(2,1)} %fp_ref.1, bf16[3,128,512]{2,1,0:T(8,128)(2,1)} %lp_ref.1, bf16[6,1024,512]{2,1,0:T(8,128)(2,1)} %bitcast.135, ...), custom_call_target="tpu_custom_call" | custom-call | tf_op jit(solution)/shard_map/tail/pallas_call | solution.py:949
  372.6 1.0 slice_bitcast_fusion.3
  373.6 0.8 copy.145
  374.4 1.3 slice_bitcast_fusion.5
  375.7 0.7 slice_bitcast_fusion.4
  376.4 0.7 copy.148
  377.1 2.1 slice_bitcast_fusion
  379.2 0.8 copy.149
  380.0 1.0 copy.162
  381.0 1.1 copy.163
  (76 shorter events, 4.7 us)
Async XLA Ops:
  0.6 143.5 %copy-start = (bf16[512,512]{1,0:T(8,128)(2,1)S(1)}, bf16[512,512]{1,0:T(8,128)(2,1)}, u32[]{:S(2)}) copy-start(bf16[512,512]{1,0:T(8,128)(2,1)} %param.29) | copy-start | bytes 1572868
  31.0 2.0 copy-start.18
  32.8 2.3 copy-start.11
  33.0 4.3 %copy-start.21 = (s32[1,8,128]{2,1,0:T(8,128)}, s32[1,8,128]{2,1,0:T(8,128)S(1)}, u32[]{:S(2)}) copy-start(s32[1,8,128]{2,1,0:T(8,128)S(1)} %get-tuple-element.171) | copy-start | bytes 12292
  34.5 0.7 copy-start.5
  34.5 2.8 copy-start.7
  34.5 3.9 %copy-start.20 = (bf16[6,2048]{1,0:T(8,128)(2,1)S(1)}, bf16[6,2048]{1,0:T(8,128)(2,1)}, u32[]{:S(2)}) copy-start(bf16[6,2048]{1,0:T(8,128)(2,1)} %param.18) | copy-start | bytes 73732
  40.8 22.7 %copy-start.4 = (bf16[6,512,512]{2,1,0:T(8,128)(2,1)S(1)}, bf16[6,512,512]{2,1,0:T(8,128)(2,1)}, u32[]{:S(2)}) copy-start(bf16[6,512,512]{2,1,0:T(8,128)(2,1)} %fp_ref.1) | copy-start | bytes 9437188
  71.0 34.6 %copy-start.19 = (s32[4,8,128]{2,1,0:T(8,128)S(1)}, s32[4,8,128]{2,1,0:T(8,128)}, u32[]{:S(2)}) copy-start(s32[4,8,128]{2,1,0:T(8,128)} %get-tuple-element.43) | copy-start | bytes 49156
  106.2 35.1 %copy-start.9 = (bf16[512,512]{1,0:T(8,128)(2,1)S(1)}, bf16[512,512]{1,0:T(8,128)(2,1)}, u32[]{:S(2)}) copy-start(bf16[512,512]{1,0:T(8,128)(2,1)} %param.28) | copy-start | bytes 1572868
  141.3 2.1 copy-start.3
  141.3 2.1 copy-start.14
  143.4 1.2 copy-start.12
  213.8 20.5 %copy-start.2 = (bf16[3,2,4,128,512]{4,3,2,1,0:T(8,128)(2,1)S(1)}, bf16[3,2,4,128,512]{4,3,2,1,0:T(8,128)(2,1)}, u32[]{:S(2)}) copy-start(bf16[3,2,4,128,512]{4,3,2,1,0:T(8,128)(2,1)} %get-tuple-element.44) | copy-start | bytes 9437188
  234.3 0.9 copy-start.17
  234.3 1.4 copy-start.24
  235.7 1.1 copy-start.23
  236.8 1.2 copy-start.1
  236.8 1.3 copy-start.16
  239.4 39.3 %copy-start.22 = (f32[1,512]{1,0:T(1,128)S(1)}, f32[1,512]{1,0:T(1,128)}, u32[]{:S(2)}) copy-start(f32[1,512]{1,0:T(1,128)} %get-tuple-element.63) | copy-start | bytes 6148
  239.4 40.6 %copy-start.6 = (bf16[2,512,128]{2,1,0:T(8,128)(2,1)S(1)}, bf16[2,512,128]{2,1,0:T(8,128)(2,1)}, u32[]{:S(2)}) copy-start(bf16[2,512,128]{2,1,0:T(8,128)(2,1)} %copy-done.5) | copy-start | bytes 786436
  239.4 40.6 %copy-start.8 = (bf16[2,512,128]{2,1,0:T(8,128)(2,1)S(1)}, bf16[2,512,128]{2,1,0:T(8,128)(2,1)}, u32[]{:S(2)}) copy-start(bf16[2,512,128]{2,1,0:T(8,128)(2,1)} %copy-done.7) | copy-start | bytes 786436
  284.5 91.2 %copy-start.15 = (f32[1,128,512]{2,1,0:T(8,128)S(1)}, f32[1,128,512]{2,1,0:T(8,128)}, u32[]{:S(2)}) copy-start(f32[1,128,512]{2,1,0:T(8,128)} %get-tuple-element.68) | copy-start | bytes 786436
  372.5 7.5 %copy-start.13 = (bf16[1,2,4,128,512]{4,3,2,1,0:T(8,128)(2,1)S(1)}, bf16[1,2,4,128,512]{4,3,2,1,0:T(8,128)(2,1)}, u32[]{:S(2)}) copy-start(bf16[1,2,4,128,512]{4,3,2,1,0:T(8,128)(2,1)} %get-tuple-element.64) | copy-start | bytes 3145732
  377.1 3.9 %copy-start.10 = (f32[6,128,512]{2,1,0:T(8,128)S(1)}, f32[6,128,512]{2,1,0:T(8,128)}, u32[]{:S(2)}) copy-start(f32[6,128,512]{2,1,0:T(8,128)} %get-tuple-element.196) | copy-start | bytes 4718596

commit v4 on v3

--- a/solution.py
+++ b/solution.py
@@ -404,43 +404,28 @@
     )(inputs, ids)
 
 
-def exchange(name, cid, seq_count, parts, others, reduce_hops, gather_hops, finish, extra, grads=None):
+def exchange(name, cid, seq_count, parts, others, reduce_hops, gather_hops, finish, extra):
     per_part = parts[0].shape[1]
     rows, width = parts[0].shape[4:]
     streams = per_part * len(parts)
     hops = max(reduce_hops, gather_hops)
-    given = [] if grads is None else [grads]
-    chunks = 0 if grads is None else grads.shape[0]
-    sums, tools = [], []
-    if chunks:
-        depth, wide = grads.shape[1:]
-        sums = [jax.ShapeDtypeStruct((chunks, depth // seq_count, wide), F32)]
-        tools = [pltpu.VMEM((depth // seq_count, wide // 2), F32)] + GradReduce.scratch(seq_count, chunks, depth, wide)
 
     def kernel(*refs):
         refs = list(refs)
         part_refs = [refs.pop(0) for _ in parts]
         other_refs = [refs.pop(0) for _ in others]
-        grad_ref = refs.pop(0) if chunks else None
         out = refs.pop(0)
         extra_refs = [refs.pop(0) for _ in extra]
-        sum_ref = refs.pop(0) if chunks else None
-        grad_tools = [refs.pop(0) for _ in tools]
         acc = refs.pop(0)
         gather_sem = refs.pop(0)
         s, t, y, c, core, far = place()
-        greet(seq_count, hops, wide=bool(chunks))
-        if chunks:
-            grad_acc = grad_tools.pop(0)
-            gr = GradReduce(seq_count, lambda c: grad_ref.at[c], lambda c: sum_ref.at[c], grad_tools)
+        greet(seq_count, hops)
         rs = ReduceScatter(
             seq_count, reduce_hops, streams, lambda h, m: part_refs[m // per_part].at[h, m % per_part], refs
         )
         ag = AllGather(seq_count, gather_hops, streams, out, gather_sem)
         for h, m in rs.order():
             rs.start(h, m)
-        for k in range(chunks):
-            gr.start(k)
         for h in range(1, gather_hops + 1):
             for m in range(streams):
                 ag.clear(h, m)
@@ -449,14 +434,10 @@
         for h, m in rs.order():
             if h:
                 rs.hop(h, m)
-        for k in range(chunks):
-            gr.spread(k)
         for m in range(streams):
             rs.total(m, acc)
             out[0, m, t] = finish(m, acc[...], other_refs, extra_refs)
             ag.start(m)
-        for k in range(chunks):
-            gr.collect(k, grad_acc)
         for m in range(streams):
             ag.pass_on(0, m)
             for h in range(1, gather_hops + 1):
@@ -467,24 +448,20 @@
         for h in range(gather_hops + 1):
             for m in range(streams):
                 ag.finish(h, m)
-        for k in range(chunks):
-            gr.finish(k)
-            gr.drain(k)
         rs.drain()
         ag.drain()
 
     return pl.pallas_call(
         kernel,
         name=name,
-        out_shape=(jax.ShapeDtypeStruct((gather_hops + 1, streams, 4, rows, width), BF),) + tuple(extra) + tuple(sums),
-        in_specs=in_vmem(len(parts) + len(others) + len(given)),
-        out_specs=tuple(in_vmem(1 + len(extra) + len(sums))),
-        scratch_shapes=tools
-        + [pltpu.VMEM((rows, width), F32)]
+        out_shape=(jax.ShapeDtypeStruct((gather_hops + 1, streams, 4, rows, width), BF),) + tuple(extra),
+        in_specs=in_vmem(len(parts) + len(others)),
+        out_specs=tuple(in_vmem(1 + len(extra))),
+        scratch_shapes=[pltpu.VMEM((rows, width), F32)]
         + AllGather.scratch(gather_hops, streams)
         + ReduceScatter.scratch(reduce_hops, streams, rows, width),
         compiler_params=params(cid),
-    )(*parts, *others, *given)
+    )(*parts, *others)
 
 
 def norm_of(values, gain_row):
@@ -773,6 +750,340 @@
         ],
         compiler_params=params(),
     )(q, k, v, lse, grad_out, row_ids, col_ids, wq, wk, wv, wo)
+
+
+def unit_terms(gate_pre, up_pre, grad_inner):
+    root = 0.7978845608028654
+    square = gate_pre * gate_pre
+    bend = jnp.tanh(root * (gate_pre + 0.044715 * (gate_pre * square)))
+    half = 0.5 * (1.0 + bend)
+    gelu = gate_pre * half
+    slope = half + 0.5 * gate_pre * (1.0 - bend * bend) * (root * (1.0 + 3.0 * 0.044715 * square))
+    return gelu * up_pre, grad_inner * up_pre * slope, grad_inner * gelu
+
+
+def middle(part, x, attn_gain, feed_gain, row_ids, col_ids, wq, wk, wv, wo, wg, wu, wd, cot, seq_count):
+    spans, streams, _, length = row_ids.shape
+    quarter, width = part.shape[4:]
+    hops = spans - 1
+    cols, units = wq.shape[1], wg.shape[1]
+    heads = cols // HD
+    tile = 2 * quarter
+    steps = 2 * streams
+    scale = HD ** (-0.5)
+    rows = width // seq_count
+    chunks = 4
+    assert streams == 2 and units == 4 * cols
+
+    def kernel(
+        part_ref, x_ref, ag_ref, fg_ref, row_ref, col_ref, wq_ref, wk_ref, wv_ref, wo_ref, wg_ref, wu_ref, wd_ref, cot_ref,
+        stu_out, layer_out, one_out, gain_out, sum_out,
+        attn_in, feed_in, grad_att, q_ref, k_ref, v_ref, a_ref, lse_ref, hid_one, hid_two, grad_two,
+        inner_ref, gg_ref, gu_ref, ga_ref, dk_acc, dv_acc, dq_ref, dkv_ref, grads, total, grad_acc,
+        o_part, feed_part, layer_part, attn_part,
+        sem_one, sem_two, sem_three, sem_layer, sem_five, *scratch,
+    ):
+        s, t, y, c, core, far = place()
+        scratch = list(scratch)
+
+        def take(count):
+            taken = scratch[:count]
+            del scratch[:count]
+            return taken
+
+        def reducer(ref, distance):
+            return ReduceScatter(seq_count, distance, streams, lambda h, m: ref.at[h, m], take(6))
+
+        rs_one, rs_two, rs_three, rs_layer = [reducer(r, 0) for r in (part_ref, o_part, feed_part, layer_part)]
+        rs_four = reducer(attn_part, hops)
+        gr = GradReduce(seq_count, lambda k: grads.at[k], lambda k: sum_out.at[k], take(8))
+        ag_one = AllGather(seq_count, hops, streams, attn_in, sem_one)
+        ag_two = AllGather(seq_count, 0, streams, feed_in, sem_two)
+        ag_three = AllGather(seq_count, 0, streams, grad_att, sem_three)
+        ag_layer = AllGather(seq_count, 0, streams, layer_out, sem_layer)
+        ag_five = AllGather(seq_count, 0, streams, stu_out, sem_five)
+        distances = range(1, hops + 1)
+
+        def flat(value):
+            return value.reshape(-1, value.shape[-1])
+
+        def all_rows(ref, m):
+            return flat(ref[0, m])
+
+        greet(seq_count, 0, wide=True)
+        for m in range(streams):
+            rs_one.start(0, m)
+        for h in distances:
+            for m in range(streams):
+                ag_one.clear(h, m)
+        for m in range(streams):
+            rs_one.middle(0, m)
+        for m in range(streams):
+            rs_one.total(m, total)
+            hidden = x_ref[m, t].astype(F32) + total[...]
+            hid_one[m] = hidden
+            attn_in[0, m, t] = norm_of(hidden, ag_ref[...]).astype(BF)
+            ag_one.start(m)
+        ag_one.pass_on(0, 0)
+        for h in distances:
+            ag_one.arrive(h, 0)
+        ag_one.pass_on(0, 1)
+        for h in distances:
+            ag_one.pass_on(h, 0)
+        for h in distances:
+            ag_one.arrive(h, 1)
+        for h in range(spans):
+            ag_one.finish(h, 0)
+
+        def split_step(i):
+            m = i // 2
+            return m, i - 2 * m
+
+        def after(i, step, *actions):
+            @pl.when(i == step)
+            def _():
+                for action in actions:
+                    action()
+
+        def masks_of(m, here, first):
+            return [allowed_keys(col_ref[m, here], row_ref[h, m], first, h * length) for h in range(spans)]
+
+        @pl.loop(0, steps)
+        def _(i):
+            m, half = split_step(i)
+            first = pl.multiple_of(half * tile, tile)
+            here = pl.ds(first, tile)
+
+            @pl.when(half == 0)
+            def _():
+                own = flat(attn_in[0, m])
+                q_ref[m] = dot_nn(own, wq_ref[...]).astype(BF)
+                for h in range(spans):
+                    block = flat(attn_in[h, m])
+                    k_ref[h, m] = dot_nn(block, wk_ref[...]).astype(BF)
+                    v_ref[h, m] = dot_nn(block, wv_ref[...]).astype(BF)
+
+            masks = masks_of(m, here, first)
+            block = q_ref[m, here]
+            result = jnp.zeros((tile, cols), F32)
+            for head in range(heads):
+                query = one_head(block, head)
+                scores = [jnp.where(masks[h], dot_nt(query, k_ref[h, m]) * scale, NEGATIVE) for h in range(spans)]
+                peak = functools.reduce(jnp.maximum, [jnp.max(v, axis=-1, keepdims=True) for v in scores])
+                raised = [jnp.exp(v - peak) for v in scores]
+                norm = sum([jnp.sum(v, axis=-1, keepdims=True) for v in raised])
+                inverse = 1.0 / norm
+                mixed = sum([dot_nn((raised[h] * inverse).astype(BF), v_ref[h, m]) for h in range(spans)])
+                result = result + one_head(mixed, head)
+                lse_ref[m, head, here] = jnp.broadcast_to(peak + jnp.log(norm), (tile, LANES))
+            low = result.astype(BF)
+            a_ref[m, here] = low
+            o_part[0, m, half] = dot_nn(low, wo_ref[...]).astype(BF).reshape(2, quarter, width)
+            after(i, 0, *[functools.partial(ag_one.pass_on, h, 1) for h in distances])
+            after(i, 1, lambda: rs_two.start(0, 0), *[functools.partial(ag_one.finish, h, 1) for h in range(spans)])
+            after(i, 2, lambda: rs_two.middle(0, 0))
+            after(i, 3, lambda: rs_two.start(0, 1))
+
+        def second_norm(m):
+            rs_two.total(m, total)
+            hidden = hid_one[m] + total[...]
+            hid_two[m] = hidden
+            feed_in[0, m, t] = norm_of(hidden, fg_ref[...]).astype(BF)
+            ag_two.start(m)
+
+        second_norm(0)
+        rs_two.middle(0, 1)
+        ag_two.pass_on(0, 0)
+        second_norm(1)
+        ag_two.finish(0, 0)
+
+        @pl.loop(0, steps)
+        def _(i):
+            m, half = split_step(i)
+            here = pl.ds(pl.multiple_of(half * tile, tile), tile)
+            block = flat(feed_in[0, m, pl.ds(2 * half, 2)])
+            inner, grad_gate, grad_up = unit_terms(
+                dot_nn(block, wg_ref[...]), dot_nn(block, wu_ref[...]), dot_nt(cot_ref[m, here], wd_ref[...])
+            )
+            inner, grad_gate, grad_up = inner.astype(BF), grad_gate.astype(BF), grad_up.astype(BF)
+            inner_ref[m, here] = inner
+            gg_ref[m, here] = grad_gate
+            gu_ref[m, here] = grad_up
+            back = dot_nt(grad_gate, wg_ref[...]) + dot_nt(grad_up, wu_ref[...])
+            feed_part[0, m, half] = back.astype(BF).reshape(2, quarter, width)
+            layer_part[0, m, half] = dot_nn(inner, wd_ref[...]).astype(BF).reshape(2, quarter, width)
+            after(i, 0, lambda: ag_two.pass_on(0, 1))
+            after(i, 1, lambda: rs_three.start(0, 0), lambda: ag_two.finish(0, 1))
+            after(i, 2, lambda: rs_three.middle(0, 0))
+            after(i, 3, lambda: rs_three.start(0, 1))
+
+        def third_norm(m):
+            rs_three.total(m, total)
+            grad_in, gain_grad = norm_back(hid_two[m], fg_ref[...], total[...])
+            value = cot_ref[m, pl.ds(pl.multiple_of(t * quarter, quarter), quarter)].astype(F32) + grad_in
+            grad_two[m] = value
+            gain_out[1:2] = gain_grad if m == 0 else gain_out[1:2] + gain_grad
+            grad_att[0, m, t] = value.astype(BF)
+            ag_three.start(m)
+
+        third_norm(0)
+        feed_all = flat(feed_in[0])
+        grads[0] = dot_tn(feed_all, flat(gg_ref[...])).astype(BF)
+        gr.start(0)
+        rs_three.middle(0, 1)
+        ag_three.pass_on(0, 0)
+        grads[1] = dot_tn(feed_all, flat(gu_ref[...])).astype(BF)
+        gr.start(1)
+        third_norm(1)
+        ag_three.finish(0, 0)
+        grads[2] = dot_tn(flat(cot_ref[...]), flat(inner_ref[...])).astype(BF)
+        gr.start(2)
+        for m in range(streams):
+            rs_layer.start(0, m)
+
+        def layer_sum(m):
+            rs_layer.total(m, total)
+            layer_out[0, m, t] = (hid_two[m] + total[...]).astype(BF)
+            ag_layer.start(m)
+
+        @pl.loop(0, steps)
+        def _(i):
+            m, half = split_step(i)
+            first = pl.multiple_of(half * tile, tile)
+            here = pl.ds(first, tile)
+
+            @pl.when(half == 0)
+            def _():
+                ga_ref[...] = dot_nt(all_rows(grad_att, m), wo_ref[...]).astype(BF)
+                dk_acc[...] = jnp.zeros_like(dk_acc)
+                dv_acc[...] = jnp.zeros_like(dv_acc)
+
+            masks = masks_of(m, here, first)
+            block = q_ref[m, here]
+            grad_block = ga_ref[here]
+            result = jnp.zeros((tile, cols), F32)
+            for head in range(heads):
+                query = one_head(block, head)
+                grad = one_head(grad_block, head)
+                level = lse_ref[m, head, here][:, :1]
+                prob = [
+                    jnp.where(masks[h], jnp.exp(dot_nt(query, k_ref[h, m]) * scale - level), 0.0) for h in range(spans)
+                ]
+                grad_prob = [dot_nt(grad, v_ref[h, m]) for h in range(spans)]
+                mean = sum([jnp.sum(p * g, axis=-1, keepdims=True) for p, g in zip(prob, grad_prob)])
+                grad_scores = [(p * (g - mean)).astype(BF) for p, g in zip(prob, grad_prob)]
+                for h in range(spans):
+                    dv_acc[h] += dot_tn(prob[h].astype(BF), grad)
+                    dk_acc[h] += dot_tn(grad_scores[h], query)
+                mixed = sum([dot_nn(grad_scores[h], k_ref[h, m]) for h in range(spans)])
+                result = result + one_head(mixed, head)
+            dq_ref[m, here] = (result * scale).astype(BF)
+
+            @pl.when(half == 1)
+            def _():
+                for h in range(hops, -1, -1):
+                    grad_k = (dk_acc[h] * scale).astype(BF)
+                    grad_v = dv_acc[h].astype(BF)
+                    dkv_ref[h, m, :, :cols] = grad_k
+                    dkv_ref[h, m, :, cols:] = grad_v
+                    back = dot_nt(grad_k, wk_ref[...]) + dot_nt(grad_v, wv_ref[...])
+                    if h == 0:
+                        back = back + dot_nt(dq_ref[m], wq_ref[...])
+                    attn_part[h, m] = back.astype(BF).reshape(2, 2, quarter, width)
+                    rs_four.start(h, m)
+
+            after(i, 0, lambda: ag_three.pass_on(0, 1), lambda: rs_layer.middle(0, 0), lambda: rs_layer.middle(0, 1))
+            after(i, 1, lambda: ag_three.finish(0, 1), lambda: gr.spread(0), lambda: layer_sum(0), lambda: layer_sum(1))
+            after(i, 2, *[functools.partial(rs_four.middle, h, 0) for h in range(hops, -1, -1)], lambda: gr.spread(1))
+            after(i, 3, *[functools.partial(rs_four.hop, h, 0) for h in range(hops, 0, -1)], lambda: gr.spread(2))
+
+        attn_all = attn_in[...].reshape(spans * streams * length, width)
+        grads[3, :, cols : 3 * cols] = dot_tn(attn_all, flat(dkv_ref[...].reshape(-1, 2 * cols))).astype(BF)
+        for h in range(hops, -1, -1):
+            rs_four.middle(h, 1)
+        grads[3, :, :cols] = dot_tn(flat(attn_in[0]), flat(dq_ref[...])).astype(BF)
+        grads[3, :, 3 * cols :] = dot_tn(flat(grad_att[0]), flat(a_ref[...])).astype(BF)
+        gr.start(3)
+        for h in range(hops, 0, -1):
+            rs_four.hop(h, 1)
+        for m in range(streams):
+            rs_four.total(m, total)
+            grad_in, gain_grad = norm_back(hid_one[m], ag_ref[...], total[...])
+            value = grad_two[m] + grad_in
+            one_out[m] = value
+            gain_out[0:1] = gain_grad if m == 0 else gain_out[0:1] + gain_grad
+            stu_out[0, m, t] = value.astype(BF)
+            ag_five.start(m)
+            gr.collect(m, grad_acc)
+            ag_layer.pass_on(0, m)
+        gr.spread(3)
+        for m in range(streams):
+            ag_five.pass_on(0, m)
+        gr.collect(2, grad_acc)
+        for m in range(streams):
+            ag_layer.finish(0, m)
+        gr.collect(3, grad_acc)
+        for m in range(streams):
+            ag_five.finish(0, m)
+        for k in range(chunks):
+            gr.finish(k)
+            gr.drain(k)
+        for item in (rs_one, rs_two, rs_three, rs_layer, rs_four, ag_one, ag_two, ag_three, ag_layer, ag_five):
+            item.drain()
+
+    rows_of = pltpu.VMEM((streams, length, cols), BF)
+    unit_rows = pltpu.VMEM((streams, length, units), BF)
+    state = pltpu.VMEM((streams, quarter, width), F32)
+    gathered = (1, streams, 4, quarter, width)
+    split_part = pltpu.VMEM((1, streams, 2, 2, quarter, width), BF)
+    zero_hops = ReduceScatter.scratch(0, streams, quarter, width)
+    return pl.pallas_call(
+        kernel,
+        name="middle",
+        out_shape=(
+            jax.ShapeDtypeStruct(gathered, BF),
+            jax.ShapeDtypeStruct(gathered, BF),
+            jax.ShapeDtypeStruct((streams, quarter, width), F32),
+            jax.ShapeDtypeStruct((2, width), F32),
+            jax.ShapeDtypeStruct((chunks, rows, units), F32),
+        ),
+        in_specs=in_vmem(14),
+        out_specs=tuple(in_vmem(5)),
+        scratch_shapes=[
+            pltpu.VMEM((spans, streams, 4, quarter, width), BF),
+            pltpu.VMEM(gathered, BF),
+            pltpu.VMEM(gathered, BF),
+            rows_of,
+            pltpu.VMEM((spans, streams, length, cols), BF),
+            pltpu.VMEM((spans, streams, length, cols), BF),
+            rows_of,
+            pltpu.VMEM((streams, heads, length, LANES), F32),
+            state,
+            state,
+            state,
+            unit_rows,
+            unit_rows,
+            unit_rows,
+            pltpu.VMEM((length, cols), BF),
+            pltpu.VMEM((spans, length, cols), F32),
+            pltpu.VMEM((spans, length, cols), F32),
+            rows_of,
+            pltpu.VMEM((spans, streams, length, 2 * cols), BF),
+            pltpu.VMEM((chunks, width, units), BF),
+            pltpu.VMEM((quarter, width), F32),
+            pltpu.VMEM((rows, units // 2), F32),
+            split_part,
+            split_part,
+            split_part,
+            pltpu.VMEM((spans, streams, 2, 2, quarter, width), BF),
+            AllGather.scratch(hops, streams)[0],
+        ]
+        + [AllGather.scratch(0, streams)[0]] * 4
+        + zero_hops * 4
+        + ReduceScatter.scratch(hops, streams, quarter, width)
+        + GradReduce.scratch(seq_count, chunks, width, units),
+        compiler_params=params(8),
+    )(part, x, attn_gain, feed_gain, row_ids, col_ids, wq, wk, wv, wo, wg, wu, wd, cot)
 
 
 def tail(
@@ -1069,6 +1380,43 @@
     mixed = jnp.einsum("kmtd,kde->mte", conv, filter_proj, preferred_element_type=F32)
     mixed = mixed + jnp.einsum("imtc,ice->mte", lag_stack, lag_proj, preferred_element_type=F32)
 
+    tokens_flat = streams * length
+    cols = query_weight.shape[1]
+
+    def answer(layer_output, input_gradient, gains, filter_grad, lag_grad, attn_grads, feed_grads):
+        query_grad, key_grad, value_grad, output_grad = jnp.split(attn_grads, [cols, 2 * cols, 3 * cols], axis=1)
+        gate_grad, up_grad, down_grad = feed_grads
+        return (
+            layer_output[:, None],
+            input_gradient[:, None],
+            gains[0],
+            filter_grad,
+            lag_grad[:, : lag_order * channels].T.reshape(lag_order, channels, -1),
+            gains[1],
+            query_grad,
+            key_grad,
+            value_grad,
+            output_grad.T,
+            gains[2],
+            gate_grad,
+            up_grad,
+            down_grad.T,
+        )
+
+    if width // seq_count % LANES == 0:
+        grad_stu, layer_output, grad_one, gain_grads, sums = middle(
+            split(mixed.astype(BF))[None], quarters(x), row(attention_gain), row(feed_gain), id_rows[: hops + 1], id_cols[0],
+            query_weight, key_weight, value_weight, output_weight, gate_weight, up_weight, down_weight, grad_three, seq_count,
+        )
+        input_gradient, filter_grad, lag_grad, gains = tail(
+            grad_stu.reshape(tokens_flat, width), filter_proj, lag_proj, conv.reshape(count, tokens_flat, width),
+            lag_stack.reshape(lag_order, tokens_flat, channels), jnp.stack(masks).astype(F32), id_rows[0],
+            id_ext.reshape(seq_count * streams, length), base_back, quarters(x), row(stu_gain), grad_one, gain_grads, seq_count,
+        )
+        return answer(
+            whole(layer_output)[0], whole(input_gradient)[0], gains, filter_grad, lag_grad, sums[3], (sums[0], sums[1], sums[2])
+        )
+
     state = jax.ShapeDtypeStruct((streams, quarter, width), F32)
     gain_state = jax.ShapeDtypeStruct((1, width), F32)
 
@@ -1121,7 +1469,6 @@
         extra[1][...] = gain_grad if m == 0 else extra[1][...] + gain_grad
         return grad_two.astype(BF)
 
-    fused = width // seq_count % LANES == 0
     feed_grads = jnp.stack(
         [
             dot_tn(feed_in, grad_gate).astype(BF),
@@ -1130,14 +1477,10 @@
         ]
     )
     shape = (1, streams, length, width)
-    results = exchange(
+    both, grad_two, feed_gain_grad = exchange(
         "exchange_three", 4, seq_count, [split(feed_part.reshape(shape)), split(layer_part.reshape(shape))],
         [hidden_two, row(feed_gain), quarters(grad_three)], 0, 0, finish_three, [state, gain_state],
-        feed_grads if fused else None,
     )
-    both, grad_two, feed_gain_grad = results[:3]
-    if fused:
-        feed_grads = results[3]
     both = whole(both)[0]
     grad_att_out = both[:streams]
     layer_output = both[streams:]
@@ -1146,7 +1489,6 @@
         q, k, v, lse, grad_att_out, id_rows[: hops + 1], id_cols[0], query_weight, key_weight, value_weight, output_weight
     )
 
-    tokens_flat = streams * length
     go = grad_att_out.reshape(tokens_flat, width)
     attn_grads = jnp.concatenate(
         [
@@ -1166,82 +1508,50 @@
         extra[1][...] = gain_grad if m == 0 else extra[1][...] + gain_grad
         return grad_one.astype(BF)
 
-    results = exchange(
+    grad_stu, grad_one, attn_gain_grad = exchange(
         "exchange_four", 5, seq_count, [split(attn_part)], [hidden_one, row(attention_gain), grad_two], hops, 0,
-        finish_four, [state, gain_state], attn_grads[None] if fused else None,
+        finish_four, [state, gain_state],
     )
-    grad_stu, grad_one, attn_gain_grad = results[:3]
     grad_stu = whole(grad_stu)[0]
-    lag_masks = jnp.stack(masks).astype(F32)
-    if fused:
-        attn_grads = results[3][0]
-        input_gradient, filter_grad, lag_grad, gains = tail(
-            grad_stu.reshape(tokens_flat, width), filter_proj, lag_proj, conv.reshape(count, tokens_flat, width),
-            lag_stack.reshape(lag_order, tokens_flat, channels), lag_masks, id_rows[0],
-            id_ext.reshape(seq_count * streams, length), base_back,
-            quarters(x), row(stu_gain), grad_one, jnp.concatenate([attn_gain_grad, feed_gain_grad], axis=0), seq_count,
-        )
-        input_gradient = whole(input_gradient)[0]
-    else:
-        grad_conv = jnp.einsum("mte,kde->kmtd", grad_stu, filter_proj, preferred_element_type=F32).astype(BF)
-        grad_lagged = jnp.einsum("mte,ice->imtc", grad_stu, lag_proj, preferred_element_type=F32)
-        ext_grad = jnp.zeros((streams, 8 + length, channels), F32)
-        for step in range(1, lag_order + 1):
-            term = jnp.where(masks[step - 1], grad_lagged[step - 1], 0.0)
-            ext_grad = ext_grad + jnp.pad(term, ((0, 0), (8 - step, step), (0, 0)))
-        terms = convolve_back(
-            grad_conv, id_rows[0], id_cols, base_back, ext_grad[:, 8:], ext_grad[:, :8], seq_count
-        )
-
-        def finish_five(m, total, others, extra):
-            x_ref, gain_ref, grad_ref = others
-            grad_in, gain_grad = norm_back(x_ref[m, place()[1]].astype(F32), gain_ref[...], total)
-            extra[0][...] = gain_grad if m == 0 else extra[0][...] + gain_grad
-            return (grad_ref[m] + grad_in).astype(BF)
-
-        input_gradient, stu_gain_grad = exchange(
-            "exchange_five", 6, seq_count, [split(terms)], [quarters(x), row(stu_gain), grad_one], seq_count - 1, 0,
-            finish_five, [gain_state],
-        )
-        input_gradient = whole(input_gradient)[0]
-        stu = grad_stu.reshape(tokens_flat, width)
-        filter_part = jnp.einsum("kmtd,mte->kde", conv, grad_stu, preferred_element_type=F32).astype(BF)
-        lag_part = jnp.concatenate(
-            [dot_tn(stu, lag_stack[i].reshape(tokens_flat, channels)).astype(BF) for i in range(lag_order)], axis=1
-        )
-        feed_grads = lax.psum(
-            lax.psum_scatter(feed_grads, "seq", scatter_dimension=1, tiled=True), "dp"
-        ).astype(F32)
-        attn_grads = lax.psum(lax.psum_scatter(attn_grads, "seq", scatter_dimension=0, tiled=True), "dp").astype(F32)
-        filter_grad = lax.psum(
-            lax.psum_scatter(filter_part, "seq", scatter_dimension=1, tiled=True), "dp"
-        ).astype(F32)
-        lag_grad = lax.psum(lax.psum_scatter(lag_part, "seq", scatter_dimension=0, tiled=True), "dp").astype(F32)
-        gains = jnp.concatenate([stu_gain_grad, attn_gain_grad, feed_gain_grad], axis=0)
-        gains = lax.psum(gains, ("dp", "seq", "tensor"))
-        gain_width = width // seq_count
-        gains = lax.dynamic_slice_in_dim(gains, lax.axis_index("seq") * gain_width, gain_width, 1)
-
-    cols = query_weight.shape[1]
-    gate_grad, up_grad, down_grad = feed_grads
-    query_grad, key_grad, value_grad, output_grad = jnp.split(attn_grads, [cols, 2 * cols, 3 * cols], axis=1)
-    lag_grad = lag_grad[:, : lag_order * channels].T.reshape(lag_order, channels, -1)
-    return (
-        layer_output[:, None],
-        input_gradient[:, None],
-        gains[0],
-        filter_grad,
-        lag_grad,
-        gains[1],
-        query_grad,
-        key_grad,
-        value_grad,
-        output_grad.T,
-        gains[2],
-        gate_grad,
-        up_grad,
-        down_grad.T,
+    grad_conv = jnp.einsum("mte,kde->kmtd", grad_stu, filter_proj, preferred_element_type=F32).astype(BF)
+    grad_lagged = jnp.einsum("mte,ice->imtc", grad_stu, lag_proj, preferred_element_type=F32)
+    ext_grad = jnp.zeros((streams, 8 + length, channels), F32)
+    for step in range(1, lag_order + 1):
+        term = jnp.where(masks[step - 1], grad_lagged[step - 1], 0.0)
+        ext_grad = ext_grad + jnp.pad(term, ((0, 0), (8 - step, step), (0, 0)))
+    terms = convolve_back(
+        grad_conv, id_rows[0], id_cols, base_back, ext_grad[:, 8:], ext_grad[:, :8], seq_count
     )
+
+    def finish_five(m, total, others, extra):
+        x_ref, gain_ref, grad_ref = others
+        grad_in, gain_grad = norm_back(x_ref[m, place()[1]].astype(F32), gain_ref[...], total)
+        extra[0][...] = gain_grad if m == 0 else extra[0][...] + gain_grad
+        return (grad_ref[m] + grad_in).astype(BF)
+
+    input_gradient, stu_gain_grad = exchange(
+        "exchange_five", 6, seq_count, [split(terms)], [quarters(x), row(stu_gain), grad_one], seq_count - 1, 0,
+        finish_five, [gain_state],
+    )
+    input_gradient = whole(input_gradient)[0]
+    stu = grad_stu.reshape(tokens_flat, width)
+    filter_part = jnp.einsum("kmtd,mte->kde", conv, grad_stu, preferred_element_type=F32).astype(BF)
+    lag_part = jnp.concatenate(
+        [dot_tn(stu, lag_stack[i].reshape(tokens_flat, channels)).astype(BF) for i in range(lag_order)], axis=1
+    )
+    feed_grads = lax.psum(
+        lax.psum_scatter(feed_grads, "seq", scatter_dimension=1, tiled=True), "dp"
+    ).astype(F32)
+    attn_grads = lax.psum(lax.psum_scatter(attn_grads, "seq", scatter_dimension=0, tiled=True), "dp").astype(F32)
+    filter_grad = lax.psum(
+        lax.psum_scatter(filter_part, "seq", scatter_dimension=1, tiled=True), "dp"
+    ).astype(F32)
+    lag_grad = lax.psum(lax.psum_scatter(lag_part, "seq", scatter_dimension=0, tiled=True), "dp").astype(F32)
+    gains = jnp.concatenate([stu_gain_grad, attn_gain_grad, feed_gain_grad], axis=0)
+    gains = lax.psum(gains, ("dp", "seq", "tensor"))
+    gain_width = width // seq_count
+    gains = lax.dynamic_slice_in_dim(gains, lax.axis_index("seq") * gain_width, gain_width, 1)
+    return answer(layer_output, input_gradient, gains, filter_grad, lag_grad, attn_grads, feed_grads)
 
 
 def solution(mesh):

time: 383 us -> 319 us (0.83)
  Pallas kernels: 323 us -> 284 us
  matrix products: 23.9 us -> 9.56 us
  local copies, waits for them, and re-layouts: 22.7 us -> 16.4 us
    pallas_call x6 -> x1, Pallas kernels: 186 us -> 145 us  [middle(): pl.pallas_call(kernel, name='middle', out_shape=(jax.ShapeDtypeStruct(gat...]
    dot_general x13 -> x0, matrix products: 14.3 us -> none  [the longest x3 5.88 us: dot_nn(): return jnp.dot(a, b, preferred_element_type=F32)]
    unnamed x56 -> x29, local copies, waits for them, and re-layouts: 7.88 us -> 5.95 us
where the time goes in v4:
time: 319 us
  Pallas kernels  284 us (89%)
  local copies, waits for them, and re-layouts  16.4 us (5%)
  matrix products  9.56 us (3%)
  other arithmetic  8.34 us (3%)
    pallas_call x1, Pallas kernels, middle(): pl.pallas_call(kernel, name='middle', out_shape=(jax.ShapeDtypeStruct(gat...  145 us
    pallas_call x1, Pallas kernels, tail(): pl.pallas_call(kernel, name='tail', out_shape=(jax.ShapeDtypeStruct((1, s...  89.6 us
    pallas_call x1, Pallas kernels, gather_rows(): pl.pallas_call(kernel, name='gather_rows', out_shape=(jax.ShapeDtypeStruc...  26.2 us
    pallas_call x1, Pallas kernels, convolve(): pl.pallas_call(whole_kernel if at_once else kernel, name='convolve', out_...  22.7 us
    dot_general x1, matrix products, local(): jnp.einsum('kmtd,kde->mte', conv, filter_proj, preferred_element_type=F32)  7.53 us

profile of v4, /device:TPU:0, one launch (start us, length us, event | category | flops | bytes accessed | tf_op | source)
XLA Modules:
  0.0 318.8 jit_solution(9890908932123523667)
XLA Ops:
  0.6 1.5 multiply_reduce_fusion
  2.2 2.5 multiply_convert_fusion.x_ref
  4.7 26.2 %gather_rows.1 = (bf16[4,2,4,128,512]{4,3,2,1,0:T(8,128)(2,1)}, s32[4,8,128]{2,1,0:T(8,128)}) custom-call(bf16[2,4,128,512]{3,2,1,0:T(8,128)(2,1)} %multiply_convert_fusion.x_ref, s32[8,128]{1,0:T(8,128)} %bitcast.110), custom_call_target="tpu_custom_call" | custom-call | tf_op jit(solution)/shard_map/gather_rows/pallas_call | solution.py:393
  30.9 0.0 copy-start.6
  30.9 0.0 copy-start.10
  30.9 1.8 slice.95
  32.7 0.0 copy-start.2
  32.8 0.1 dynamic-slice_bitcast_fusion.1
  32.9 0.0 copy-done.6
  32.9 0.0 copy-start.9
  32.9 0.1 slice.117
  33.0 0.0 copy-done.10
  33.0 0.1 fusion.20
  33.1 0.6 fusion.15
  33.7 1.0 pad_maximum_fusion.lag_ref
  34.7 0.0 copy-done.2
  34.7 2.0 fusion.5
  36.7 0.0 copy-done.9
  36.7 1.1 squeeze.61.col_ref
  37.8 0.0 copy-done.8
  37.8 1.3 reverse
  39.1 0.1 slice_bitcast_fusion.9
  39.2 0.1 slice.91
  39.3 0.1 rev.9
  39.4 0.2 concatenate.43
  39.6 0.7 convert_element_type.40.base_ref
  40.3 22.7 %convolve.1 = bf16[6,2,512,512]{3,2,1,0:T(8,128)(2,1)} custom-call(bf16[4,2,512,512]{3,2,1,0:T(8,128)(2,1)} %bitcast.89, s32[4,2,1,512]{3,2,1,0:T(1,128)} %bitcast.103, s32[2,512,1]{2,1,0:T(8,128)} %squeeze.61.col_ref, f32[6,1,2560]{2,1,0:T(1,128)} %convert_element_type.40.base_ref), custom_call_target="tpu_custom_call" | custom-call | tf_op jit(solution)/shard_map/convolve/pallas_call | solution.py:536
  63.0 7.5 %fusion.2 = bf16[2,512,512]{2,1,0:T(8,128)(2,1)} fusion(f32[2,512,512,1]{2,1,3,0:T(8,128)} %fusion.5, bf16[6,2,512,512]{3,2,1,0:T(8,128)(2,1)} %convolve.1, bf16[6,512,512]{2,1,0:T(8,128)(2,1)S(1)} %copy-done), kind=kOutput, calls=%fused_computation.3 | convolution fusion | flops 3222274048 | bytes 12582912 | tf_op jit(solution)/shard_map/kmtd,kde->mte/dot_general | solution.py:1380
  70.5 0.6 slice.105
  71.1 145.1 %middle.1 = (bf16[1,2,4,128,512]{4,3,2,1,0:T(8,128)(2,1)}, bf16[1,2,4,128,512]{4,3,2,1,0:T(8,128)(2,1)}, f32[2,128,512]{2,1,0:T(8,128)}, f32[2,512]{1,0:T(2,128)}, f32[4,128,512]{2,1,0:T(8,128)}) custom-call(bf16[1,2,2,2,128,512]{5,4,3,2,1,0:T(8,128)(2,1)} %bitcast.101, bf16[2,4,128,512]{3,2,1,0:T(8,128)(2,1)} %bitcast.87, f32[1,512]{1,0:T(1,128)} %bitcast.114, ...), custom_call_target="tpu_custom_call" | custom-call | tf_op jit(solution)/shard_map/middle/pallas_call | solution.py:1040
  216.2 0.3 copy.106
  216.5 0.3 copy.107
  216.8 0.3 copy.108
  217.1 1.3 add_convert_fusion.mask_ref
  218.4 0.6 reshape_reshape.3.ext_ref
  219.1 0.7 maximum_convert_fusion.base_ref
  219.8 89.6 %tail.1 = (bf16[1,2,4,128,512]{4,3,2,1,0:T(8,128)(2,1)}, f32[6,128,512]{2,1,0:T(8,128)}, f32[128,512]{1,0:T(8,128)}, f32[8,128]{1,0:T(8,128)}) custom-call(bf16[1024,512]{1,0:T(8,128)(2,1)} %bitcast.97, bf16[6,512,512]{2,1,0:T(8,128)(2,1)} %fp_ref.1, bf16[3,128,512]{2,1,0:T(8,128)(2,1)} %lp_ref.1, bf16[6,1024,512]{2,1,0:T(8,128)(2,1)} %bitcast.85, ...), custom_call_target="tpu_custom_call" | custom-call | tf_op jit(solution)/shard_map/tail/pallas_call | solution.py:1260
  309.4 0.0 copy-start.3
  309.4 1.0 slice_bitcast_fusion.4
  310.5 0.8 copy.110
  311.3 1.3 slice_bitcast_fusion.6
  312.6 0.9 slice_bitcast_fusion
  313.5 0.7 slice_bitcast_fusion.5
  314.2 0.7 copy.113
  314.9 0.8 copy.114
  315.7 1.0 copy.123
  316.7 1.0 copy.124
  317.7 1.1 copy.125
  (26 shorter events, 0.2 us)
Async XLA Ops:
  30.9 2.0 copy-start.6
  30.9 2.1 copy-start.10
  32.7 1.9 copy-start.2
  32.9 3.8 %copy-start.9 = (s32[1,8,128]{2,1,0:T(8,128)}, s32[1,8,128]{2,1,0:T(8,128)S(1)}, u32[]{:S(2)}) copy-start(s32[1,8,128]{2,1,0:T(8,128)S(1)} %get-tuple-element.133) | copy-start | bytes 12292
  34.7 3.2 copy-start.8
  40.3 22.7 %copy-start = (bf16[6,512,512]{2,1,0:T(8,128)(2,1)S(1)}, bf16[6,512,512]{2,1,0:T(8,128)(2,1)}, u32[]{:S(2)}) copy-start(bf16[6,512,512]{2,1,0:T(8,128)(2,1)} %fp_ref.1) | copy-start | bytes 9437188
  63.0 7.5 %copy-start.7 = (s32[4,8,128]{2,1,0:T(8,128)S(1)}, s32[4,8,128]{2,1,0:T(8,128)}, u32[]{:S(2)}) copy-start(s32[4,8,128]{2,1,0:T(8,128)} %get-tuple-element.26) | copy-start | bytes 49156
  219.8 92.8 %copy-start.4 = (f32[4,128,512]{2,1,0:T(8,128)S(1)}, f32[4,128,512]{2,1,0:T(8,128)}, u32[]{:S(2)}) copy-start(f32[4,128,512]{2,1,0:T(8,128)} %get-tuple-element.35) | copy-start | bytes 3145732
  309.4 6.3 %copy-start.3 = (bf16[1,2,4,128,512]{4,3,2,1,0:T(8,128)(2,1)S(1)}, bf16[1,2,4,128,512]{4,3,2,1,0:T(8,128)(2,1)}, u32[]{:S(2)}) copy-start(bf16[1,2,4,128,512]{4,3,2,1,0:T(8,128)(2,1)} %get-tuple-element.27) | copy-start | bytes 3145732
  313.5 3.2 %copy-start.5 = (bf16[1,2,4,128,512]{4,3,2,1,0:T(8,128)(2,1)S(1)}, bf16[1,2,4,128,512]{4,3,2,1,0:T(8,128)(2,1)}, u32[]{:S(2)}) copy-start(bf16[1,2,4,128,512]{4,3,2,1,0:T(8,128)(2,1)} %get-tuple-element.31) | copy-start | bytes 3145732
  315.7 1.9 copy-start.1

commit v5 on v3

--- a/solution.py
+++ b/solution.py
@@ -15,7 +15,7 @@
 MESH = pl.DeviceIdType.MESH
 BF = jnp.bfloat16
 F32 = jnp.float32
-VMEM_LIMIT = 60 * 1024 * 1024
+VMEM_LIMIT = 63 * 1024 * 1024
 
 
 def place():
@@ -82,12 +82,13 @@
     @staticmethod
     def scratch(hops, streams, rows, width):
         quarter = (hops + 1, streams, rows, width)
+        over_seq = quarter if hops else (1, 1, 16, LANES)
         return [
             pltpu.VMEM((hops + 1, streams, 2, rows, width), BF),
             pltpu.VMEM(quarter, BF),
             pltpu.VMEM(quarter, BF),
-            pltpu.VMEM(quarter, BF),
-            pltpu.VMEM(quarter, BF),
+            pltpu.VMEM(over_seq, BF),
+            pltpu.VMEM(over_seq, BF),
             pltpu.SemaphoreType.DMA((6, hops + 1, streams)),
         ]
 
@@ -103,8 +104,18 @@
 
     def to_hop(self, h, m, peer):
         return remote(
-            self.hop_out.at[h, m], self.hop_in.at[h, m], self.sem.at[4, h, m], self.sem.at[5, h, m], {"seq": peer}
+            self.hop_out.at[h, m], self.hop_in.at[h - 1, m], self.sem.at[4, h, m], self.sem.at[5, h - 1, m], {"seq": peer}
         )
+
+    def add_hop(self, h, m, acc):
+        s = lax.axis_index("seq")
+
+        @pl.when(s + 1 < self.seq_count)
+        def _():
+            remote(
+                self.hop_out.at[h, m], self.hop_in.at[h, m], self.sem.at[4, h, m], self.sem.at[5, h, m], {"seq": s + 1}
+            ).wait_recv()
+            acc[...] += self.hop_in[h, m].astype(F32)
 
     def there(self, h):
         return True if isinstance(h, int) and h == 0 else lax.axis_index("seq") - h >= 0
@@ -133,22 +144,23 @@
             self.part(h, m)[y, c].astype(F32) + self.near[h, m, y].astype(F32) + self.over[h, m].astype(F32)
         )
 
-    def hop(self, h, m):
+    def hop(self, h, m, acc):
         def act():
-            self.hop_out[h, m] = self.own(h, m).astype(BF)
-            self.to_hop(h, m, lax.axis_index("seq") - h).start()
+            acc[...] = self.own(h, m)
+            if isinstance(h, int):
+                if h < self.hops:
+                    self.add_hop(h, m, acc)
+            else:
+                pl.when(h < self.hops)(lambda: self.add_hop(h, m, acc))
+            self.hop_out[h, m] = acc[...].astype(BF)
+            self.to_hop(h, m, lax.axis_index("seq") - 1).start()
 
         when(self.there(h), act)
 
     def total(self, m, acc):
         acc[...] = self.own(0, m)
-        for h in range(1, self.hops + 1):
-            s = lax.axis_index("seq")
-
-            @pl.when(s + h < self.seq_count)
-            def _():
-                self.to_hop(h, m, s + h).wait_recv()
-                acc[...] += self.hop_in[h, m].astype(F32)
+        if self.hops:
+            self.add_hop(0, m, acc)
 
     def drain(self):
         for h, m in self.order():
@@ -157,14 +169,15 @@
                 self.to_core(h, m).wait_send()
                 self.to_far(h, m).wait_send()
                 if h:
-                    self.to_hop(h, m, lax.axis_index("seq") - h).wait_send()
+                    self.to_hop(h, m, lax.axis_index("seq") - 1).wait_send()
 
             when(self.there(h), act)
 
 
 class AllGather:
-    def __init__(self, seq_count, hops, streams, out, sem, first=0):
-        self.seq_count, self.hops, self.streams, self.out, self.sem, self.first = seq_count, hops, streams, out, sem, first
+    def __init__(self, seq_count, hops, streams, at, sem, first=0):
+        self.seq_count, self.hops, self.streams, self.sem, self.first = seq_count, hops, streams, sem, first
+        self.at = at if callable(at) else lambda h, m, quarter: at.at[h, m, quarter]
 
     @staticmethod
     def scratch(hops, streams):
@@ -173,12 +186,23 @@
     def there(self, h):
         return True if h == 0 else lax.axis_index("seq") - h >= 0
 
-    def copy(self, kind, h, m, quarter, device, to=None):
-        source = self.out.at[0 if kind == 0 else h, m, quarter]
-        return remote(source, self.out.at[h, m, quarter], self.sem.at[2 * kind, h, m], self.sem.at[2 * kind + 1, h, m], device)
-
-    def to_hop(self, h, m, peer):
-        return self.copy(0, h, m, place()[1], {"seq": peer})
+    def copy(self, kind, h, m, quarter, device):
+        ref = self.at(h, m, quarter)
+        return remote(ref, ref, self.sem.at[2 * kind, h, m], self.sem.at[2 * kind + 1, h, m], device)
+
+    def relay(self, h, m):
+        s, t = lax.axis_index("seq"), place()[1]
+        return remote(
+            self.at(h, m, t), self.at(h + 1, m, t), self.sem.at[0, h, m], self.sem.at[1, h + 1, m], {"seq": s + 1}
+        )
+
+    def relays(self, h):
+        s = lax.axis_index("seq")
+        return (s - h >= 0) & (s + 1 < self.seq_count)
+
+    def forward(self, h, m):
+        if h < self.hops:
+            pl.when(self.relays(h))(lambda: self.relay(h, m).start())
 
     def spread(self, h, m):
         s, t, y, c, core, far = place()
@@ -186,21 +210,17 @@
         self.copy(2, h, m, t, {"tensor": core}).start()
 
     def start(self, m):
-        s, t, y, c, core, far = place()
-        for h in range(1, self.hops + 1):
-
-            @pl.when(s + h < self.seq_count)
-            def _():
-                self.to_hop(h, m, s + h).start()
-
+        self.forward(0, m)
         if self.first == 0:
             self.spread(0, m)
 
     def arrive(self, h, m):
         @pl.when(self.there(h))
         def _():
-            self.to_hop(h, m, lax.axis_index("seq") - h).wait_recv()
-            self.spread(h, m)
+            self.copy(0, h, m, place()[1], {"seq": lax.axis_index("seq") - 1}).wait_recv()
+
+        self.forward(h, m)
+        pl.when(self.there(h))(lambda: self.spread(h, m))
 
     def pass_on(self, h, m):
         s, t, y, c, core, far = place()
@@ -223,17 +243,15 @@
     def clear(self, h, m):
         @pl.when(lax.axis_index("seq") - h < 0)
         def _():
-            self.out[h, m] = jnp.zeros(self.out.shape[2:], self.out.dtype)
+            for quarter in range(4):
+                ref = self.at(h, m, quarter)
+                ref[...] = jnp.zeros(ref.shape, ref.dtype)
 
     def drain(self):
         s, t, y, c, core, far = place()
         for m in range(self.streams):
-            for h in range(1, self.hops + 1):
-
-                @pl.when(s + h < self.seq_count)
-                def _():
-                    self.to_hop(h, m, s + h).wait_send()
-
+            for h in range(self.hops):
+                pl.when(self.relays(h))(functools.partial(lambda h, m: self.relay(h, m).wait_send(), h, m))
             for h in range(self.first, self.hops + 1):
 
                 def act():
@@ -357,9 +375,6 @@
             def _():
                 id_copy(h, s + h).start()
 
-        ag.to_hop = lambda h, m, peer: remote(
-            x_ref.at[m, t], out.at[h, m, t], sem.at[0, h, m], sem.at[1, h, m], {"seq": peer}
-        )
         for m in range(streams):
             ag.start(m)
         for h in range(1, hops + 1):
@@ -404,43 +419,28 @@
     )(inputs, ids)
 
 
-def exchange(name, cid, seq_count, parts, others, reduce_hops, gather_hops, finish, extra, grads=None):
+def exchange(name, cid, seq_count, parts, others, reduce_hops, gather_hops, finish, extra):
     per_part = parts[0].shape[1]
     rows, width = parts[0].shape[4:]
     streams = per_part * len(parts)
     hops = max(reduce_hops, gather_hops)
-    given = [] if grads is None else [grads]
-    chunks = 0 if grads is None else grads.shape[0]
-    sums, tools = [], []
-    if chunks:
-        depth, wide = grads.shape[1:]
-        sums = [jax.ShapeDtypeStruct((chunks, depth // seq_count, wide), F32)]
-        tools = [pltpu.VMEM((depth // seq_count, wide // 2), F32)] + GradReduce.scratch(seq_count, chunks, depth, wide)
 
     def kernel(*refs):
         refs = list(refs)
         part_refs = [refs.pop(0) for _ in parts]
         other_refs = [refs.pop(0) for _ in others]
-        grad_ref = refs.pop(0) if chunks else None
         out = refs.pop(0)
         extra_refs = [refs.pop(0) for _ in extra]
-        sum_ref = refs.pop(0) if chunks else None
-        grad_tools = [refs.pop(0) for _ in tools]
         acc = refs.pop(0)
         gather_sem = refs.pop(0)
         s, t, y, c, core, far = place()
-        greet(seq_count, hops, wide=bool(chunks))
-        if chunks:
-            grad_acc = grad_tools.pop(0)
-            gr = GradReduce(seq_count, lambda c: grad_ref.at[c], lambda c: sum_ref.at[c], grad_tools)
+        greet(seq_count, hops)
         rs = ReduceScatter(
             seq_count, reduce_hops, streams, lambda h, m: part_refs[m // per_part].at[h, m % per_part], refs
         )
         ag = AllGather(seq_count, gather_hops, streams, out, gather_sem)
         for h, m in rs.order():
             rs.start(h, m)
-        for k in range(chunks):
-            gr.start(k)
         for h in range(1, gather_hops + 1):
             for m in range(streams):
                 ag.clear(h, m)
@@ -448,15 +448,11 @@
             rs.middle(h, m)
         for h, m in rs.order():
             if h:
-                rs.hop(h, m)
-        for k in range(chunks):
-            gr.spread(k)
+                rs.hop(h, m, acc)
         for m in range(streams):
             rs.total(m, acc)
             out[0, m, t] = finish(m, acc[...], other_refs, extra_refs)
             ag.start(m)
-        for k in range(chunks):
-            gr.collect(k, grad_acc)
         for m in range(streams):
             ag.pass_on(0, m)
             for h in range(1, gather_hops + 1):
@@ -467,24 +463,20 @@
         for h in range(gather_hops + 1):
             for m in range(streams):
                 ag.finish(h, m)
-        for k in range(chunks):
-            gr.finish(k)
-            gr.drain(k)
         rs.drain()
         ag.drain()
 
     return pl.pallas_call(
         kernel,
         name=name,
-        out_shape=(jax.ShapeDtypeStruct((gather_hops + 1, streams, 4, rows, width), BF),) + tuple(extra) + tuple(sums),
-        in_specs=in_vmem(len(parts) + len(others) + len(given)),
-        out_specs=tuple(in_vmem(1 + len(extra) + len(sums))),
-        scratch_shapes=tools
-        + [pltpu.VMEM((rows, width), F32)]
+        out_shape=(jax.ShapeDtypeStruct((gather_hops + 1, streams, 4, rows, width), BF),) + tuple(extra),
+        in_specs=in_vmem(len(parts) + len(others)),
+        out_specs=tuple(in_vmem(1 + len(extra))),
+        scratch_shapes=[pltpu.VMEM((rows, width), F32)]
         + AllGather.scratch(gather_hops, streams)
         + ReduceScatter.scratch(reduce_hops, streams, rows, width),
         compiler_params=params(cid),
-    )(*parts, *others, *given)
+    )(*parts, *others)
 
 
 def norm_of(values, gain_row):
@@ -775,14 +767,514 @@
     )(q, k, v, lse, grad_out, row_ids, col_ids, wq, wk, wv, wo)
 
 
+def unit_terms(gate_pre, up_pre, grad_inner):
+    root = 0.7978845608028654
+    square = gate_pre * gate_pre
+    bend = jnp.tanh(root * (gate_pre + 0.044715 * (gate_pre * square)))
+    half = 0.5 * (1.0 + bend)
+    gelu = gate_pre * half
+    slope = half + 0.5 * gate_pre * (1.0 - bend * bend) * (root * (1.0 + 3.0 * 0.044715 * square))
+    return gelu * up_pre, grad_inner * up_pre * slope, grad_inner * gelu
+
+
+def head(
+    x, ids, stu_gain, filter_proj, lag_proj, base, base_back, attn_gain, feed_gain, wq, wk, wv, wo, wg, wu, wd, cot, seq_count
+):
+    streams, _, quarter, width = x.shape
+    length = 4 * quarter
+    hops = WINDOW // length
+    spans = hops + 1
+    count, _, wide = base.shape
+    lag_order, channels = lag_proj.shape[:2]
+    blocks = length // LANES
+    id_rows_each = length // LANES
+    cols, units = wq.shape[1], wg.shape[1]
+    heads = cols // HD
+    tile = 2 * quarter
+    steps = 2 * streams
+    scale = HD ** (-0.5)
+    rows = width // seq_count
+    chunks = 4
+    assert streams == 2 and units == 4 * cols
+
+    rows_of = pltpu.VMEM((streams, length, cols), BF)
+    unit_rows = pltpu.VMEM((streams, length, units), BF)
+    state = pltpu.VMEM((streams, quarter, width), F32)
+    gathered = (1, streams, 4, quarter, width)
+    split_part = pltpu.VMEM((1, streams, 2, 2, quarter, width), BF)
+    zero_hops = ReduceScatter.scratch(0, streams, quarter, width)
+
+    def kernel(
+        x_ref, id_ref, sg_ref, fp_ref, lp_ref, base_ref, back_ref, ag_ref, fg_ref,
+        wq_ref, wk_ref, wv_ref, wo_ref, wg_ref, wu_ref, wd_ref, cot_ref,
+        stu_out, layer_out, one_out, gain_out, sum_out, lag_out, ids_out, conv_out, strip_out,
+        rows_in, ids_in, cols_in, id_ext, lag_ext, part_ref, id_sem, strip_sem, conv_sem,
+        attn_in, feed_in, grad_att, hid_one, hid_two, grad_two, grads, total, grad_acc,
+        o_part, feed_part, layer_part, attn_part,
+        sem_rows, sem_one, sem_two, sem_three, sem_layer, sem_five, *scratch,
+    ):
+        s, t, y, c, core, far = place()
+        scratch = list(scratch)
+
+        def take(count):
+            taken = scratch[:count]
+            del scratch[:count]
+            return taken
+
+        def reducer(ref, distance):
+            return ReduceScatter(seq_count, distance, streams, lambda h, m: ref.at[h, m], take(6))
+
+        rs_one, rs_two, rs_three, rs_layer = [reducer(r, 0) for r in (part_ref, o_part, feed_part, layer_part)]
+        rs_four = reducer(attn_part, hops)
+        gr = GradReduce(seq_count, lambda k: grads.at[k], lambda k: sum_out.at[k], take(8))
+        ag_rows = AllGather(
+            seq_count, seq_count - 1, streams, lambda h, m, q: rows_in.at[m, h, q], sem_rows, first=1
+        )
+        ag_one = AllGather(seq_count, hops, streams, attn_in, sem_one)
+        ag_two = AllGather(seq_count, 0, streams, feed_in, sem_two)
+        ag_three = AllGather(seq_count, 0, streams, grad_att, sem_three)
+        ag_layer = AllGather(seq_count, 0, streams, layer_out, sem_layer)
+        ag_five = AllGather(seq_count, 0, streams, stu_out, sem_five)
+
+        def flat(value):
+            return value.reshape(-1, value.shape[-1])
+
+        def all_rows(ref, m):
+            return flat(ref[0, m])
+
+        def masks_of(m, here, first):
+            return [
+                allowed_keys(cols_in[m, here], ids_out[pl.ds(h * streams + m, 1)], first, h * length) for h in range(spans)
+            ]
+
+        def first_norm(m):
+            rs_one.total(m, total)
+            hidden = x_ref[m, t].astype(F32) + total[...]
+            hid_one[m] = hidden
+            attn_in[0, m, t] = norm_of(hidden, ag_ref[...]).astype(BF)
+            ag_one.start(m)
+
+        def after(i, step, *actions):
+            @pl.when(i == step)
+            def _():
+                for action in actions:
+                    action()
+
+        def id_copy(h, peer):
+            return remote(id_ref, ids_in.at[h], id_sem.at[0, h], id_sem.at[1, h], {"seq": peer})
+
+        far_back = range(1, seq_count)
+
+        def front(strip, left, mask, conv):
+            for m in range(streams):
+                rows_in[m, 0, t] = norm_of(x_ref[m, t].astype(F32), sg_ref[...]).astype(BF)
+            greet(seq_count, 0, wide=True)
+            for m in range(streams):
+                ag_rows.start(m)
+            for h in far_back:
+                pl.when(s + h < seq_count)(functools.partial(lambda h: id_copy(h, s + h).start(), h))
+            for m in range(streams):
+                for q in range(4):
+
+                    @pl.when(t != q)
+                    def _():
+                        rows_in[m, 0, q] = norm_of(x_ref[m, q].astype(F32), sg_ref[...]).astype(BF)
+
+            for m in range(streams):
+                for h in far_back:
+                    ag_rows.clear(h, m)
+                for h in range(1, spans):
+                    ag_one.clear(h, m)
+            ids_in[0] = id_ref[...]
+            for h in far_back:
+
+                @pl.when(s - h < 0)
+                def _():
+                    ids_in[h] = jnp.full(ids_in.shape[1:], -1, jnp.int32)
+
+            strips(back_ref, strip)
+            strip_copy = pltpu.make_async_copy(strip, strip_out, strip_sem)
+            strip_copy.start()
+            for h in far_back:
+                ag_rows.arrive(h, 0)
+            for h in far_back:
+                pl.when(s - h >= 0)(functools.partial(lambda h: id_copy(h, s - h).wait_recv(), h))
+            for h in range(seq_count):
+                values = ids_in[h].astype(F32)
+                for m in range(streams):
+                    first = m * id_rows_each
+                    ids_out[h * streams + m : h * streams + m + 1] = jnp.concatenate(
+                        [values[first + r : first + r + 1] for r in range(id_rows_each)], axis=1
+                    )
+            turned = jnp.transpose(ids_out[...])
+            for m in range(streams):
+                cols_in[m] = turned[:, m : m + 1]
+                id_ext[m, :8] = turned[length - 8 :, streams + m : streams + m + 1]
+                id_ext[m, 8:] = turned[:, m : m + 1]
+            strip_copy.wait()
+            strips(base_ref, strip)
+            for h in far_back:
+                ag_rows.pass_on(h, 0)
+            for h in far_back:
+                ag_rows.arrive(h, 1)
+            for h in far_back:
+                ag_rows.finish(h, 0)
+            mine = pl.ds(pl.multiple_of(t * channels, LANES), channels)
+
+            def lags(m):
+                own = rows_in[m, 0, :, :, mine].reshape(length, channels)
+                lag_ext[:8] = rows_in[m, 1, 3, quarter - 8 :, mine].astype(F32)
+                lag_ext[8:] = own.astype(F32)
+                for i in range(lag_order):
+                    same = id_ext[m, 7 - i : 7 - i + length] == cols_in[m]
+                    lag_out[i, m] = jnp.where(same, lag_ext[7 - i : 7 - i + length], 0.0).astype(BF)
+
+            def conv_copy(k, m):
+                return pltpu.make_async_copy(
+                    conv.at[k], conv_out.at[k, pl.ds(pl.multiple_of(m * length, LANES), length)], conv_sem.at[k]
+                )
+
+            lags(0)
+
+            @pl.loop(0, streams * count)
+            def _(j):
+                m = j // count
+                k = j - m * count
+
+                @pl.when(k == 0)
+                def _():
+                    for h in range(seq_count):
+                        mask[:, h * length : (h + 1) * length] = jnp.where(
+                            cols_in[m] == ids_out[pl.ds(h * streams + m, 1)], 1.0, 0.0
+                        ).astype(BF)
+
+                for a in range(blocks):
+                    for h in range(seq_count):
+                        start = LANES * (blocks * (seq_count - h) - 1 - a)
+                        down, across = slice(a * LANES, (a + 1) * LANES), slice(h * length, (h + 1) * length)
+                        left[down, across] = strip[k, :, start : start + length] * mask[down, across]
+                result = dot_nn(left[...], rows_in[m].reshape(seq_count * length, width)).astype(BF)
+                pl.when(m > 0)(lambda: conv_copy(k, m - 1).wait())
+                conv[k] = result
+                conv_copy(k, m).start()
+
+                @pl.when(k == count - 1)
+                def _():
+                    @pl.loop(0, 2)
+                    def _(half):
+                        here = pl.ds(pl.multiple_of(half * tile, tile), tile)
+                        mixed = sum([dot_nn(conv[q, here], fp_ref[q]) for q in range(count)])
+                        mixed = mixed + sum([dot_nn(lag_out[i, m, here], lp_ref[i]) for i in range(lag_order)])
+                        part_ref[0, m, half] = mixed.astype(BF).reshape(2, quarter, width)
+
+                after(j, 1, *[functools.partial(ag_rows.pass_on, h, 1) for h in far_back])
+                after(
+                    j,
+                    count - 1,
+                    lambda: rs_one.start(0, 0),
+                    *[functools.partial(ag_rows.finish, h, 1) for h in far_back],
+                    lambda: lags(1),
+                )
+                after(j, count, lambda: rs_one.middle(0, 0))
+                after(j, count + 2, lambda: first_norm(0))
+                after(j, count + 4, lambda: ag_one.pass_on(0, 0), lambda: ag_one.arrive(1, 0) if hops > 0 else None)
+
+            rs_one.start(0, 1)
+            for k in range(count):
+                conv_copy(k, streams - 1).wait()
+
+        pl.run_scoped(
+            front,
+            pltpu.VMEM((count, LANES, wide), BF),
+            pltpu.VMEM((length, seq_count * length), BF),
+            pltpu.VMEM((length, seq_count * length), BF),
+            pltpu.VMEM((count, length, width), BF),
+        )
+
+        def attention_on(
+            q_ref, k_ref, v_ref, a_ref, lse_ref, inner_ref, gg_ref, gu_ref, ga_ref, dk_acc, dv_acc, dq_ref, dkv_ref
+        ):
+            rs_one.middle(0, 1)
+            for h in range(2, spans):
+                ag_one.arrive(h, 0)
+            for h in range(1, spans):
+                ag_one.pass_on(h, 0)
+            first_norm(1)
+            for h in range(spans):
+                ag_one.finish(h, 0)
+
+            def split_step(i):
+                m = i // 2
+                return m, i - 2 * m
+
+            @pl.loop(0, steps)
+            def _(i):
+                m, half = split_step(i)
+                first = pl.multiple_of(half * tile, tile)
+                here = pl.ds(first, tile)
+
+                @pl.when(half == 0)
+                def _():
+                    own = flat(attn_in[0, m])
+                    q_ref[m] = dot_nn(own, wq_ref[...]).astype(BF)
+                    for h in range(spans):
+                        block = flat(attn_in[h, m])
+                        k_ref[h, m] = dot_nn(block, wk_ref[...]).astype(BF)
+                        v_ref[h, m] = dot_nn(block, wv_ref[...]).astype(BF)
+
+                masks = masks_of(m, here, first)
+                block = q_ref[m, here]
+                result = jnp.zeros((tile, cols), F32)
+                for head in range(heads):
+                    query = one_head(block, head)
+                    scores = [jnp.where(masks[h], dot_nt(query, k_ref[h, m]) * scale, NEGATIVE) for h in range(spans)]
+                    peak = functools.reduce(jnp.maximum, [jnp.max(v, axis=-1, keepdims=True) for v in scores])
+                    raised = [jnp.exp(v - peak) for v in scores]
+                    norm = sum([jnp.sum(v, axis=-1, keepdims=True) for v in raised])
+                    inverse = 1.0 / norm
+                    mixed = sum([dot_nn((raised[h] * inverse).astype(BF), v_ref[h, m]) for h in range(spans)])
+                    result = result + one_head(mixed, head)
+                    lse_ref[m, head, here] = jnp.broadcast_to(peak + jnp.log(norm), (tile, LANES))
+                low = result.astype(BF)
+                a_ref[m, here] = low
+                o_part[0, m, half] = dot_nn(low, wo_ref[...]).astype(BF).reshape(2, quarter, width)
+                after(i, 0, lambda: ag_one.pass_on(0, 1), *[functools.partial(ag_one.arrive, h, 1) for h in range(1, spans)])
+                after(
+                    i,
+                    1,
+                    lambda: rs_two.start(0, 0),
+                    *[functools.partial(ag_one.pass_on, h, 1) for h in range(1, spans)],
+                    *[functools.partial(ag_one.finish, h, 1) for h in range(spans)],
+                )
+                after(i, 2, lambda: rs_two.middle(0, 0))
+                after(i, 3, lambda: rs_two.start(0, 1))
+
+            def second_norm(m):
+                rs_two.total(m, total)
+                hidden = hid_one[m] + total[...]
+                hid_two[m] = hidden
+                feed_in[0, m, t] = norm_of(hidden, fg_ref[...]).astype(BF)
+                ag_two.start(m)
+
+            second_norm(0)
+            rs_two.middle(0, 1)
+            ag_two.pass_on(0, 0)
+            second_norm(1)
+            ag_two.finish(0, 0)
+
+            @pl.loop(0, steps)
+            def _(i):
+                m, half = split_step(i)
+                here = pl.ds(pl.multiple_of(half * tile, tile), tile)
+                block = flat(feed_in[0, m, pl.ds(2 * half, 2)])
+                inner, grad_gate, grad_up = unit_terms(
+                    dot_nn(block, wg_ref[...]), dot_nn(block, wu_ref[...]), dot_nt(cot_ref[m, here], wd_ref[...])
+                )
+                inner, grad_gate, grad_up = inner.astype(BF), grad_gate.astype(BF), grad_up.astype(BF)
+                inner_ref[m, here] = inner
+                gg_ref[m, here] = grad_gate
+                gu_ref[m, here] = grad_up
+                back = dot_nt(grad_gate, wg_ref[...]) + dot_nt(grad_up, wu_ref[...])
+                feed_part[0, m, half] = back.astype(BF).reshape(2, quarter, width)
+                layer_part[0, m, half] = dot_nn(inner, wd_ref[...]).astype(BF).reshape(2, quarter, width)
+                after(i, 0, lambda: ag_two.pass_on(0, 1))
+                after(i, 1, lambda: rs_three.start(0, 0), lambda: ag_two.finish(0, 1))
+                after(i, 2, lambda: rs_three.middle(0, 0))
+                after(i, 3, lambda: rs_three.start(0, 1))
+
+            def third_norm(m):
+                rs_three.total(m, total)
+                grad_in, gain_grad = norm_back(hid_two[m], fg_ref[...], total[...])
+                value = cot_ref[m, pl.ds(pl.multiple_of(t * quarter, quarter), quarter)].astype(F32) + grad_in
+                grad_two[m] = value
+                gain_out[1:2] = gain_grad if m == 0 else gain_out[1:2] + gain_grad
+                grad_att[0, m, t] = value.astype(BF)
+                ag_three.start(m)
+
+            third_norm(0)
+            feed_all = flat(feed_in[0])
+            grads[0] = dot_tn(feed_all, flat(gg_ref[...])).astype(BF)
+            gr.start(0)
+            rs_three.middle(0, 1)
+            ag_three.pass_on(0, 0)
+            grads[1] = dot_tn(feed_all, flat(gu_ref[...])).astype(BF)
+            gr.start(1)
+            third_norm(1)
+            ag_three.finish(0, 0)
+            grads[2] = dot_tn(flat(cot_ref[...]), flat(inner_ref[...])).astype(BF)
+            gr.start(2)
+            for m in range(streams):
+                rs_layer.start(0, m)
+
+            def layer_sum(m):
+                rs_layer.total(m, total)
+                layer_out[0, m, t] = (hid_two[m] + total[...]).astype(BF)
+                ag_layer.start(m)
+
+            @pl.loop(0, steps)
+            def _(i):
+                m, half = split_step(i)
+                first = pl.multiple_of(half * tile, tile)
+                here = pl.ds(first, tile)
+
+                @pl.when(half == 0)
+                def _():
+                    ga_ref[...] = dot_nt(all_rows(grad_att, m), wo_ref[...]).astype(BF)
+                    dk_acc[...] = jnp.zeros_like(dk_acc)
+                    dv_acc[...] = jnp.zeros_like(dv_acc)
+
+                masks = masks_of(m, here, first)
+                block = q_ref[m, here]
+                grad_block = ga_ref[here]
+                result = jnp.zeros((tile, cols), F32)
+                for head in range(heads):
+                    query = one_head(block, head)
+                    grad = one_head(grad_block, head)
+                    level = lse_ref[m, head, here][:, :1]
+                    prob = [
+                        jnp.where(masks[h], jnp.exp(dot_nt(query, k_ref[h, m]) * scale - level), 0.0) for h in range(spans)
+                    ]
+                    grad_prob = [dot_nt(grad, v_ref[h, m]) for h in range(spans)]
+                    mean = sum([jnp.sum(p * g, axis=-1, keepdims=True) for p, g in zip(prob, grad_prob)])
+                    grad_scores = [(p * (g - mean)).astype(BF) for p, g in zip(prob, grad_prob)]
+                    for h in range(spans):
+                        dv_acc[h] += dot_tn(prob[h].astype(BF), grad)
+                        dk_acc[h] += dot_tn(grad_scores[h], query)
+                    mixed = sum([dot_nn(grad_scores[h], k_ref[h, m]) for h in range(spans)])
+                    result = result + one_head(mixed, head)
+                dq_ref[m, here] = (result * scale).astype(BF)
+
+                @pl.when(half == 1)
+                def _():
+                    for h in range(hops, -1, -1):
+                        grad_k = (dk_acc[h] * scale).astype(BF)
+                        grad_v = dv_acc[h].astype(BF)
+                        dkv_ref[h, m, :, :cols] = grad_k
+                        dkv_ref[h, m, :, cols:] = grad_v
+                        back = dot_nt(grad_k, wk_ref[...]) + dot_nt(grad_v, wv_ref[...])
+                        if h == 0:
+                            back = back + dot_nt(dq_ref[m], wq_ref[...])
+                        attn_part[h, m] = back.astype(BF).reshape(2, 2, quarter, width)
+                        rs_four.start(h, m)
+
+                after(i, 0, lambda: ag_three.pass_on(0, 1), lambda: rs_layer.middle(0, 0), lambda: rs_layer.middle(0, 1))
+                after(i, 1, lambda: ag_three.finish(0, 1), lambda: gr.spread(0), lambda: layer_sum(0), lambda: layer_sum(1))
+                after(i, 2, *[functools.partial(rs_four.middle, h, 0) for h in range(hops, -1, -1)], lambda: gr.spread(1))
+                after(i, 3, *[functools.partial(rs_four.hop, h, 0, total) for h in range(hops, 0, -1)], lambda: gr.spread(2))
+
+            attn_all = attn_in[...].reshape(spans * streams * length, width)
+            grads[3, :, cols : 3 * cols] = dot_tn(attn_all, flat(dkv_ref[...].reshape(-1, 2 * cols))).astype(BF)
+            for h in range(hops, -1, -1):
+                rs_four.middle(h, 1)
+            grads[3, :, :cols] = dot_tn(flat(attn_in[0]), flat(dq_ref[...])).astype(BF)
+            grads[3, :, 3 * cols :] = dot_tn(flat(grad_att[0]), flat(a_ref[...])).astype(BF)
+            gr.start(3)
+            for h in range(hops, 0, -1):
+                rs_four.hop(h, 1, total)
+            for m in range(streams):
+                rs_four.total(m, total)
+                grad_in, gain_grad = norm_back(hid_one[m], ag_ref[...], total[...])
+                value = grad_two[m] + grad_in
+                one_out[m] = value
+                gain_out[0:1] = gain_grad if m == 0 else gain_out[0:1] + gain_grad
+                stu_out[0, m, t] = value.astype(BF)
+                ag_five.start(m)
+                gr.collect(m, grad_acc)
+                ag_layer.pass_on(0, m)
+            gr.spread(3)
+            for m in range(streams):
+                ag_five.pass_on(0, m)
+            gr.collect(2, grad_acc)
+            for m in range(streams):
+                ag_layer.finish(0, m)
+            gr.collect(3, grad_acc)
+            for m in range(streams):
+                ag_five.finish(0, m)
+            for k in range(chunks):
+                gr.finish(k)
+                gr.drain(k)
+            for item in (rs_one, rs_two, rs_three, rs_layer, rs_four, ag_rows, ag_one, ag_two, ag_three, ag_layer, ag_five):
+                item.drain()
+            for h in far_back:
+                pl.when(s + h < seq_count)(functools.partial(lambda h: id_copy(h, s + h).wait_send(), h))
+
+        pl.run_scoped(
+            attention_on,
+            rows_of,
+            pltpu.VMEM((spans, streams, length, cols), BF),
+            pltpu.VMEM((spans, streams, length, cols), BF),
+            rows_of,
+            pltpu.VMEM((streams, heads, length, LANES), F32),
+            unit_rows,
+            unit_rows,
+            unit_rows,
+            pltpu.VMEM((length, cols), BF),
+            pltpu.VMEM((spans, length, cols), F32),
+            pltpu.VMEM((spans, length, cols), F32),
+            rows_of,
+            pltpu.VMEM((spans, streams, length, 2 * cols), BF),
+        )
+
+    anywhere = pl.BlockSpec(memory_space=pl.ANY)
+    return pl.pallas_call(
+        kernel,
+        name="head",
+        out_shape=(
+            jax.ShapeDtypeStruct(gathered, BF),
+            jax.ShapeDtypeStruct(gathered, BF),
+            jax.ShapeDtypeStruct((streams, quarter, width), F32),
+            jax.ShapeDtypeStruct((2, width), F32),
+            jax.ShapeDtypeStruct((chunks, rows, units), F32),
+            jax.ShapeDtypeStruct((lag_order, streams, length, channels), BF),
+            jax.ShapeDtypeStruct((seq_count * streams, length), F32),
+            jax.ShapeDtypeStruct((count, streams * length, width), BF),
+            jax.ShapeDtypeStruct((count, LANES, wide), BF),
+        ),
+        in_specs=in_vmem(17),
+        out_specs=tuple(in_vmem(7)) + (anywhere, anywhere),
+        scratch_shapes=[
+            pltpu.VMEM((streams, seq_count, 4, quarter, width), BF),
+            pltpu.VMEM((seq_count,) + ids.shape, jnp.int32),
+            pltpu.VMEM((streams, length, 1), F32),
+            pltpu.VMEM((streams, length + 8, 1), F32),
+            pltpu.VMEM((length + 8, channels), F32),
+            split_part,
+            pltpu.SemaphoreType.DMA((2, seq_count)),
+            pltpu.SemaphoreType.DMA,
+            pltpu.SemaphoreType.DMA((count,)),
+            pltpu.VMEM((spans, streams, 4, quarter, width), BF),
+            pltpu.VMEM(gathered, BF),
+            pltpu.VMEM(gathered, BF),
+            state,
+            state,
+            state,
+            pltpu.VMEM((chunks, width, units), BF),
+            pltpu.VMEM((quarter, width), F32),
+            pltpu.VMEM((rows, units // 2), F32),
+            split_part,
+            split_part,
+            split_part,
+            pltpu.VMEM((spans, streams, 2, 2, quarter, width), BF),
+            AllGather.scratch(seq_count - 1, streams)[0],
+            AllGather.scratch(hops, streams)[0],
+        ]
+        + [AllGather.scratch(0, streams)[0]] * 4
+        + zero_hops * 4
+        + ReduceScatter.scratch(hops, streams, quarter, width)
+        + GradReduce.scratch(seq_count, chunks, width, units),
+        compiler_params=params(8),
+    )(
+        x, ids, stu_gain, filter_proj, lag_proj, base, base_back, attn_gain, feed_gain, wq, wk, wv, wo, wg, wu, wd, cot
+    )
+
+
 def tail(
-    grad_stu, filter_proj, lag_proj, conv, lag_stack, lag_masks, row_ids, ext_ids, base, x, gain, grad_one, gains, seq_count
+    grad_stu, filter_proj, lag_proj, conv, lag_stack, ext_ids, strip_back, x, gain, grad_one, gains, seq_count
 ):
     count, length_all, width = conv.shape
     streams, _, quarter, _ = x.shape
     length = length_all // streams
     lag_order, channels = lag_proj.shape[:2]
-    wide = base.shape[2]
     blocks = length // LANES
     hops = seq_count - 1
     chunks = count + 1
@@ -791,14 +1283,27 @@
     gain_rows = 8
 
     def kernel(
-        gs_ref, fp_ref, lp_ref, conv_ref, lag_ref, mask_ref, row_ref, ext_ref, base_ref, x_ref, gain_ref, one_ref, gains_ref,
+        gs_ref, fp_hbm, lp_ref, conv_hbm, lag_ref, ext_ref, strip_hbm, x_ref, gain_ref, one_ref, gains_ref,
         out, filter_out, lag_out, gain_out,
-        strip, mask, cols, left, acc, terms, grad_conv, grads, lag_ext, total, grad_acc, gather_sem,
+        conv_ref, fp_ref, strip, conv_sem, fp_sem, strip_sem, id_ext,
+        mask, cols, left, acc, terms, grad_conv, grads, lag_ext, total, grad_acc, gather_sem,
         gain_own, gain_near, gain_sum, gain_far, near_sem, far_sem, *scratch,
     ):
         s, t, y, c, core, far = place()
         p = lax.axis_index("dp")
         rs_scratch, gr_scratch = scratch[:6], scratch[6:]
+
+        def conv_copy(k):
+            return pltpu.make_async_copy(conv_hbm.at[k], conv_ref.at[k], conv_sem.at[k])
+
+        def fp_copy(k):
+            return pltpu.make_async_copy(fp_hbm.at[k], fp_ref.at[k], fp_sem.at[k])
+
+        strip_copy = pltpu.make_async_copy(strip_hbm, strip, strip_sem)
+        for k in range(count):
+            conv_copy(k).start()
+            fp_copy(k).start()
+        strip_copy.start()
         greet(seq_count, hops, wide=True, gains=True)
 
         def source(k):
@@ -815,8 +1320,10 @@
 
         @pl.loop(0, count)
         def _(k):
+            conv_copy(k).wait()
             grads[k] = dot_tn(conv_ref[k], gs_ref[...]).astype(BF)
             gr.start(k)
+            fp_copy(k).wait()
             product = dot_nt(gs_ref[...], fp_ref[k]).astype(BF)
             for m in range(streams):
                 here = pl.ds(pl.multiple_of(k * length, LANES), length)
@@ -830,15 +1337,18 @@
         for i in range(lag_order):
             grads[count, :, i * channels : (i + 1) * channels] = dot_tn(gs_ref[...], lag_ref[i]).astype(BF)
         gr.start(count)
+        turned = jnp.transpose(ext_ref[...])
+        for j in range(steps):
+            cols[j] = turned[:, j : j + 1]
         for m in range(streams):
             lag_ext[m] = jnp.zeros_like(lag_ext.at[m])
+            id_ext[:8] = turned[length - 8 :, streams + m : streams + m + 1]
+            id_ext[8:] = turned[:, m : m + 1]
             for i in range(lag_order):
-                term = dot_nt(gs_ref[m * length : (m + 1) * length], lp_ref[i]) * mask_ref[i, m]
-                lag_ext[m, 7 - i : 7 - i + length] += term
-        strips(base_ref, strip)
-        turned = jnp.transpose(ext_ref[...].astype(F32))
-        for j in range(steps):
-            cols[j] = turned[:, j : j + 1]
+                term = dot_nt(gs_ref[m * length : (m + 1) * length], lp_ref[i])
+                same = id_ext[7 - i : 7 - i + length] == cols[m]
+                lag_ext[m, 7 - i : 7 - i + length] += jnp.where(same, term, 0.0)
+        strip_copy.wait()
         mine = pl.ds(pl.multiple_of(t * channels, LANES), channels)
         spread_at = {}
         collect_at = {}
@@ -858,7 +1368,7 @@
 
             @pl.when(h <= s)
             def _():
-                mask[...] = jnp.where(cols[h * streams + m] == row_ref[m].astype(F32), 1.0, 0.0).astype(BF)
+                mask[...] = jnp.where(cols[h * streams + m] == ext_ref[pl.ds(m, 1)], 1.0, 0.0).astype(BF)
                 for k in range(count):
                     for a in range(blocks):
                         start = pl.multiple_of(LANES * (blocks * h + blocks - 1 - a), LANES)
@@ -886,7 +1396,7 @@
 
             @pl.when((i >= 2) & (i < steps - streams + 2))
             def _():
-                rs.hop(*step_of(i - 2))
+                rs.hop(*step_of(i - 2), total)
 
             for step, k in spread_at.items():
                 pl.when(i == step)(functools.partial(gr.spread, k))
@@ -946,6 +1456,7 @@
         rs.drain()
         ag.drain()
 
+    anywhere = pl.BlockSpec(memory_space=pl.ANY)
     return pl.pallas_call(
         kernel,
         name="tail",
@@ -955,10 +1466,16 @@
             jax.ShapeDtypeStruct((rows, width), F32),
             jax.ShapeDtypeStruct((gain_rows, rows), F32),
         ),
-        in_specs=in_vmem(13),
+        in_specs=[anywhere if i in (1, 3, 6) else spec for i, spec in enumerate(in_vmem(11))],
         out_specs=tuple(in_vmem(4)),
         scratch_shapes=[
-            pltpu.VMEM((count, LANES, wide), BF),
+            pltpu.VMEM(conv.shape, BF),
+            pltpu.VMEM(filter_proj.shape, BF),
+            pltpu.VMEM(strip_back.shape, BF),
+            pltpu.SemaphoreType.DMA((count,)),
+            pltpu.SemaphoreType.DMA((count,)),
+            pltpu.SemaphoreType.DMA,
+            pltpu.VMEM((length + 8, 1), F32),
             pltpu.VMEM((length, length), BF),
             pltpu.VMEM((steps, length, 1), F32),
             pltpu.VMEM((length, count * length), BF),
@@ -981,7 +1498,7 @@
         + GradReduce.scratch(seq_count, chunks, width, width),
         compiler_params=params(7),
     )(
-        grad_stu, filter_proj, lag_proj, conv, lag_stack, lag_masks, row_ids, ext_ids, base, x, gain, grad_one, gains
+        grad_stu, filter_proj, lag_proj, conv, lag_stack, ext_ids, strip_back, x, gain, grad_one, gains
     )
 
 
@@ -1032,14 +1549,7 @@
     x = tokens[:, 0]
     grad_three = cotangent[:, 0]
     ids = document_index[:, 0]
-    inputs = norm_of(x.astype(F32), stu_gain).astype(BF)
     id_tile = ids.reshape(streams * length // LANES, LANES)
-    rows_ext, id_ext = gather_rows(quarters(inputs), id_tile, seq_count)
-    rows_ext = whole(rows_ext)
-    id_ext = id_ext.reshape(seq_count, streams, length)
-    id_rows = id_ext[:, :, None, :]
-    id_cols = id_ext[:, :, :, None]
-
     pad = jnp.zeros((count, 4 * LANES), filters.dtype)
     ahead = row_len - LANES
     base = jnp.concatenate(
@@ -1053,6 +1563,51 @@
     base_back = jnp.concatenate(
         [pad[:, : length - LANES], filters, pad[:, :LANES]], axis=1
     ).astype(F32)[:, None]
+
+    tokens_flat = streams * length
+    cols = query_weight.shape[1]
+
+    def answer(layer_output, input_gradient, gains, filter_grad, lag_grad, attn_grads, feed_grads):
+        query_grad, key_grad, value_grad, output_grad = jnp.split(attn_grads, [cols, 2 * cols, 3 * cols], axis=1)
+        gate_grad, up_grad, down_grad = feed_grads
+        return (
+            layer_output[:, None],
+            input_gradient[:, None],
+            gains[0],
+            filter_grad,
+            lag_grad[:, : lag_order * channels].T.reshape(lag_order, channels, -1),
+            gains[1],
+            query_grad,
+            key_grad,
+            value_grad,
+            output_grad.T,
+            gains[2],
+            gate_grad,
+            up_grad,
+            down_grad.T,
+        )
+
+    if width // seq_count % LANES == 0:
+        grad_stu, layer_output, grad_one, gain_grads, sums, lag_stack, ext_ids, conv, strip_back = head(
+            quarters(x), id_tile, row(stu_gain), filter_proj, lag_proj, base, base_back, row(attention_gain), row(feed_gain),
+            query_weight, key_weight, value_weight, output_weight, gate_weight, up_weight, down_weight, grad_three, seq_count,
+        )
+        input_gradient, filter_grad, lag_grad, gains = tail(
+            grad_stu.reshape(tokens_flat, width), filter_proj, lag_proj, conv,
+            lag_stack.reshape(lag_order, tokens_flat, channels), ext_ids, strip_back, quarters(x), row(stu_gain), grad_one,
+            gain_grads, seq_count,
+        )
+        return answer(
+            whole(layer_output)[0], whole(input_gradient)[0], gains, filter_grad, lag_grad, sums[3], (sums[0], sums[1], sums[2])
+        )
+
+    inputs = norm_of(x.astype(F32), stu_gain).astype(BF)
+    rows_ext, id_ext = gather_rows(quarters(inputs), id_tile, seq_count)
+    rows_ext = whole(rows_ext)
+    id_ext = id_ext.reshape(seq_count, streams, length)
+    id_rows = id_ext[:, :, None, :]
+    id_cols = id_ext[:, :, :, None]
+
     conv = convolve(rows_ext, id_rows, id_cols[0], base, seq_count)
 
     chan_rows = lax.dynamic_slice_in_dim(rows_ext[:2], chan_start, channels, 3)
@@ -1121,7 +1676,6 @@
         extra[1][...] = gain_grad if m == 0 else extra[1][...] + gain_grad
         return grad_two.astype(BF)
 
-    fused = width // seq_count % LANES == 0
     feed_grads = jnp.stack(
         [
             dot_tn(feed_in, grad_gate).astype(BF),
@@ -1130,14 +1684,10 @@
         ]
     )
     shape = (1, streams, length, width)
-    results = exchange(
+    both, grad_two, feed_gain_grad = exchange(
         "exchange_three", 4, seq_count, [split(feed_part.reshape(shape)), split(layer_part.reshape(shape))],
         [hidden_two, row(feed_gain), quarters(grad_three)], 0, 0, finish_three, [state, gain_state],
-        feed_grads if fused else None,
     )
-    both, grad_two, feed_gain_grad = results[:3]
-    if fused:
-        feed_grads = results[3]
     both = whole(both)[0]
     grad_att_out = both[:streams]
     layer_output = both[streams:]
@@ -1146,7 +1696,6 @@
         q, k, v, lse, grad_att_out, id_rows[: hops + 1], id_cols[0], query_weight, key_weight, value_weight, output_weight
     )
 
-    tokens_flat = streams * length
     go = grad_att_out.reshape(tokens_flat, width)
     attn_grads = jnp.concatenate(
         [
@@ -1166,82 +1715,50 @@
         extra[1][...] = gain_grad if m == 0 else extra[1][...] + gain_grad
         return grad_one.astype(BF)
 
-    results = exchange(
+    grad_stu, grad_one, attn_gain_grad = exchange(
         "exchange_four", 5, seq_count, [split(attn_part)], [hidden_one, row(attention_gain), grad_two], hops, 0,
-        finish_four, [state, gain_state], attn_grads[None] if fused else None,
+        finish_four, [state, gain_state],
     )
-    grad_stu, grad_one, attn_gain_grad = results[:3]
     grad_stu = whole(grad_stu)[0]
-    lag_masks = jnp.stack(masks).astype(F32)
-    if fused:
-        attn_grads = results[3][0]
-        input_gradient, filter_grad, lag_grad, gains = tail(
-            grad_stu.reshape(tokens_flat, width), filter_proj, lag_proj, conv.reshape(count, tokens_flat, width),
-            lag_stack.reshape(lag_order, tokens_flat, channels), lag_masks, id_rows[0],
-            id_ext.reshape(seq_count * streams, length), base_back,
-            quarters(x), row(stu_gain), grad_one, jnp.concatenate([attn_gain_grad, feed_gain_grad], axis=0), seq_count,
-        )
-        input_gradient = whole(input_gradient)[0]
-    else:
-        grad_conv = jnp.einsum("mte,kde->kmtd", grad_stu, filter_proj, preferred_element_type=F32).astype(BF)
-        grad_lagged = jnp.einsum("mte,ice->imtc", grad_stu, lag_proj, preferred_element_type=F32)
-        ext_grad = jnp.zeros((streams, 8 + length, channels), F32)
-        for step in range(1, lag_order + 1):
-            term = jnp.where(masks[step - 1], grad_lagged[step - 1], 0.0)
-            ext_grad = ext_grad + jnp.pad(term, ((0, 0), (8 - step, step), (0, 0)))
-        terms = convolve_back(
-            grad_conv, id_rows[0], id_cols, base_back, ext_grad[:, 8:], ext_grad[:, :8], seq_count
-        )
-
-        def finish_five(m, total, others, extra):
-            x_ref, gain_ref, grad_ref = others
-            grad_in, gain_grad = norm_back(x_ref[m, place()[1]].astype(F32), gain_ref[...], total)
-            extra[0][...] = gain_grad if m == 0 else extra[0][...] + gain_grad
-            return (grad_ref[m] + grad_in).astype(BF)
-
-        input_gradient, stu_gain_grad = exchange(
-            "exchange_five", 6, seq_count, [split(terms)], [quarters(x), row(stu_gain), grad_one], seq_count - 1, 0,
-            finish_five, [gain_state],
-        )
-        input_gradient = whole(input_gradient)[0]
-        stu = grad_stu.reshape(tokens_flat, width)
-        filter_part = jnp.einsum("kmtd,mte->kde", conv, grad_stu, preferred_element_type=F32).astype(BF)
-        lag_part = jnp.concatenate(
-            [dot_tn(stu, lag_stack[i].reshape(tokens_flat, channels)).astype(BF) for i in range(lag_order)], axis=1
-        )
-        feed_grads = lax.psum(
-            lax.psum_scatter(feed_grads, "seq", scatter_dimension=1, tiled=True), "dp"
-        ).astype(F32)
-        attn_grads = lax.psum(lax.psum_scatter(attn_grads, "seq", scatter_dimension=0, tiled=True), "dp").astype(F32)
-        filter_grad = lax.psum(
-            lax.psum_scatter(filter_part, "seq", scatter_dimension=1, tiled=True), "dp"
-        ).astype(F32)
-        lag_grad = lax.psum(lax.psum_scatter(lag_part, "seq", scatter_dimension=0, tiled=True), "dp").astype(F32)
-        gains = jnp.concatenate([stu_gain_grad, attn_gain_grad, feed_gain_grad], axis=0)
-        gains = lax.psum(gains, ("dp", "seq", "tensor"))
-        gain_width = width // seq_count
-        gains = lax.dynamic_slice_in_dim(gains, lax.axis_index("seq") * gain_width, gain_width, 1)
-
-    cols = query_weight.shape[1]
-    gate_grad, up_grad, down_grad = feed_grads
-    query_grad, key_grad, value_grad, output_grad = jnp.split(attn_grads, [cols, 2 * cols, 3 * cols], axis=1)
-    lag_grad = lag_grad[:, : lag_order * channels].T.reshape(lag_order, channels, -1)
-    return (
-        layer_output[:, None],
-        input_gradient[:, None],
-        gains[0],
-        filter_grad,
-        lag_grad,
-        gains[1],
-        query_grad,
-        key_grad,
-        value_grad,
-        output_grad.T,
-        gains[2],
-        gate_grad,
-        up_grad,
-        down_grad.T,
+    grad_conv = jnp.einsum("mte,kde->kmtd", grad_stu, filter_proj, preferred_element_type=F32).astype(BF)
+    grad_lagged = jnp.einsum("mte,ice->imtc", grad_stu, lag_proj, preferred_element_type=F32)
+    ext_grad = jnp.zeros((streams, 8 + length, channels), F32)
+    for step in range(1, lag_order + 1):
+        term = jnp.where(masks[step - 1], grad_lagged[step - 1], 0.0)
+        ext_grad = ext_grad + jnp.pad(term, ((0, 0), (8 - step, step), (0, 0)))
+    terms = convolve_back(
+        grad_conv, id_rows[0], id_cols, base_back, ext_grad[:, 8:], ext_grad[:, :8], seq_count
     )
+
+    def finish_five(m, total, others, extra):
+        x_ref, gain_ref, grad_ref = others
+        grad_in, gain_grad = norm_back(x_ref[m, place()[1]].astype(F32), gain_ref[...], total)
+        extra[0][...] = gain_grad if m == 0 else extra[0][...] + gain_grad
+        return (grad_ref[m] + grad_in).astype(BF)
+
+    input_gradient, stu_gain_grad = exchange(
+        "exchange_five", 6, seq_count, [split(terms)], [quarters(x), row(stu_gain), grad_one], seq_count - 1, 0,
+        finish_five, [gain_state],
+    )
+    input_gradient = whole(input_gradient)[0]
+    stu = grad_stu.reshape(tokens_flat, width)
+    filter_part = jnp.einsum("kmtd,mte->kde", conv, grad_stu, preferred_element_type=F32).astype(BF)
+    lag_part = jnp.concatenate(
+        [dot_tn(stu, lag_stack[i].reshape(tokens_flat, channels)).astype(BF) for i in range(lag_order)], axis=1
+    )
+    feed_grads = lax.psum(
+        lax.psum_scatter(feed_grads, "seq", scatter_dimension=1, tiled=True), "dp"
+    ).astype(F32)
+    attn_grads = lax.psum(lax.psum_scatter(attn_grads, "seq", scatter_dimension=0, tiled=True), "dp").astype(F32)
+    filter_grad = lax.psum(
+        lax.psum_scatter(filter_part, "seq", scatter_dimension=1, tiled=True), "dp"
+    ).astype(F32)
+    lag_grad = lax.psum(lax.psum_scatter(lag_part, "seq", scatter_dimension=0, tiled=True), "dp").astype(F32)
+    gains = jnp.concatenate([stu_gain_grad, attn_gain_grad, feed_gain_grad], axis=0)
+    gains = lax.psum(gains, ("dp", "seq", "tensor"))
+    gain_width = width // seq_count
+    gains = lax.dynamic_slice_in_dim(gains, lax.axis_index("seq") * gain_width, gain_width, 1)
+    return answer(layer_output, input_gradient, gains, filter_grad, lag_grad, attn_grads, feed_grads)
 
 
 def solution(mesh):

time: 383 us -> 269 us (0.70)
  Pallas kernels: 323 us -> 246 us
  matrix products: 23.9 us -> 0 us
  other arithmetic: 11.9 us -> 1.38 us
    pallas_call x8 -> x1, Pallas kernels: 235 us -> 172 us  [head(): pl.pallas_call(kernel, name='head', out_shape=(jax.ShapeDtypeStruct(gathe...]
    dot_general x15 -> x0, matrix products: 23.9 us -> none  [the longest x1 7.51 us: local(): jnp.einsum('kmtd,kde->mte', conv, filter_proj, preferred_element_type=F32)]
    pallas_call x1, Pallas kernels: 88 us -> 73.8 us  [tail(): pl.pallas_call(kernel, name='tail', out_shape=(jax.ShapeDtypeStruct((1, s...]
    slice x7 -> x0, local copies, waits for them, and re-layouts: 5.63 us -> none  [the longest x1 3.04 us: local(): grad_att_out = both[:streams]]
    unnamed x56 -> x10, local copies, waits for them, and re-layouts: 7.88 us -> 12.1 us
where the time goes in v5:
time: 269 us; the launch traced here: 268 us
  Pallas kernels  246 us (91%)
  local copies, waits for them, and re-layouts  19.9 us (7%)
    pallas_call x1, Pallas kernels, head(): pl.pallas_call(kernel, name='head', out_shape=(jax.ShapeDtypeStruct(gathe...  172 us
    pallas_call x1, Pallas kernels, tail(): pl.pallas_call(kernel, name='tail', out_shape=(jax.ShapeDtypeStruct((1, s...  73.8 us
    unnamed x10, local copies, waits for them, and re-layouts  12.1 us

profile of v5, /device:TPU:0, one launch (start us, length us, event | category | flops | bytes accessed | tf_op | source)
XLA Modules:
  0.0 268.2 jit_solution(11023648333760994672)
XLA Ops:
  0.6 0.8 slice.37
  1.4 0.1 rev.9
  1.5 6.1 %reverse = bf16[6,2048]{1,0:T(8,128)(2,1)S(1)} reverse(bf16[6,2048]{1,0:T(8,128)(2,1)} %param.18), dimensions={1} | reverse | bytes 49152
  7.7 0.1 slice_bitcast_fusion.9
  7.8 0.2 concatenate.28
  8.0 0.7 convert_element_type.20.base_ref
  8.7 0.8 copy.37
  9.5 0.7 maximum_convert_fusion.back_ref
  10.2 172.5 %head.1 = (bf16[1,2,4,128,512]{4,3,2,1,0:T(8,128)(2,1)}, bf16[1,2,4,128,512]{4,3,2,1,0:T(8,128)(2,1)}, f32[2,128,512]{2,1,0:T(8,128)}, f32[2,512]{1,0:T(2,128)},...) custom-call(bf16[2,4,128,512]{3,2,1,0:T(8,128)(2,1)} %bitcast.41, ...), custom_call_target="tpu_custom_call" | custom-call | tf_op jit(solution)/shard_map/head/pallas_call | solution.py:1219
  182.6 73.8 %tail.1 = (bf16[1,2,4,128,512]{4,3,2,1,0:T(8,128)(2,1)}, f32[6,128,512]{2,1,0:T(8,128)}, f32[128,512]{1,0:T(8,128)}, f32[8,128]{1,0:T(8,128)}) custom-call(bf16[1024,512]{1,0:T(8,128)(2,1)} %bitcast.44, bf16[6,512,512]{2,1,0:T(8,128)(2,1)} %fp_hbm.1, bf16[3,128,512]{2,1,0:T(8,128)(2,1)} %lp_ref.3, bf16[6,1024,512]{2,1,0:T(8,128)(2,1)} %get-tuple-element.29.conv_hbm, ...), custom_call_target="tpu_custom_call" | custom-call | tf_op jit(solution)/shard_map/tail/pallas_call | solution.py:1460
  256.5 0.0 copy-start.1
  256.5 1.3 slice_bitcast_fusion.6
  257.8 0.9 slice_bitcast_fusion.4
  258.7 0.8 copy.38
  259.5 2.1 slice_bitcast_fusion
  261.6 0.0 copy-start
  261.6 0.8 copy.42
  262.4 0.7 slice_bitcast_fusion.5
  263.1 0.7 copy.41
  263.9 0.0 copy-done.1
  263.9 1.0 copy.46
  264.8 2.3 copy.47
  267.1 0.0 copy-done
  267.1 1.1 copy.48
  (7 shorter events, 0.1 us)
Async XLA Ops:
  256.5 7.4 %copy-start.1 = (bf16[1,2,4,128,512]{4,3,2,1,0:T(8,128)(2,1)S(1)}, bf16[1,2,4,128,512]{4,3,2,1,0:T(8,128)(2,1)}, u32[]{:S(2)}) copy-start(bf16[1,2,4,128,512]{4,3,2,1,0:T(8,128)(2,1)} %get-tuple-element.27) | copy-start | bytes 3145732
  261.6 5.5 %copy-start = (f32[6,128,512]{2,1,0:T(8,128)S(1)}, f32[6,128,512]{2,1,0:T(8,128)}, u32[]{:S(2)}) copy-start(f32[6,128,512]{2,1,0:T(8,128)} %get-tuple-element.96) | copy-start | bytes 4718596

commit v6 on v5

--- a/solution.py
+++ b/solution.py
@@ -336,8 +336,8 @@
     def finish(self, c):
         p = lax.axis_index("dp")
         self.back(c).wait_recv()
-        self.result(c)[:, self.columns(p)] = self.back_out[c].astype(F32)
-        self.result(c)[:, self.columns(1 - p)] = self.back_in[c].astype(F32)
+        self.result(c)[:, self.columns(p)] = self.back_out[c]
+        self.result(c)[:, self.columns(1 - p)] = self.back_in[c]
 
     def drain(self, c):
         self.over(c).wait_send()
@@ -495,8 +495,29 @@
 def strips(base_ref, strip):
     @pl.loop(0, base_ref.shape[0])
     def _(k):
-        row = jnp.broadcast_to(base_ref[k], strip.shape[1:])
+        taps = base_ref[k] if len(base_ref.shape) == 3 else base_ref[pl.ds(k, 1)]
+        row = jnp.broadcast_to(taps, strip.shape[1:])
         strip[k] = pltpu.roll(row, 0, 1, stride=1, stride_axis=0).astype(BF)
+
+
+def lay_taps(taps_ref, base_ref, back):
+    count, length = taps_ref.shape
+    blocks = length // LANES
+    base_ref[...] = jnp.zeros_like(base_ref)
+    if back:
+        base_ref[:, 3 * LANES : 3 * LANES + length] = taps_ref[...].astype(F32)
+        return
+    row = lax.broadcasted_iota(jnp.int32, (LANES, LANES), 0)
+    lane = lax.broadcasted_iota(jnp.int32, (LANES, LANES), 1)
+    turn = jnp.where(row + lane == LANES, 1.0, 0.0).astype(BF)
+    first = lax.broadcasted_iota(jnp.int32, (count, LANES), 1) == 0
+    turned = [dot_nn(taps_ref[:, j * LANES : (j + 1) * LANES], turn) for j in range(blocks)]
+    for b in range(blocks):
+        j = blocks - 1 - b
+        below = turned[j - 1] if j else jnp.zeros((count, LANES), F32)
+        taps = taps_ref[:, j * LANES : (j + 1) * LANES].astype(F32)
+        base_ref[:, b * LANES : (b + 1) * LANES] = jnp.where(first, taps, below)
+    base_ref[:, (blocks + 3) * LANES :] = turned[blocks - 1]
 
 
 def convolve(rows, row_ids, col_ids, base, seq_count):
@@ -778,16 +799,16 @@
 
 
 def head(
-    x, ids, stu_gain, filter_proj, lag_proj, base, base_back, attn_gain, feed_gain, wq, wk, wv, wo, wg, wu, wd, cot, seq_count
+    x, ids, stu_gain, filter_proj, lag_proj, filters, attn_gain, feed_gain, wq, wk, wv, wo, wg, wu, wd, cot, seq_count
 ):
     streams, _, quarter, width = x.shape
     length = 4 * quarter
     hops = WINDOW // length
     spans = hops + 1
-    count, _, wide = base.shape
+    count, taps = filters.shape
+    wide = taps + 4 * LANES
     lag_order, channels = lag_proj.shape[:2]
     blocks = length // LANES
-    id_rows_each = length // LANES
     cols, units = wq.shape[1], wg.shape[1]
     heads = cols // HD
     tile = 2 * quarter
@@ -805,9 +826,10 @@
     zero_hops = ReduceScatter.scratch(0, streams, quarter, width)
 
     def kernel(
-        x_ref, id_ref, sg_ref, fp_ref, lp_ref, base_ref, back_ref, ag_ref, fg_ref,
-        wq_ref, wk_ref, wv_ref, wo_ref, wg_ref, wu_ref, wd_ref, cot_ref,
+        x_ref, id_ref, sg_ref, fp_hbm, lp_ref, taps_ref, ag_ref, fg_ref,
+        wq_ref, wk_ref, wv_ref, wo_ref, wg_hbm, wu_hbm, wd_hbm, cot_hbm,
         stu_out, layer_out, one_out, gain_out, sum_out, lag_out, ids_out, conv_out, strip_out,
+        fp_ref, wg_ref, wu_ref, wd_ref, cot_ref, load_sem, base_ref,
         rows_in, ids_in, cols_in, id_ext, lag_ext, part_ref, id_sem, strip_sem, conv_sem,
         attn_in, feed_in, grad_att, hid_one, hid_two, grad_two, grads, total, grad_acc,
         o_part, feed_part, layer_part, attn_part,
@@ -865,6 +887,11 @@
 
         far_back = range(1, seq_count)
 
+        pairs = ((fp_hbm, fp_ref), (wg_hbm, wg_ref), (wu_hbm, wu_ref), (wd_hbm, wd_ref), (cot_hbm, cot_ref))
+        loads = [pltpu.make_async_copy(a, b, load_sem.at[i]) for i, (a, b) in enumerate(pairs)]
+        for load in loads:
+            load.start()
+
         def front(strip, left, mask, conv):
             for m in range(streams):
                 rows_in[m, 0, t] = norm_of(x_ref[m, t].astype(F32), sg_ref[...]).astype(BF)
@@ -892,7 +919,8 @@
                 def _():
                     ids_in[h] = jnp.full(ids_in.shape[1:], -1, jnp.int32)
 
-            strips(back_ref, strip)
+            lay_taps(taps_ref, base_ref, True)
+            strips(base_ref, strip)
             strip_copy = pltpu.make_async_copy(strip, strip_out, strip_sem)
             strip_copy.start()
             for h in far_back:
@@ -900,19 +928,18 @@
             for h in far_back:
                 pl.when(s - h >= 0)(functools.partial(lambda h: id_copy(h, s - h).wait_recv(), h))
             for h in range(seq_count):
-                values = ids_in[h].astype(F32)
                 for m in range(streams):
-                    first = m * id_rows_each
-                    ids_out[h * streams + m : h * streams + m + 1] = jnp.concatenate(
-                        [values[first + r : first + r + 1] for r in range(id_rows_each)], axis=1
-                    )
+                    ids_out[h * streams + m : h * streams + m + 1] = ids_in[h, m].astype(F32)
             turned = jnp.transpose(ids_out[...])
             for m in range(streams):
                 cols_in[m] = turned[:, m : m + 1]
                 id_ext[m, :8] = turned[length - 8 :, streams + m : streams + m + 1]
                 id_ext[m, 8:] = turned[:, m : m + 1]
+            lay_taps(taps_ref, base_ref, False)
             strip_copy.wait()
             strips(base_ref, strip)
+            for load in loads:
+                load.wait()
             for h in far_back:
                 ag_rows.pass_on(h, 0)
             for h in far_back:
@@ -1059,7 +1086,6 @@
             second_norm(0)
             rs_two.middle(0, 1)
             ag_two.pass_on(0, 0)
-            second_norm(1)
             ag_two.finish(0, 0)
 
             @pl.loop(0, steps)
@@ -1077,9 +1103,15 @@
                 back = dot_nt(grad_gate, wg_ref[...]) + dot_nt(grad_up, wu_ref[...])
                 feed_part[0, m, half] = back.astype(BF).reshape(2, quarter, width)
                 layer_part[0, m, half] = dot_nn(inner, wd_ref[...]).astype(BF).reshape(2, quarter, width)
-                after(i, 0, lambda: ag_two.pass_on(0, 1))
-                after(i, 1, lambda: rs_three.start(0, 0), lambda: ag_two.finish(0, 1))
-                after(i, 2, lambda: rs_three.middle(0, 0))
+                after(i, 0, lambda: second_norm(1))
+                after(
+                    i,
+                    1,
+                    lambda: rs_three.start(0, 0),
+                    lambda: ag_two.pass_on(0, 1),
+                    lambda: rs_three.middle(0, 0),
+                    lambda: ag_two.finish(0, 1),
+                )
                 after(i, 3, lambda: rs_three.start(0, 1))
 
             def third_norm(m):
@@ -1096,13 +1128,12 @@
             grads[0] = dot_tn(feed_all, flat(gg_ref[...])).astype(BF)
             gr.start(0)
             rs_three.middle(0, 1)
-            ag_three.pass_on(0, 0)
             grads[1] = dot_tn(feed_all, flat(gu_ref[...])).astype(BF)
             gr.start(1)
-            third_norm(1)
-            ag_three.finish(0, 0)
             grads[2] = dot_tn(flat(cot_ref[...]), flat(inner_ref[...])).astype(BF)
             gr.start(2)
+            ag_three.pass_on(0, 0)
+            ag_three.finish(0, 0)
             for m in range(streams):
                 rs_layer.start(0, m)
 
@@ -1157,10 +1188,17 @@
                         attn_part[h, m] = back.astype(BF).reshape(2, 2, quarter, width)
                         rs_four.start(h, m)
 
-                after(i, 0, lambda: ag_three.pass_on(0, 1), lambda: rs_layer.middle(0, 0), lambda: rs_layer.middle(0, 1))
-                after(i, 1, lambda: ag_three.finish(0, 1), lambda: gr.spread(0), lambda: layer_sum(0), lambda: layer_sum(1))
+                after(i, 0, lambda: third_norm(1), lambda: rs_layer.middle(0, 0), lambda: rs_layer.middle(0, 1))
+                after(i, 1, lambda: gr.spread(0), lambda: ag_three.pass_on(0, 1), lambda: ag_three.finish(0, 1))
                 after(i, 2, *[functools.partial(rs_four.middle, h, 0) for h in range(hops, -1, -1)], lambda: gr.spread(1))
-                after(i, 3, *[functools.partial(rs_four.hop, h, 0, total) for h in range(hops, 0, -1)], lambda: gr.spread(2))
+                after(
+                    i,
+                    3,
+                    *[functools.partial(rs_four.hop, h, 0, total) for h in range(hops, 0, -1)],
+                    lambda: gr.spread(2),
+                    lambda: layer_sum(0),
+                    lambda: layer_sum(1),
+                )
 
             attn_all = attn_in[...].reshape(spans * streams * length, width)
             grads[3, :, cols : 3 * cols] = dot_tn(attn_all, flat(dkv_ref[...].reshape(-1, 2 * cols))).astype(BF)
@@ -1169,9 +1207,8 @@
             grads[3, :, :cols] = dot_tn(flat(attn_in[0]), flat(dq_ref[...])).astype(BF)
             grads[3, :, 3 * cols :] = dot_tn(flat(grad_att[0]), flat(a_ref[...])).astype(BF)
             gr.start(3)
-            for h in range(hops, 0, -1):
-                rs_four.hop(h, 1, total)
-            for m in range(streams):
+
+            def fourth_norm(m):
                 rs_four.total(m, total)
                 grad_in, gain_grad = norm_back(hid_one[m], ag_ref[...], total[...])
                 value = grad_two[m] + grad_in
@@ -1179,17 +1216,24 @@
                 gain_out[0:1] = gain_grad if m == 0 else gain_out[0:1] + gain_grad
                 stu_out[0, m, t] = value.astype(BF)
                 ag_five.start(m)
-                gr.collect(m, grad_acc)
-                ag_layer.pass_on(0, m)
+
+            fourth_norm(0)
+            for h in range(hops, 0, -1):
+                rs_four.hop(h, 1, total)
             gr.spread(3)
+            gr.collect(0, grad_acc)
+            fourth_norm(1)
             for m in range(streams):
                 ag_five.pass_on(0, m)
+            for m in range(streams):
+                ag_layer.pass_on(0, m)
+            gr.collect(1, grad_acc)
             gr.collect(2, grad_acc)
             for m in range(streams):
-                ag_layer.finish(0, m)
+                ag_five.finish(0, m)
             gr.collect(3, grad_acc)
             for m in range(streams):
-                ag_five.finish(0, m)
+                ag_layer.finish(0, m)
             for k in range(chunks):
                 gr.finish(k)
                 gr.drain(k)
@@ -1224,15 +1268,22 @@
             jax.ShapeDtypeStruct(gathered, BF),
             jax.ShapeDtypeStruct((streams, quarter, width), F32),
             jax.ShapeDtypeStruct((2, width), F32),
-            jax.ShapeDtypeStruct((chunks, rows, units), F32),
+            jax.ShapeDtypeStruct((chunks, rows, units), BF),
             jax.ShapeDtypeStruct((lag_order, streams, length, channels), BF),
             jax.ShapeDtypeStruct((seq_count * streams, length), F32),
             jax.ShapeDtypeStruct((count, streams * length, width), BF),
             jax.ShapeDtypeStruct((count, LANES, wide), BF),
         ),
-        in_specs=in_vmem(17),
+        in_specs=[anywhere if i in (3, 12, 13, 14, 15) else spec for i, spec in enumerate(in_vmem(16))],
         out_specs=tuple(in_vmem(7)) + (anywhere, anywhere),
         scratch_shapes=[
+            pltpu.VMEM(filter_proj.shape, BF),
+            pltpu.VMEM(wg.shape, BF),
+            pltpu.VMEM(wu.shape, BF),
+            pltpu.VMEM(wd.shape, BF),
+            pltpu.VMEM(cot.shape, BF),
+            pltpu.SemaphoreType.DMA((5,)),
+            pltpu.VMEM((count, wide), F32),
             pltpu.VMEM((streams, seq_count, 4, quarter, width), BF),
             pltpu.VMEM((seq_count,) + ids.shape, jnp.int32),
             pltpu.VMEM((streams, length, 1), F32),
@@ -1264,7 +1315,7 @@
         + GradReduce.scratch(seq_count, chunks, width, units),
         compiler_params=params(8),
     )(
-        x, ids, stu_gain, filter_proj, lag_proj, base, base_back, attn_gain, feed_gain, wq, wk, wv, wo, wg, wu, wd, cot
+        x, ids, stu_gain, filter_proj, lag_proj, filters, attn_gain, feed_gain, wq, wk, wv, wo, wg, wu, wd, cot
     )
 
 
@@ -1283,9 +1334,9 @@
     gain_rows = 8
 
     def kernel(
-        gs_ref, fp_hbm, lp_ref, conv_hbm, lag_ref, ext_ref, strip_hbm, x_ref, gain_ref, one_ref, gains_ref,
+        gs_ref, fp_hbm, lp_ref, conv_hbm, lag_ref, ext_ref, strip_hbm, x_hbm, gain_ref, one_ref, gains_ref,
         out, filter_out, lag_out, gain_out,
-        conv_ref, fp_ref, strip, conv_sem, fp_sem, strip_sem, id_ext,
+        conv_ref, fp_ref, strip, x_own, conv_sem, fp_sem, strip_sem, x_sem, id_ext,
         mask, cols, left, acc, terms, grad_conv, grads, lag_ext, total, grad_acc, gather_sem,
         gain_own, gain_near, gain_sum, gain_far, near_sem, far_sem, *scratch,
     ):
@@ -1304,6 +1355,8 @@
             conv_copy(k).start()
             fp_copy(k).start()
         strip_copy.start()
+        x_copy = pltpu.make_async_copy(x_hbm.at[:, t], x_own, x_sem)
+        x_copy.start()
         greet(seq_count, hops, wide=True, gains=True)
 
         def source(k):
@@ -1315,8 +1368,6 @@
         gr = GradReduce(seq_count, source, result, gr_scratch)
         rs = ReduceScatter(seq_count, hops, streams, lambda h, m: terms.at[h, m], rs_scratch)
         ag = AllGather(seq_count, 0, streams, out, gather_sem)
-
-        early = min(2, count)
 
         @pl.loop(0, count)
         def _(k):
@@ -1328,10 +1379,6 @@
             for m in range(streams):
                 here = pl.ds(pl.multiple_of(k * length, LANES), length)
                 grad_conv[m, here] = product[m * length : (m + 1) * length]
-
-            @pl.when(k >= count - early)
-            def _():
-                gr.spread(k - (count - early))
 
         grads[count] = jnp.zeros_like(grads.at[count])
         for i in range(lag_order):
@@ -1349,15 +1396,10 @@
                 same = id_ext[7 - i : 7 - i + length] == cols[m]
                 lag_ext[m, 7 - i : 7 - i + length] += jnp.where(same, term, 0.0)
         strip_copy.wait()
+        x_copy.wait()
         mine = pl.ds(pl.multiple_of(t * channels, LANES), channels)
-        spread_at = {}
-        collect_at = {}
-        for k in range(early, chunks):
-            if 2 * (k - early) < steps:
-                spread_at[2 * (k - early)] = k
-        for k in range(chunks):
-            if 2 * k + 3 < steps and k < early + len(spread_at):
-                collect_at[2 * k + 3] = k
+        spread_at = {0: 0, 1: 1, 4: 2, 6: 3} if steps == 8 and chunks >= 7 else {}
+        collect_at = {5: 0, 7: 1} if spread_at else {}
 
         def step_of(i):
             return seq_count - 1 - i // streams, i - i // streams * streams
@@ -1404,15 +1446,21 @@
                 pl.when(i == step)(functools.partial(gr.collect, k, grad_acc))
 
         rs.middle(0, streams - 1)
-        for k in range(early + len(spread_at), chunks):
-            gr.spread(k)
+        waiting = list(range(len(spread_at), chunks))
+        gathered = list(range(len(collect_at), chunks))
+
+        def next_spread():
+            if waiting:
+                gr.spread(waiting.pop(0))
+
         gain_own[...] = jnp.zeros_like(gain_own)
         for m in range(streams):
             rs.total(m, total)
-            grad_in, gain_grad = norm_back(x_ref[m, t].astype(F32), gain_ref[...], total[...])
+            grad_in, gain_grad = norm_back(x_own[m].astype(F32), gain_ref[...], total[...])
             out[0, m, t] = (one_ref[m] + grad_in).astype(BF)
             ag.start(m)
             gain_own[0:1] += gain_grad
+            next_spread()
         gain_own[1:3] = gains_ref[...]
         gain_near[t] = gain_own[...]
 
@@ -1420,13 +1468,13 @@
             return remote(gain_own, gain_near.at[slot], near_sem.at[0, j], near_sem.at[1, slot], {"tensor": j})
 
         for j in range(4):
-            pl.when(t != j)(lambda: near_copy(j, t).start())
+            pl.when(t != j)(functools.partial(lambda j: near_copy(j, t).start(), j))
+        while len(gathered) > 3 and chunks - len(gathered) < chunks - len(waiting):
+            gr.collect(gathered.pop(0), grad_acc)
         for m in range(streams):
             ag.pass_on(0, m)
-        for k in range(len(collect_at), chunks):
-            gr.collect(k, grad_acc)
         for j in range(4):
-            pl.when(t != j)(lambda: near_copy(j, j).wait_recv())
+            pl.when(t != j)(functools.partial(lambda j: near_copy(j, j).wait_recv(), j))
         gain_sum[...] = gain_near[0] + gain_near[1] + gain_near[2] + gain_near[3]
         me = p * seq_count + s
 
@@ -1440,13 +1488,17 @@
         gain_far[me] = gain_sum[:, pl.ds(pl.multiple_of(s * rows, LANES), rows)]
         for j in range(2 * seq_count):
             pl.when(me != j)(lambda: far_copy(j, me).start())
+        while waiting:
+            next_spread()
         for m in range(streams):
             ag.finish(0, m)
-        for k in range(chunks):
-            gr.finish(k)
+        while gathered:
+            gr.collect(gathered.pop(0), grad_acc)
         for j in range(2 * seq_count):
             pl.when(me != j)(lambda: far_copy(j, j).wait_recv())
         gain_out[...] = functools.reduce(jnp.add, [gain_far[j] for j in range(2 * seq_count)])
+        for k in range(chunks):
+            gr.finish(k)
         for j in range(4):
             pl.when(t != j)(lambda: near_copy(j, t).wait_send())
         for j in range(2 * seq_count):
@@ -1462,18 +1514,20 @@
         name="tail",
         out_shape=(
             jax.ShapeDtypeStruct((1, streams, 4, quarter, width), BF),
-            jax.ShapeDtypeStruct((count, rows, width), F32),
-            jax.ShapeDtypeStruct((rows, width), F32),
+            jax.ShapeDtypeStruct((count, rows, width), BF),
+            jax.ShapeDtypeStruct((rows, width), BF),
             jax.ShapeDtypeStruct((gain_rows, rows), F32),
         ),
-        in_specs=[anywhere if i in (1, 3, 6) else spec for i, spec in enumerate(in_vmem(11))],
+        in_specs=[anywhere if i in (1, 3, 6, 7) else spec for i, spec in enumerate(in_vmem(11))],
         out_specs=tuple(in_vmem(4)),
         scratch_shapes=[
             pltpu.VMEM(conv.shape, BF),
             pltpu.VMEM(filter_proj.shape, BF),
             pltpu.VMEM(strip_back.shape, BF),
+            pltpu.VMEM((streams, quarter, width), BF),
             pltpu.SemaphoreType.DMA((count,)),
             pltpu.SemaphoreType.DMA((count,)),
+            pltpu.SemaphoreType.DMA,
             pltpu.SemaphoreType.DMA,
             pltpu.VMEM((length + 8, 1), F32),
             pltpu.VMEM((length, length), BF),
@@ -1500,6 +1554,60 @@
     )(
         grad_stu, filter_proj, lag_proj, conv, lag_stack, ext_ids, strip_back, x, gain, grad_one, gains
     )
+
+
+def write_out(layer_output, input_gradient, gains, filter_grad, lag_grad, sums, lag_order, channels, cols):
+    _, streams, _, quarter, width = layer_output.shape
+    rows, units = sums.shape[1:]
+    count = filter_grad.shape[0]
+
+    def kernel(
+        layer_ref, input_ref, gains_ref, filter_ref, lag_ref, sums_ref,
+        layer_out, input_out, stu_out, filter_out, lag_out, attn_out, q_out, k_out, v_out, o_out, feed_out, gate_out, up_out,
+        down_out,
+    ):
+        layer_out[...] = layer_ref[0].reshape(streams, 1, 4 * quarter, width)
+        input_out[...] = input_ref[0].reshape(streams, 1, 4 * quarter, width)
+        filter_out[...] = filter_ref[...].astype(F32)
+        for i, ref in enumerate((stu_out, attn_out, feed_out)):
+            ref[...] = gains_ref[i : i + 1]
+        for i in range(lag_order):
+            lag_out[i] = jnp.transpose(lag_ref[:, i * channels : (i + 1) * channels].astype(F32))
+        for i, ref in enumerate((q_out, k_out, v_out)):
+            ref[...] = sums_ref[3, :, i * cols : (i + 1) * cols].astype(F32)
+        o_out[...] = jnp.transpose(sums_ref[3, :, 3 * cols :].astype(F32))
+        gate_out[...] = sums_ref[0].astype(F32)
+        up_out[...] = sums_ref[1].astype(F32)
+        down_out[...] = jnp.transpose(sums_ref[2].astype(F32))
+
+    def out(*shape, kind=F32):
+        return jax.ShapeDtypeStruct(shape, kind)
+
+    shapes = (
+        out(streams, 1, 4 * quarter, width, kind=BF),
+        out(streams, 1, 4 * quarter, width, kind=BF),
+        out(1, rows),
+        out(count, rows, width),
+        out(lag_order, channels, rows),
+        out(1, rows),
+        out(rows, cols),
+        out(rows, cols),
+        out(rows, cols),
+        out(cols, rows),
+        out(1, rows),
+        out(rows, units),
+        out(rows, units),
+        out(units, rows),
+    )
+    results = pl.pallas_call(
+        kernel,
+        name="write_out",
+        out_shape=shapes,
+        in_specs=in_vmem(6),
+        out_specs=tuple(in_vmem(len(shapes))),
+        compiler_params=params(),
+    )(layer_output, input_gradient, gains, filter_grad, lag_grad, sums)
+    return tuple(r.reshape(rows) if r.shape == (1, rows) else r for r in results)
 
 
 def gated_unit(gate_pre, up_pre):
@@ -1546,6 +1654,22 @@
     def row(gain):
         return gain.reshape(1, width)
 
+    if width // seq_count % LANES == 0:
+        rows = tokens.reshape(streams, 4, quarter, width)
+        grad_stu, layer_output, grad_one, gain_grads, sums, lag_stack, ext_ids, conv, strip_back = head(
+            rows, document_index, row(stu_gain), filter_proj, lag_proj, filters, row(attention_gain), row(feed_gain),
+            query_weight, key_weight, value_weight, output_weight, gate_weight, up_weight, down_weight,
+            cotangent.reshape(streams, length, width), seq_count,
+        )
+        input_gradient, filter_grad, lag_grad, gains = tail(
+            grad_stu.reshape(streams * length, width), filter_proj, lag_proj, conv,
+            lag_stack.reshape(lag_order, streams * length, channels), ext_ids, strip_back, rows, row(stu_gain), grad_one,
+            gain_grads, seq_count,
+        )
+        return write_out(
+            layer_output, input_gradient, gains, filter_grad, lag_grad, sums, lag_order, channels, query_weight.shape[1]
+        )
+
     x = tokens[:, 0]
     grad_three = cotangent[:, 0]
     ids = document_index[:, 0]
@@ -1585,20 +1709,6 @@
             gate_grad,
             up_grad,
             down_grad.T,
-        )
-
-    if width // seq_count % LANES == 0:
-        grad_stu, layer_output, grad_one, gain_grads, sums, lag_stack, ext_ids, conv, strip_back = head(
-            quarters(x), id_tile, row(stu_gain), filter_proj, lag_proj, base, base_back, row(attention_gain), row(feed_gain),
-            query_weight, key_weight, value_weight, output_weight, gate_weight, up_weight, down_weight, grad_three, seq_count,
-        )
-        input_gradient, filter_grad, lag_grad, gains = tail(
-            grad_stu.reshape(tokens_flat, width), filter_proj, lag_proj, conv,
-            lag_stack.reshape(lag_order, tokens_flat, channels), ext_ids, strip_back, quarters(x), row(stu_gain), grad_one,
-            gain_grads, seq_count,
-        )
-        return answer(
-            whole(layer_output)[0], whole(input_gradient)[0], gains, filter_grad, lag_grad, sums[3], (sums[0], sums[1], sums[2])
         )
 
     inputs = norm_of(x.astype(F32), stu_gain).astype(BF)

time: 269 us -> 254 us (0.944)
  local copies, waits for them, and re-layouts: 19.9 us -> 0 us
  Pallas kernels: 246 us -> 253 us
    unnamed x10 -> x0, local copies, waits for them, and re-layouts: 12.1 us -> none
    transpose x4 -> x0, local copies, waits for them, and re-layouts: 4.5 us -> none  [the longest x2 2.75 us: answer(): return (layer_output[:, None], input_gradient[:, None], gains[0], filter_...]
    pallas_call x0 -> x1, Pallas kernels: none -> 4.33 us  [write_out(): pl.pallas_call(kernel, name='write_out', out_shape=shapes, in_specs=in_vm...]
    pallas_call x1, Pallas kernels: 73.8 us -> 78.1 us  [tail(): pl.pallas_call(kernel, name='tail', out_shape=(jax.ShapeDtypeStruct((1, s...]
where the time goes in v6:
time: 254 us; the launch traced here: 253 us
  Pallas kernels  253 us (100%)
    pallas_call x1, Pallas kernels, head(): pl.pallas_call(kernel, name='head', out_shape=(jax.ShapeDtypeStruct(gathe...  170 us
    pallas_call x1, Pallas kernels, tail(): pl.pallas_call(kernel, name='tail', out_shape=(jax.ShapeDtypeStruct((1, s...  78.1 us

profile of v6, /device:TPU:0, one launch (start us, length us, event | category | flops | bytes accessed | tf_op | source)
XLA Modules:
  0.0 253.4 jit_solution(1477698384927655094)
XLA Ops:
  0.6 170.2 %head.1 = (bf16[1,2,4,128,512]{4,3,2,1,0:T(8,128)(2,1)}, bf16[1,2,4,128,512]{4,3,2,1,0:T(8,128)(2,1)}, f32[2,128,512]{2,1,0:T(8,128)}, f32[2,512]{1,0:T(2,128)},...) custom-call(bf16[2,4,128,512]{3,2,1,0:T(8,128)(2,1)} %bitcast.10, ...), custom_call_target="tpu_custom_call" | custom-call | tf_op jit(solution)/shard_map/head/pallas_call | solution.py:1263
  170.9 78.1 %tail.1 = (bf16[1,2,4,128,512]{4,3,2,1,0:T(8,128)(2,1)}, bf16[6,128,512]{2,1,0:T(8,128)(2,1)}, bf16[128,512]{1,0:T(8,128)(2,1)}, f32[8,128]{1,0:T(8,128)}) custom-call(bf16[1024,512]{1,0:T(8,128)(2,1)} %bitcast.13, bf16[6,512,512]{2,1,0:T(8,128)(2,1)} %fp_hbm.3, bf16[3,128,512]{2,1,0:T(8,128)(2,1)} %lp_ref.3, ...), custom_call_target="tpu_custom_call" | custom-call | tf_op jit(solution)/shard_map/tail/pallas_call | solution.py:1512
  249.0 4.3 %write_out.1 = (bf16[2,1,512,512]{3,2,1,0:T(8,128)(2,1)}, bf16[2,1,512,512]{3,2,1,0:T(8,128)(2,1)}, f32[1,128]{1,0:T(1,128)}, f32[6,128,512]{2,1,0:T(8,128)}, f3...) custom-call(bf16[1,2,4,128,512]{4,3,2,1,0:T(8,128)(2,1)} %get-tuple-, ...), custom_call_target="tpu_custom_call" | custom-call | tf_op jit(solution)/shard_map/write_out/pallas_call | solution.py:1602

commit v7 on v6

--- a/solution.py
+++ b/solution.py
@@ -78,44 +78,50 @@
     def __init__(self, seq_count, hops, streams, part, scratch):
         self.seq_count, self.hops, self.streams, self.part = seq_count, hops, streams, part
         self.near, self.half, self.over, self.hop_out, self.hop_in, self.sem = scratch
+        self.pieces, self.rows = self.half.shape[2:4]
 
     @staticmethod
-    def scratch(hops, streams, rows, width):
-        quarter = (hops + 1, streams, rows, width)
-        over_seq = quarter if hops else (1, 1, 16, LANES)
+    def scratch(hops, streams, rows, width, pieces=1):
+        quarter = (hops + 1, streams, pieces, rows // pieces, width)
+        over_seq = quarter if hops else (1, 1, 1, 16, LANES)
         return [
-            pltpu.VMEM((hops + 1, streams, 2, rows, width), BF),
+            pltpu.VMEM((hops + 1, streams, pieces, 2, rows // pieces, width), BF),
             pltpu.VMEM(quarter, BF),
             pltpu.VMEM(quarter, BF),
             pltpu.VMEM(over_seq, BF),
             pltpu.VMEM(over_seq, BF),
-            pltpu.SemaphoreType.DMA((6, hops + 1, streams)),
+            pltpu.SemaphoreType.DMA((6, hops + 1, streams, pieces)),
         ]
 
-    def to_core(self, h, m):
+    def span(self, n):
+        return slice(n * self.rows, (n + 1) * self.rows)
+
+    def move(self, kind, source, target, h, m, n, device, at=None):
+        at = h if at is None else at
+        return remote(source, target, self.sem.at[2 * kind, h, m, n], self.sem.at[2 * kind + 1, at, m, n], device)
+
+    def to_core(self, h, m, n):
         s, t, y, c, core, far = place()
-        return remote(
-            self.part(h, m).at[:, 1 - c], self.near.at[h, m], self.sem.at[0, h, m], self.sem.at[1, h, m], {"tensor": core}
-        )
-
-    def to_far(self, h, m):
-        s, t, y, c, core, far = place()
-        return remote(self.half.at[h, m], self.over.at[h, m], self.sem.at[2, h, m], self.sem.at[3, h, m], {"tensor": far})
-
-    def to_hop(self, h, m, peer):
-        return remote(
-            self.hop_out.at[h, m], self.hop_in.at[h - 1, m], self.sem.at[4, h, m], self.sem.at[5, h - 1, m], {"seq": peer}
-        )
+        source = self.part(h, m).at[:, 1 - c, pl.ds(n * self.rows, self.rows)]
+        return self.move(0, source, self.near.at[h, m, n], h, m, n, {"tensor": core})
+
+    def to_far(self, h, m, n):
+        far = place()[5]
+        return self.move(1, self.half.at[h, m, n], self.over.at[h, m, n], h, m, n, {"tensor": far})
+
+    def to_hop(self, h, m, n):
+        peer = {"seq": lax.axis_index("seq") - 1}
+        return self.move(2, self.hop_out.at[h, m, n], self.hop_in.at[h - 1, m, n], h, m, n, peer, at=h - 1)
 
     def add_hop(self, h, m, acc):
         s = lax.axis_index("seq")
 
         @pl.when(s + 1 < self.seq_count)
         def _():
-            remote(
-                self.hop_out.at[h, m], self.hop_in.at[h, m], self.sem.at[4, h, m], self.sem.at[5, h, m], {"seq": s + 1}
-            ).wait_recv()
-            acc[...] += self.hop_in[h, m].astype(F32)
+            for n in range(self.pieces):
+                ref = self.hop_in.at[h, m, n]
+                self.move(2, self.hop_out.at[h, m, n], ref, h, m, n, {"seq": s + 1}).wait_recv()
+                acc[self.span(n)] += self.hop_in[h, m, n].astype(F32)
 
     def there(self, h):
         return True if isinstance(h, int) and h == 0 else lax.axis_index("seq") - h >= 0
@@ -124,41 +130,47 @@
         return [(h, m) for h in range(self.hops, -1, -1) for m in range(self.streams)]
 
     def start(self, h, m):
-        when(self.there(h), lambda: self.to_core(h, m).start())
+        def act():
+            for n in range(self.pieces):
+                self.to_core(h, m, n).start()
+
+        when(self.there(h), act)
 
     def middle(self, h, m):
         s, t, y, c, core, far = place()
 
         def act():
-            self.to_core(h, m).wait_recv()
-            mine = self.part(h, m)[1 - y, c].astype(F32) + self.near[h, m, 1 - y].astype(F32)
-            self.half[h, m] = mine.astype(BF)
-            self.to_far(h, m).start()
+            for n in range(self.pieces):
+                self.to_core(h, m, n).wait_recv()
+                mine = self.part(h, m)[1 - y, c, self.span(n)].astype(F32) + self.near[h, m, n, 1 - y].astype(F32)
+                self.half[h, m, n] = mine.astype(BF)
+                self.to_far(h, m, n).start()
 
         when(self.there(h), act)
 
-    def own(self, h, m):
+    def own(self, h, m, acc):
         s, t, y, c, core, far = place()
-        self.to_far(h, m).wait_recv()
-        return (
-            self.part(h, m)[y, c].astype(F32) + self.near[h, m, y].astype(F32) + self.over[h, m].astype(F32)
-        )
+        for n in range(self.pieces):
+            self.to_far(h, m, n).wait_recv()
+            mine = self.part(h, m)[y, c, self.span(n)].astype(F32) + self.near[h, m, n, y].astype(F32)
+            acc[self.span(n)] = mine + self.over[h, m, n].astype(F32)
 
     def hop(self, h, m, acc):
         def act():
-            acc[...] = self.own(h, m)
+            self.own(h, m, acc)
             if isinstance(h, int):
                 if h < self.hops:
                     self.add_hop(h, m, acc)
             else:
                 pl.when(h < self.hops)(lambda: self.add_hop(h, m, acc))
-            self.hop_out[h, m] = acc[...].astype(BF)
-            self.to_hop(h, m, lax.axis_index("seq") - 1).start()
+            for n in range(self.pieces):
+                self.hop_out[h, m, n] = acc[self.span(n)].astype(BF)
+                self.to_hop(h, m, n).start()
 
         when(self.there(h), act)
 
     def total(self, m, acc):
-        acc[...] = self.own(0, m)
+        self.own(0, m, acc)
         if self.hops:
             self.add_hop(0, m, acc)
 
@@ -166,10 +178,11 @@
         for h, m in self.order():
 
             def act():
-                self.to_core(h, m).wait_send()
-                self.to_far(h, m).wait_send()
-                if h:
-                    self.to_hop(h, m, lax.axis_index("seq") - 1).wait_send()
+                for n in range(self.pieces):
+                    self.to_core(h, m, n).wait_send()
+                    self.to_far(h, m, n).wait_send()
+                    if h:
+                        self.to_hop(h, m, n).wait_send()
 
             when(self.there(h), act)
 
@@ -178,56 +191,68 @@
     def __init__(self, seq_count, hops, streams, at, sem, first=0):
         self.seq_count, self.hops, self.streams, self.sem, self.first = seq_count, hops, streams, sem, first
         self.at = at if callable(at) else lambda h, m, quarter: at.at[h, m, quarter]
+        self.pieces = sem.shape[3]
 
     @staticmethod
-    def scratch(hops, streams):
-        return [pltpu.SemaphoreType.DMA((8, hops + 1, streams))]
+    def scratch(hops, streams, pieces=1):
+        return [pltpu.SemaphoreType.DMA((8, hops + 1, streams, pieces))]
 
     def there(self, h):
         return True if h == 0 else lax.axis_index("seq") - h >= 0
 
-    def copy(self, kind, h, m, quarter, device):
+    def piece(self, h, m, quarter, n):
         ref = self.at(h, m, quarter)
-        return remote(ref, ref, self.sem.at[2 * kind, h, m], self.sem.at[2 * kind + 1, h, m], device)
-
-    def relay(self, h, m):
+        rows = ref.shape[0] // self.pieces
+        return ref.at[pl.ds(n * rows, rows)]
+
+    def copy(self, kind, h, m, quarter, n, device):
+        ref = self.piece(h, m, quarter, n)
+        return remote(ref, ref, self.sem.at[2 * kind, h, m, n], self.sem.at[2 * kind + 1, h, m, n], device)
+
+    def relay(self, h, m, n):
         s, t = lax.axis_index("seq"), place()[1]
         return remote(
-            self.at(h, m, t), self.at(h + 1, m, t), self.sem.at[0, h, m], self.sem.at[1, h + 1, m], {"seq": s + 1}
+            self.piece(h, m, t, n),
+            self.piece(h + 1, m, t, n),
+            self.sem.at[0, h, m, n],
+            self.sem.at[1, h + 1, m, n],
+            {"seq": s + 1},
         )
 
     def relays(self, h):
         s = lax.axis_index("seq")
         return (s - h >= 0) & (s + 1 < self.seq_count)
 
-    def forward(self, h, m):
+    def forward(self, h, m, n):
         if h < self.hops:
-            pl.when(self.relays(h))(lambda: self.relay(h, m).start())
-
-    def spread(self, h, m):
+            pl.when(self.relays(h))(lambda: self.relay(h, m, n).start())
+
+    def spread(self, h, m, n):
         s, t, y, c, core, far = place()
-        self.copy(1, h, m, t, {"tensor": far}).start()
-        self.copy(2, h, m, t, {"tensor": core}).start()
+        self.copy(1, h, m, t, n, {"tensor": far}).start()
+        self.copy(2, h, m, t, n, {"tensor": core}).start()
 
     def start(self, m):
-        self.forward(0, m)
-        if self.first == 0:
-            self.spread(0, m)
+        for n in range(self.pieces):
+            self.forward(0, m, n)
+            if self.first == 0:
+                self.spread(0, m, n)
 
     def arrive(self, h, m):
         @pl.when(self.there(h))
         def _():
-            self.copy(0, h, m, place()[1], {"seq": lax.axis_index("seq") - 1}).wait_recv()
-
-        self.forward(h, m)
-        pl.when(self.there(h))(lambda: self.spread(h, m))
+            for n in range(self.pieces):
+                self.copy(0, h, m, place()[1], n, {"seq": lax.axis_index("seq") - 1}).wait_recv()
+                self.forward(h, m, n)
+                self.spread(h, m, n)
 
     def pass_on(self, h, m):
         s, t, y, c, core, far = place()
 
         def act():
-            self.copy(1, h, m, far, {"tensor": far}).wait_recv()
-            self.copy(3, h, m, far, {"tensor": core}).start()
+            for n in range(self.pieces):
+                self.copy(1, h, m, far, n, {"tensor": far}).wait_recv()
+                self.copy(3, h, m, far, n, {"tensor": core}).start()
 
         when(self.there(h), act)
 
@@ -235,8 +260,9 @@
         s, t, y, c, core, far = place()
 
         def act():
-            self.copy(2, h, m, core, {"tensor": core}).wait_recv()
-            self.copy(3, h, m, 3 - t, {"tensor": core}).wait_recv()
+            for n in range(self.pieces):
+                self.copy(2, h, m, core, n, {"tensor": core}).wait_recv()
+                self.copy(3, h, m, 3 - t, n, {"tensor": core}).wait_recv()
 
         when(self.there(h), act)
 
@@ -250,16 +276,17 @@
     def drain(self):
         s, t, y, c, core, far = place()
         for m in range(self.streams):
-            for h in range(self.hops):
-                pl.when(self.relays(h))(functools.partial(lambda h, m: self.relay(h, m).wait_send(), h, m))
-            for h in range(self.first, self.hops + 1):
-
-                def act():
-                    self.copy(1, h, m, t, {"tensor": far}).wait_send()
-                    self.copy(2, h, m, t, {"tensor": core}).wait_send()
-                    self.copy(3, h, m, far, {"tensor": core}).wait_send()
-
-                when(self.there(h), act)
+            for n in range(self.pieces):
+                for h in range(self.hops):
+                    pl.when(self.relays(h))(functools.partial(lambda h, m, n: self.relay(h, m, n).wait_send(), h, m, n))
+                for h in range(self.first, self.hops + 1):
+
+                    def act():
+                        self.copy(1, h, m, t, n, {"tensor": far}).wait_send()
+                        self.copy(2, h, m, t, n, {"tensor": core}).wait_send()
+                        self.copy(3, h, m, far, n, {"tensor": core}).wait_send()
+
+                    when(self.there(h), act)
 
 
 class GradReduce:
@@ -809,6 +836,10 @@
     wide = taps + 4 * LANES
     lag_order, channels = lag_proj.shape[:2]
     blocks = length // LANES
+    reach = taps * 5 // 8
+    window = reach + 2 * quarter
+    own = 4 * (seq_count - 1)
+    assert reach % (2 * quarter) == 0 and window <= taps
     cols, units = wq.shape[1], wg.shape[1]
     heads = cols // HD
     tile = 2 * quarter
@@ -823,13 +854,14 @@
     state = pltpu.VMEM((streams, quarter, width), F32)
     gathered = (1, streams, 4, quarter, width)
     split_part = pltpu.VMEM((1, streams, 2, 2, quarter, width), BF)
-    zero_hops = ReduceScatter.scratch(0, streams, quarter, width)
+    pieces = 2
+    zero_hops = ReduceScatter.scratch(0, streams, quarter, width, pieces)
 
     def kernel(
         x_ref, id_ref, sg_ref, fp_hbm, lp_ref, taps_ref, ag_ref, fg_ref,
         wq_ref, wk_ref, wv_ref, wo_ref, wg_hbm, wu_hbm, wd_hbm, cot_hbm,
         stu_out, layer_out, one_out, gain_out, sum_out, lag_out, ids_out, conv_out, strip_out,
-        fp_ref, wg_ref, wu_ref, wd_ref, cot_ref, load_sem, base_ref,
+        fp_ref, wg_ref, wu_ref, wd_ref, cot_ref, load_sem, base_ref, ids_row,
         rows_in, ids_in, cols_in, id_ext, lag_ext, part_ref, id_sem, strip_sem, conv_sem,
         attn_in, feed_in, grad_att, hid_one, hid_two, grad_two, grads, total, grad_acc,
         o_part, feed_part, layer_part, attn_part,
@@ -850,7 +882,12 @@
         rs_four = reducer(attn_part, hops)
         gr = GradReduce(seq_count, lambda k: grads.at[k], lambda k: sum_out.at[k], take(8))
         ag_rows = AllGather(
-            seq_count, seq_count - 1, streams, lambda h, m, q: rows_in.at[m, h, q], sem_rows, first=1
+            seq_count,
+            seq_count - 1,
+            streams,
+            lambda h, m, q: rows_in.at[m, 4 * (seq_count - 1 - h) + q],
+            sem_rows,
+            first=1,
         )
         ag_one = AllGather(seq_count, hops, streams, attn_in, sem_one)
         ag_two = AllGather(seq_count, 0, streams, feed_in, sem_two)
@@ -894,7 +931,7 @@
 
         def front(strip, left, mask, conv):
             for m in range(streams):
-                rows_in[m, 0, t] = norm_of(x_ref[m, t].astype(F32), sg_ref[...]).astype(BF)
+                rows_in[m, own + t] = norm_of(x_ref[m, t].astype(F32), sg_ref[...]).astype(BF)
             greet(seq_count, 0, wide=True)
             for m in range(streams):
                 ag_rows.start(m)
@@ -905,7 +942,7 @@
 
                     @pl.when(t != q)
                     def _():
-                        rows_in[m, 0, q] = norm_of(x_ref[m, q].astype(F32), sg_ref[...]).astype(BF)
+                        rows_in[m, own + q] = norm_of(x_ref[m, q].astype(F32), sg_ref[...]).astype(BF)
 
             for m in range(streams):
                 for h in far_back:
@@ -923,13 +960,15 @@
             strips(base_ref, strip)
             strip_copy = pltpu.make_async_copy(strip, strip_out, strip_sem)
             strip_copy.start()
-            for h in far_back:
-                ag_rows.arrive(h, 0)
+            ag_rows.arrive(1, 0)
+            ag_rows.arrive(2, 0)
             for h in far_back:
                 pl.when(s - h >= 0)(functools.partial(lambda h: id_copy(h, s - h).wait_recv(), h))
             for h in range(seq_count):
                 for m in range(streams):
                     ids_out[h * streams + m : h * streams + m + 1] = ids_in[h, m].astype(F32)
+                    start = (seq_count - 1 - h) * length
+                    ids_row[m : m + 1, start : start + length] = ids_in[h, m].astype(F32)
             turned = jnp.transpose(ids_out[...])
             for m in range(streams):
                 cols_in[m] = turned[:, m : m + 1]
@@ -940,93 +979,99 @@
             strips(base_ref, strip)
             for load in loads:
                 load.wait()
-            for h in far_back:
-                ag_rows.pass_on(h, 0)
-            for h in far_back:
-                ag_rows.arrive(h, 1)
-            for h in far_back:
-                ag_rows.finish(h, 0)
+            ag_rows.pass_on(1, 0)
+            ag_rows.arrive(3, 0)
+            ag_rows.pass_on(2, 0)
+            ag_rows.finish(1, 0)
+            ag_rows.finish(2, 0)
             mine = pl.ds(pl.multiple_of(t * channels, LANES), channels)
 
             def lags(m):
-                own = rows_in[m, 0, :, :, mine].reshape(length, channels)
-                lag_ext[:8] = rows_in[m, 1, 3, quarter - 8 :, mine].astype(F32)
-                lag_ext[8:] = own.astype(F32)
+                lag_ext[:8] = rows_in[m, own - 1, quarter - 8 :, mine].astype(F32)
+                lag_ext[8:] = rows_in[m, own : own + 4, :, mine].reshape(length, channels).astype(F32)
                 for i in range(lag_order):
                     same = id_ext[m, 7 - i : 7 - i + length] == cols_in[m]
                     lag_out[i, m] = jnp.where(same, lag_ext[7 - i : 7 - i + length], 0.0).astype(BF)
 
-            def conv_copy(k, m):
+            def conv_copy(k, m, half):
+                first = pl.multiple_of(half * tile, tile)
                 return pltpu.make_async_copy(
-                    conv.at[k], conv_out.at[k, pl.ds(pl.multiple_of(m * length, LANES), length)], conv_sem.at[k]
+                    conv.at[k, pl.ds(first, tile)],
+                    conv_out.at[k, pl.ds(pl.multiple_of(m * length + first, tile), tile)],
+                    conv_sem.at[k, half],
                 )
 
             lags(0)
-
-            @pl.loop(0, streams * count)
+            per = 2 * count
+
+            @pl.loop(0, streams * per)
             def _(j):
-                m = j // count
-                k = j - m * count
+                m = j // per
+                half = 1 - (j - m * per) // count
+                k = j - m * per - (1 - half) * count
+                first = pl.multiple_of(half * tile, tile)
+                here = pl.ds(first, tile)
+                offset = taps - length - reach
 
                 @pl.when(k == 0)
                 def _():
-                    for h in range(seq_count):
-                        mask[:, h * length : (h + 1) * length] = jnp.where(
-                            cols_in[m] == ids_out[pl.ds(h * streams + m, 1)], 1.0, 0.0
-                        ).astype(BF)
-
-                for a in range(blocks):
-                    for h in range(seq_count):
-                        start = LANES * (blocks * (seq_count - h) - 1 - a)
-                        down, across = slice(a * LANES, (a + 1) * LANES), slice(h * length, (h + 1) * length)
-                        left[down, across] = strip[k, :, start : start + length] * mask[down, across]
-                result = dot_nn(left[...], rows_in[m].reshape(seq_count * length, width)).astype(BF)
-                pl.when(m > 0)(lambda: conv_copy(k, m - 1).wait())
-                conv[k] = result
-                conv_copy(k, m).start()
+                    ids_there = ids_row[pl.ds(m, 1), pl.ds(pl.multiple_of(offset + first, tile), window)]
+                    mask[...] = jnp.where(cols_in[m, here] == ids_there, 1.0, 0.0).astype(BF)
+
+                for a in range(2 * quarter // LANES):
+                    start = taps - LANES - reach - a * LANES
+                    down = slice(a * LANES, (a + 1) * LANES)
+                    left[down] = strip[k, :, start : start + window] * mask[down]
+                right = rows_in[m, pl.ds(offset // quarter + 2 * half, window // quarter)].reshape(window, width)
+                result = dot_nn(left[...], right).astype(BF)
+                pl.when(m > 0)(lambda: conv_copy(k, m - 1, half).wait())
+                conv[k, here] = result
+                conv_copy(k, m, half).start()
 
                 @pl.when(k == count - 1)
                 def _():
-                    @pl.loop(0, 2)
-                    def _(half):
-                        here = pl.ds(pl.multiple_of(half * tile, tile), tile)
-                        mixed = sum([dot_nn(conv[q, here], fp_ref[q]) for q in range(count)])
-                        mixed = mixed + sum([dot_nn(lag_out[i, m, here], lp_ref[i]) for i in range(lag_order)])
-                        part_ref[0, m, half] = mixed.astype(BF).reshape(2, quarter, width)
-
-                after(j, 1, *[functools.partial(ag_rows.pass_on, h, 1) for h in far_back])
+                    mixed = sum([dot_nn(conv[q, here], fp_ref[q]) for q in range(count)])
+                    mixed = mixed + sum([dot_nn(lag_out[i, m, here], lp_ref[i]) for i in range(lag_order)])
+                    part_ref[0, m, half] = mixed.astype(BF).reshape(2, quarter, width)
+
+                after(j, 0, lambda: ag_rows.arrive(1, 1))
+                after(j, 1, lambda: ag_rows.pass_on(3, 0), lambda: ag_rows.arrive(2, 1))
+                after(j, 3, lambda: ag_rows.arrive(3, 1), lambda: ag_rows.pass_on(1, 1))
+                after(j, count - 1, lambda: ag_rows.finish(3, 0), lambda: ag_rows.pass_on(2, 1))
+                after(j, count + 1, lambda: ag_rows.pass_on(3, 1))
                 after(
                     j,
-                    count - 1,
+                    per - 1,
                     lambda: rs_one.start(0, 0),
                     *[functools.partial(ag_rows.finish, h, 1) for h in far_back],
                     lambda: lags(1),
                 )
-                after(j, count, lambda: rs_one.middle(0, 0))
-                after(j, count + 2, lambda: first_norm(0))
-                after(j, count + 4, lambda: ag_one.pass_on(0, 0), lambda: ag_one.arrive(1, 0) if hops > 0 else None)
+                after(j, per + 1, lambda: rs_one.middle(0, 0))
+                after(j, per + 8, lambda: first_norm(0))
 
             rs_one.start(0, 1)
             for k in range(count):
-                conv_copy(k, streams - 1).wait()
+                for half in range(2):
+                    conv_copy(k, streams - 1, half).wait()
 
         pl.run_scoped(
             front,
             pltpu.VMEM((count, LANES, wide), BF),
-            pltpu.VMEM((length, seq_count * length), BF),
-            pltpu.VMEM((length, seq_count * length), BF),
+            pltpu.VMEM((tile, window), BF),
+            pltpu.VMEM((tile, window), BF),
             pltpu.VMEM((count, length, width), BF),
         )
 
         def attention_on(
             q_ref, k_ref, v_ref, a_ref, lse_ref, inner_ref, gg_ref, gu_ref, ga_ref, dk_acc, dv_acc, dq_ref, dkv_ref
         ):
+            ag_one.pass_on(0, 0)
             rs_one.middle(0, 1)
-            for h in range(2, spans):
+            for h in range(1, spans):
                 ag_one.arrive(h, 0)
+            first_norm(1)
             for h in range(1, spans):
                 ag_one.pass_on(h, 0)
-            first_norm(1)
             for h in range(spans):
                 ag_one.finish(h, 0)
 
@@ -1284,7 +1329,8 @@
             pltpu.VMEM(cot.shape, BF),
             pltpu.SemaphoreType.DMA((5,)),
             pltpu.VMEM((count, wide), F32),
-            pltpu.VMEM((streams, seq_count, 4, quarter, width), BF),
+            pltpu.VMEM((streams, taps), F32),
+            pltpu.VMEM((streams, 4 * seq_count, quarter, width), BF),
             pltpu.VMEM((seq_count,) + ids.shape, jnp.int32),
             pltpu.VMEM((streams, length, 1), F32),
             pltpu.VMEM((streams, length + 8, 1), F32),
@@ -1292,7 +1338,7 @@
             split_part,
             pltpu.SemaphoreType.DMA((2, seq_count)),
             pltpu.SemaphoreType.DMA,
-            pltpu.SemaphoreType.DMA((count,)),
+            pltpu.SemaphoreType.DMA((count, 2)),
             pltpu.VMEM((spans, streams, 4, quarter, width), BF),
             pltpu.VMEM(gathered, BF),
             pltpu.VMEM(gathered, BF),
@@ -1306,12 +1352,12 @@
             split_part,
             split_part,
             pltpu.VMEM((spans, streams, 2, 2, quarter, width), BF),
-            AllGather.scratch(seq_count - 1, streams)[0],
-            AllGather.scratch(hops, streams)[0],
+            AllGather.scratch(seq_count - 1, streams, pieces)[0],
+            AllGather.scratch(hops, streams, pieces)[0],
         ]
-        + [AllGather.scratch(0, streams)[0]] * 4
+        + [AllGather.scratch(0, streams, pieces)[0]] * 4
         + zero_hops * 4
-        + ReduceScatter.scratch(hops, streams, quarter, width)
+        + ReduceScatter.scratch(hops, streams, quarter, width, pieces)
         + GradReduce.scratch(seq_count, chunks, width, units),
         compiler_params=params(8),
     )(
@@ -1453,6 +1499,8 @@
             if waiting:
                 gr.spread(waiting.pop(0))
 
+        next_spread()
+        next_spread()
         gain_own[...] = jnp.zeros_like(gain_own)
         for m in range(streams):
             rs.total(m, total)
@@ -1460,7 +1508,7 @@
             out[0, m, t] = (one_ref[m] + grad_in).astype(BF)
             ag.start(m)
             gain_own[0:1] += gain_grad
-            next_spread()
+        next_spread()
         gain_own[1:3] = gains_ref[...]
         gain_near[t] = gain_own[...]
 

time: 254 us -> 253 us (level)
  no operation moved by 1% of the time
where the time goes in v7:
time: 253 us
  Pallas kernels  252 us (100%)
    pallas_call x1, Pallas kernels, head(): pl.pallas_call(kernel, name='head', out_shape=(jax.ShapeDtypeStruct(gathe...  172 us
    pallas_call x1, Pallas kernels, tail(): pl.pallas_call(kernel, name='tail', out_shape=(jax.ShapeDtypeStruct((1, s...  76.2 us

profile of v7, /device:TPU:0, one launch (start us, length us, event | category | flops | bytes accessed | tf_op | source)
XLA Modules:
  0.0 253.1 jit_solution(10005447123885671043)
XLA Ops:
  0.6 171.8 %head.1 = (bf16[1,2,4,128,512]{4,3,2,1,0:T(8,128)(2,1)}, bf16[1,2,4,128,512]{4,3,2,1,0:T(8,128)(2,1)}, f32[2,128,512]{2,1,0:T(8,128)}, f32[2,512]{1,0:T(2,128)},...) custom-call(bf16[2,4,128,512]{3,2,1,0:T(8,128)(2,1)} %bitcast.10, ...), custom_call_target="tpu_custom_call" | custom-call | tf_op jit(solution)/shard_map/head/pallas_call | solution.py:1308
  172.5 76.2 %tail.1 = (bf16[1,2,4,128,512]{4,3,2,1,0:T(8,128)(2,1)}, bf16[6,128,512]{2,1,0:T(8,128)(2,1)}, bf16[128,512]{1,0:T(8,128)(2,1)}, f32[8,128]{1,0:T(8,128)}) custom-call(bf16[1024,512]{1,0:T(8,128)(2,1)} %bitcast.13, bf16[6,512,512]{2,1,0:T(8,128)(2,1)} %fp_hbm.3, bf16[3,128,512]{2,1,0:T(8,128)(2,1)} %lp_ref.3, ...), custom_call_target="tpu_custom_call" | custom-call | tf_op jit(solution)/shard_map/tail/pallas_call | solution.py:1560
  248.6 4.3 %write_out.1 = (bf16[2,1,512,512]{3,2,1,0:T(8,128)(2,1)}, bf16[2,1,512,512]{3,2,1,0:T(8,128)(2,1)}, f32[1,128]{1,0:T(1,128)}, f32[6,128,512]{2,1,0:T(8,128)}, f3...) custom-call(bf16[1,2,4,128,512]{4,3,2,1,0:T(8,128)(2,1)} %get-tuple-, ...), custom_call_target="tpu_custom_call" | custom-call | tf_op jit(solution)/shard_map/write_out/pallas_call | solution.py:1650

commit v8 on v7

--- a/solution.py
+++ b/solution.py
@@ -302,11 +302,11 @@
         return [
             pltpu.VMEM((chunks, depth, half), BF),
             pltpu.VMEM((chunks, depth, half), BF),
-            pltpu.VMEM((chunks, seq_count, rows, half), BF),
+            pltpu.VMEM((chunks, seq_count + 1, rows, half), BF),
             pltpu.VMEM((chunks, rows, half), BF),
             pltpu.VMEM((chunks, rows, half), BF),
             pltpu.SemaphoreType.DMA((2, chunks)),
-            pltpu.SemaphoreType.DMA((2, chunks, seq_count)),
+            pltpu.SemaphoreType.DMA((2, chunks, seq_count + 1)),
             pltpu.SemaphoreType.DMA((2, chunks)),
         ]
 
@@ -322,10 +322,15 @@
             self.source(c).at[:, self.columns(1 - p)], self.x_in.at[c], self.x_sem.at[0, c], self.x_sem.at[1, c], {"dp": 1 - p}
         )
 
-    def row_copy(self, c, j, slot):
-        return remote(
-            self.z_out.at[c, self.block(j)], self.z_in.at[c, slot], self.z_sem.at[0, c, j], self.z_sem.at[1, c, slot], {"seq": j}
-        )
+    def row_copy(self, c, s, j):
+        peer = s + 1 if j > s else s - 1
+        slot = self.seq_count if j == peer and j < s else j
+        rows = self.z_out.at[c, j * self.rows : (j + 1) * self.rows]
+        return remote(rows, self.z_in.at[c, slot], self.z_sem.at[0, c, j], self.z_sem.at[1, c, slot], {"seq": peer})
+
+    def arrival(self, c, slot, peer):
+        ref = self.z_in.at[c, slot]
+        return remote(ref, ref, self.z_sem.at[0, c, slot], self.z_sem.at[1, c, slot], {"seq": peer})
 
     def back(self, c):
         p = lax.axis_index("dp")
@@ -333,30 +338,50 @@
             self.back_out.at[c], self.back_in.at[c], self.back_sem.at[0, c], self.back_sem.at[1, c], {"dp": 1 - p}
         )
 
-    def others(self, action):
-        for j in range(self.seq_count):
-            pl.when(lax.axis_index("seq") != j)(functools.partial(action, j))
-
     def start(self, c):
         self.over(c).start()
 
     def spread(self, c):
-        s, p = lax.axis_index("seq"), lax.axis_index("dp")
+        p = lax.axis_index("dp")
         self.over(c).wait_recv()
         mine = self.source(c)[:, self.columns(p)].astype(F32) + self.x_in[c].astype(F32)
         self.z_out[c] = mine.astype(BF)
-        self.others(lambda j: self.row_copy(c, j, s).start())
+        last = self.seq_count - 1
+        for s in {0, last}:
+
+            @pl.when(lax.axis_index("seq") == s)
+            def _():
+                for j in range(self.seq_count):
+                    if j != s:
+                        self.row_copy(c, s, j).start()
+
+    def relay(self, c, d):
+        for right in (True, False):
+            s = d if right else self.seq_count - 1 - d
+            targets = range(s + 1, self.seq_count) if right else range(s)
+
+            @pl.when(lax.axis_index("seq") == s)
+            def _():
+                for j in targets:
+                    self.arrival(c, j, s - 1 if right else s + 1).wait_recv()
+                    rows = slice(j * self.rows, (j + 1) * self.rows)
+                    added = self.z_out[c, rows].astype(F32) + self.z_in[c, j].astype(F32)
+                    self.z_out[c, rows] = added.astype(BF)
+                    self.row_copy(c, s, j).start()
 
     def collect(self, c, acc):
         s, p = lax.axis_index("seq"), lax.axis_index("dp")
         here = self.block(s)
         acc[...] = self.source(c)[here, self.columns(p)].astype(F32) + self.x_in[c, here].astype(F32)
-
-        def add(j):
-            self.row_copy(c, j, j).wait_recv()
-            acc[...] += self.z_in[c, j].astype(F32)
-
-        self.others(add)
+        for n in range(self.seq_count):
+
+            @pl.when(s == n)
+            def _():
+                for there, slot, peer in ((n > 0, n, n - 1), (n + 1 < self.seq_count, self.seq_count, n + 1)):
+                    if there:
+                        self.arrival(c, slot, peer).wait_recv()
+                        acc[...] += self.z_in[c, slot].astype(F32)
+
         self.back_out[c] = acc[...].astype(BF)
         self.back(c).start()
 
@@ -368,7 +393,14 @@
 
     def drain(self, c):
         self.over(c).wait_send()
-        self.others(lambda j: self.row_copy(c, j, lax.axis_index("seq")).wait_send())
+        for s in range(self.seq_count):
+
+            @pl.when(lax.axis_index("seq") == s)
+            def _():
+                for j in range(self.seq_count):
+                    if j != s:
+                        self.row_copy(c, s, j).wait_send()
+
         self.back(c).wait_send()
 
 
@@ -1047,7 +1079,7 @@
                     lambda: lags(1),
                 )
                 after(j, per + 1, lambda: rs_one.middle(0, 0))
-                after(j, per + 8, lambda: first_norm(0))
+                after(j, per + 6, lambda: first_norm(0))
 
             rs_one.start(0, 1)
             for k in range(count):
@@ -1130,6 +1162,10 @@
 
             second_norm(0)
             rs_two.middle(0, 1)
+            rs_one.drain()
+            ag_rows.drain()
+            for h in far_back:
+                pl.when(s + h < seq_count)(functools.partial(lambda h: id_copy(h, s + h).wait_send(), h))
             ag_two.pass_on(0, 0)
             ag_two.finish(0, 0)
 
@@ -1177,6 +1213,8 @@
             gr.start(1)
             grads[2] = dot_tn(flat(cot_ref[...]), flat(inner_ref[...])).astype(BF)
             gr.start(2)
+            rs_two.drain()
+            ag_one.drain()
             ag_three.pass_on(0, 0)
             ag_three.finish(0, 0)
             for m in range(streams):
@@ -1235,20 +1273,26 @@
 
                 after(i, 0, lambda: third_norm(1), lambda: rs_layer.middle(0, 0), lambda: rs_layer.middle(0, 1))
                 after(i, 1, lambda: gr.spread(0), lambda: ag_three.pass_on(0, 1), lambda: ag_three.finish(0, 1))
-                after(i, 2, *[functools.partial(rs_four.middle, h, 0) for h in range(hops, -1, -1)], lambda: gr.spread(1))
+                after(
+                    i,
+                    2,
+                    *[functools.partial(rs_four.middle, h, 0) for h in range(hops, -1, -1)],
+                    lambda: gr.spread(1),
+                    lambda: gr.relay(0, 1),
+                )
                 after(
                     i,
                     3,
                     *[functools.partial(rs_four.hop, h, 0, total) for h in range(hops, 0, -1)],
                     lambda: gr.spread(2),
-                    lambda: layer_sum(0),
-                    lambda: layer_sum(1),
+                    lambda: gr.relay(0, 2),
+                    lambda: gr.relay(1, 1),
                 )
 
+            for h in range(hops, -1, -1):
+                rs_four.middle(h, 1)
             attn_all = attn_in[...].reshape(spans * streams * length, width)
             grads[3, :, cols : 3 * cols] = dot_tn(attn_all, flat(dkv_ref[...].reshape(-1, 2 * cols))).astype(BF)
-            for h in range(hops, -1, -1):
-                rs_four.middle(h, 1)
             grads[3, :, :cols] = dot_tn(flat(attn_in[0]), flat(dq_ref[...])).astype(BF)
             grads[3, :, 3 * cols :] = dot_tn(flat(grad_att[0]), flat(a_ref[...])).astype(BF)
             gr.start(3)
@@ -1262,30 +1306,40 @@
                 stu_out[0, m, t] = value.astype(BF)
                 ag_five.start(m)
 
+            gr.relay(1, 2)
+            gr.relay(2, 1)
+            rs_three.drain()
+            ag_two.drain()
+            ag_three.drain()
             fourth_norm(0)
             for h in range(hops, 0, -1):
                 rs_four.hop(h, 1, total)
             gr.spread(3)
+            gr.relay(2, 2)
             gr.collect(0, grad_acc)
             fourth_norm(1)
             for m in range(streams):
+                layer_sum(m)
+            gr.relay(3, 1)
+            gr.collect(1, grad_acc)
+            for m in range(streams):
                 ag_five.pass_on(0, m)
-            for m in range(streams):
-                ag_layer.pass_on(0, m)
-            gr.collect(1, grad_acc)
+            gr.relay(3, 2)
             gr.collect(2, grad_acc)
             for m in range(streams):
                 ag_five.finish(0, m)
+            for m in range(streams):
+                ag_layer.pass_on(0, m)
             gr.collect(3, grad_acc)
+            rs_layer.drain()
+            rs_four.drain()
             for m in range(streams):
                 ag_layer.finish(0, m)
             for k in range(chunks):
                 gr.finish(k)
                 gr.drain(k)
-            for item in (rs_one, rs_two, rs_three, rs_layer, rs_four, ag_rows, ag_one, ag_two, ag_three, ag_layer, ag_five):
-                item.drain()
-            for h in far_back:
-                pl.when(s + h < seq_count)(functools.partial(lambda h: id_copy(h, s + h).wait_send(), h))
+            ag_five.drain()
+            ag_layer.drain()
 
         pl.run_scoped(
             attention_on,
@@ -1444,8 +1498,10 @@
         strip_copy.wait()
         x_copy.wait()
         mine = pl.ds(pl.multiple_of(t * channels, LANES), channels)
-        spread_at = {0: 0, 1: 1, 4: 2, 6: 3} if steps == 8 and chunks >= 7 else {}
-        collect_at = {5: 0, 7: 1} if spread_at else {}
+        assert seq_count == 4 and steps == 8 and chunks == 7
+        spread_at = {0: 0, 1: 1, 4: 2, 6: 3}
+        relay_at = {2: (0, 1), 3: (1, 1), 4: (0, 2), 5: (1, 2), 6: (2, 1), 7: (2, 2)}
+        collect_at = {6: 0, 7: 1}
 
         def step_of(i):
             return seq_count - 1 - i // streams, i - i // streams * streams
@@ -1488,27 +1544,32 @@
 
             for step, k in spread_at.items():
                 pl.when(i == step)(functools.partial(gr.spread, k))
+            for step, (k, d) in relay_at.items():
+                pl.when(i == step)(functools.partial(gr.relay, k, d))
             for step, k in collect_at.items():
                 pl.when(i == step)(functools.partial(gr.collect, k, grad_acc))
 
         rs.middle(0, streams - 1)
-        waiting = list(range(len(spread_at), chunks))
-        gathered = list(range(len(collect_at), chunks))
-
-        def next_spread():
-            if waiting:
-                gr.spread(waiting.pop(0))
-
-        next_spread()
-        next_spread()
+        gr.spread(4)
+        gr.relay(3, 1)
+        gr.spread(5)
+        gr.relay(3, 2)
+        gr.relay(4, 1)
         gain_own[...] = jnp.zeros_like(gain_own)
-        for m in range(streams):
+
+        def last_norm(m):
             rs.total(m, total)
             grad_in, gain_grad = norm_back(x_own[m].astype(F32), gain_ref[...], total[...])
             out[0, m, t] = (one_ref[m] + grad_in).astype(BF)
             ag.start(m)
             gain_own[0:1] += gain_grad
-        next_spread()
+
+        last_norm(0)
+        gr.relay(4, 2)
+        gr.relay(5, 1)
+        gr.spread(6)
+        last_norm(1)
+        gr.relay(5, 2)
         gain_own[1:3] = gains_ref[...]
         gain_near[t] = gain_own[...]
 
@@ -1517,10 +1578,13 @@
 
         for j in range(4):
             pl.when(t != j)(functools.partial(lambda j: near_copy(j, t).start(), j))
-        while len(gathered) > 3 and chunks - len(gathered) < chunks - len(waiting):
-            gr.collect(gathered.pop(0), grad_acc)
+        gr.collect(2, grad_acc)
+        gr.relay(6, 1)
+        gr.collect(3, grad_acc)
         for m in range(streams):
             ag.pass_on(0, m)
+        gr.relay(6, 2)
+        gr.collect(4, grad_acc)
         for j in range(4):
             pl.when(t != j)(functools.partial(lambda j: near_copy(j, j).wait_recv(), j))
         gain_sum[...] = gain_near[0] + gain_near[1] + gain_near[2] + gain_near[3]
@@ -1536,24 +1600,24 @@
         gain_far[me] = gain_sum[:, pl.ds(pl.multiple_of(s * rows, LANES), rows)]
         for j in range(2 * seq_count):
             pl.when(me != j)(lambda: far_copy(j, me).start())
-        while waiting:
-            next_spread()
+        gr.collect(5, grad_acc)
+        rs.drain()
         for m in range(streams):
             ag.finish(0, m)
-        while gathered:
-            gr.collect(gathered.pop(0), grad_acc)
+        gr.collect(6, grad_acc)
+        for k in range(4):
+            gr.finish(k)
+            gr.drain(k)
         for j in range(2 * seq_count):
             pl.when(me != j)(lambda: far_copy(j, j).wait_recv())
         gain_out[...] = functools.reduce(jnp.add, [gain_far[j] for j in range(2 * seq_count)])
-        for k in range(chunks):
+        for k in range(4, chunks):
             gr.finish(k)
+            gr.drain(k)
         for j in range(4):
             pl.when(t != j)(lambda: near_copy(j, t).wait_send())
         for j in range(2 * seq_count):
             pl.when(me != j)(lambda: far_copy(j, me).wait_send())
-        for k in range(chunks):
-            gr.drain(k)
-        rs.drain()
         ag.drain()
 
     anywhere = pl.BlockSpec(memory_space=pl.ANY)

time: 253 us -> 249 us (0.984)
  Pallas kernels: 252 us -> 248 us
    pallas_call x1, Pallas kernels: 172 us -> 167 us  [head(): pl.pallas_call(kernel, name='head', out_shape=(jax.ShapeDtypeStruct(gathe...]
where the time goes in v8:
time: 249 us; the launch traced here: 248 us
  Pallas kernels  248 us (100%)
    pallas_call x1, Pallas kernels, head(): pl.pallas_call(kernel, name='head', out_shape=(jax.ShapeDtypeStruct(gathe...  167 us
    pallas_call x1, Pallas kernels, tail(): pl.pallas_call(kernel, name='tail', out_shape=(jax.ShapeDtypeStruct((1, s...  76.5 us

profile of v8, /device:TPU:0, one launch (start us, length us, event | category | flops | bytes accessed | tf_op | source)
XLA Modules:
  0.0 248.3 jit_solution(10151948672186498809)
XLA Ops:
  0.6 166.7 %head.1 = (bf16[1,2,4,128,512]{4,3,2,1,0:T(8,128)(2,1)}, bf16[1,2,4,128,512]{4,3,2,1,0:T(8,128)(2,1)}, f32[2,128,512]{2,1,0:T(8,128)}, f32[2,512]{1,0:T(2,128)},...) custom-call(bf16[2,4,128,512]{3,2,1,0:T(8,128)(2,1)} %bitcast.10, ...), custom_call_target="tpu_custom_call" | custom-call | tf_op jit(solution)/shard_map/head/pallas_call | solution.py:1362
  167.4 76.5 %tail.1 = (bf16[1,2,4,128,512]{4,3,2,1,0:T(8,128)(2,1)}, bf16[6,128,512]{2,1,0:T(8,128)(2,1)}, bf16[128,512]{1,0:T(8,128)(2,1)}, f32[8,128]{1,0:T(8,128)}) custom-call(bf16[1024,512]{1,0:T(8,128)(2,1)} %bitcast.13, bf16[6,512,512]{2,1,0:T(8,128)(2,1)} %fp_hbm.3, bf16[3,128,512]{2,1,0:T(8,128)(2,1)} %lp_ref.3, ...), custom_call_target="tpu_custom_call" | custom-call | tf_op jit(solution)/shard_map/tail/pallas_call | solution.py:1624
  243.9 4.3 %write_out.1 = (bf16[2,1,512,512]{3,2,1,0:T(8,128)(2,1)}, bf16[2,1,512,512]{3,2,1,0:T(8,128)(2,1)}, f32[1,128]{1,0:T(1,128)}, f32[6,128,512]{2,1,0:T(8,128)}, f3...) custom-call(bf16[1,2,4,128,512]{4,3,2,1,0:T(8,128)(2,1)} %get-tuple-, ...), custom_call_target="tpu_custom_call" | custom-call | tf_op jit(solution)/shard_map/write_out/pallas_call | solution.py:1714

commit v9 on v8

--- a/solution.py
+++ b/solution.py
@@ -892,7 +892,8 @@
     def kernel(
         x_ref, id_ref, sg_ref, fp_hbm, lp_ref, taps_ref, ag_ref, fg_ref,
         wq_ref, wk_ref, wv_ref, wo_ref, wg_hbm, wu_hbm, wd_hbm, cot_hbm,
-        stu_out, layer_out, one_out, gain_out, sum_out, lag_out, ids_out, conv_out, strip_out,
+        stu_hbm, layer_hbm, one_hbm, gain_out, sum_hbm, lag_hbm, ids_out, conv_out, strip_out,
+        stu_out, layer_out, one_out, sum_out, lag_out, store_sem,
         fp_ref, wg_ref, wu_ref, wd_ref, cot_ref, load_sem, base_ref, ids_row,
         rows_in, ids_in, cols_in, id_ext, lag_ext, part_ref, id_sem, strip_sem, conv_sem,
         attn_in, feed_in, grad_att, hid_one, hid_two, grad_two, grads, total, grad_acc,
@@ -958,6 +959,8 @@
 
         pairs = ((fp_hbm, fp_ref), (wg_hbm, wg_ref), (wu_hbm, wu_ref), (wd_hbm, wd_ref), (cot_hbm, cot_ref))
         loads = [pltpu.make_async_copy(a, b, load_sem.at[i]) for i, (a, b) in enumerate(pairs)]
+        pairs = ((stu_out, stu_hbm), (layer_out, layer_hbm), (one_out, one_hbm), (sum_out, sum_hbm), (lag_out, lag_hbm))
+        stores = [pltpu.make_async_copy(a, b, store_sem.at[i]) for i, (a, b) in enumerate(pairs)]
         for load in loads:
             load.start()
 
@@ -1082,6 +1085,7 @@
                 after(j, per + 6, lambda: first_norm(0))
 
             rs_one.start(0, 1)
+            stores[4].start()
             for k in range(count):
                 for half in range(2):
                     conv_copy(k, streams - 1, half).wait()
@@ -1318,6 +1322,7 @@
             gr.relay(2, 2)
             gr.collect(0, grad_acc)
             fourth_norm(1)
+            stores[2].start()
             for m in range(streams):
                 layer_sum(m)
             gr.relay(3, 1)
@@ -1328,6 +1333,7 @@
             gr.collect(2, grad_acc)
             for m in range(streams):
                 ag_five.finish(0, m)
+            stores[0].start()
             for m in range(streams):
                 ag_layer.pass_on(0, m)
             gr.collect(3, grad_acc)
@@ -1335,11 +1341,17 @@
             rs_four.drain()
             for m in range(streams):
                 ag_layer.finish(0, m)
-            for k in range(chunks):
+            stores[1].start()
+            for k in range(chunks - 1):
                 gr.finish(k)
                 gr.drain(k)
             ag_five.drain()
             ag_layer.drain()
+            gr.finish(chunks - 1)
+            stores[3].start()
+            gr.drain(chunks - 1)
+            for store in stores:
+                store.wait()
 
         pl.run_scoped(
             attention_on,
@@ -1374,8 +1386,14 @@
             jax.ShapeDtypeStruct((count, LANES, wide), BF),
         ),
         in_specs=[anywhere if i in (3, 12, 13, 14, 15) else spec for i, spec in enumerate(in_vmem(16))],
-        out_specs=tuple(in_vmem(7)) + (anywhere, anywhere),
+        out_specs=tuple(spec if i in (3, 6) else anywhere for i, spec in enumerate(in_vmem(9))),
         scratch_shapes=[
+            pltpu.VMEM(gathered, BF),
+            pltpu.VMEM(gathered, BF),
+            pltpu.VMEM((streams, quarter, width), F32),
+            pltpu.VMEM((chunks, rows, units), BF),
+            pltpu.VMEM((lag_order, streams, length, channels), BF),
+            pltpu.SemaphoreType.DMA((5,)),
             pltpu.VMEM(filter_proj.shape, BF),
             pltpu.VMEM(wg.shape, BF),
             pltpu.VMEM(wu.shape, BF),
@@ -1435,7 +1453,8 @@
 
     def kernel(
         gs_ref, fp_hbm, lp_ref, conv_hbm, lag_ref, ext_ref, strip_hbm, x_hbm, gain_ref, one_ref, gains_ref,
-        out, filter_out, lag_out, gain_out,
+        out_hbm, filter_hbm, lag_out, gain_out,
+        out, filter_out, out_sem, filter_sem,
         conv_ref, fp_ref, strip, x_own, conv_sem, fp_sem, strip_sem, x_sem, id_ext,
         mask, cols, left, acc, terms, grad_conv, grads, lag_ext, total, grad_acc, gather_sem,
         gain_own, gain_near, gain_sum, gain_far, near_sem, far_sem, *scratch,
@@ -1443,6 +1462,10 @@
         s, t, y, c, core, far = place()
         p = lax.axis_index("dp")
         rs_scratch, gr_scratch = scratch[:6], scratch[6:]
+        out_copy = pltpu.make_async_copy(out, out_hbm, out_sem)
+
+        def filter_copy(k):
+            return pltpu.make_async_copy(filter_out.at[k], filter_hbm.at[k], filter_sem.at[k])
 
         def conv_copy(k):
             return pltpu.make_async_copy(conv_hbm.at[k], conv_ref.at[k], conv_sem.at[k])
@@ -1479,6 +1502,7 @@
             for m in range(streams):
                 here = pl.ds(pl.multiple_of(k * length, LANES), length)
                 grad_conv[m, here] = product[m * length : (m + 1) * length]
+            pl.when(k == count - 1)(lambda: gr.spread(0))
 
         grads[count] = jnp.zeros_like(grads.at[count])
         for i in range(lag_order):
@@ -1499,9 +1523,9 @@
         x_copy.wait()
         mine = pl.ds(pl.multiple_of(t * channels, LANES), channels)
         assert seq_count == 4 and steps == 8 and chunks == 7
-        spread_at = {0: 0, 1: 1, 4: 2, 6: 3}
-        relay_at = {2: (0, 1), 3: (1, 1), 4: (0, 2), 5: (1, 2), 6: (2, 1), 7: (2, 2)}
-        collect_at = {6: 0, 7: 1}
+        spread_at = {0: 1, 2: 2, 4: 3, 6: 4}
+        relay_at = {1: (0, 1), 2: (0, 2), 3: (1, 1), 4: (1, 2), 5: (2, 1), 6: (2, 2), 7: (3, 1)}
+        collect_at = {5: 0, 7: 1}
 
         def step_of(i):
             return seq_count - 1 - i // streams, i - i // streams * streams
@@ -1550,8 +1574,6 @@
                 pl.when(i == step)(functools.partial(gr.collect, k, grad_acc))
 
         rs.middle(0, streams - 1)
-        gr.spread(4)
-        gr.relay(3, 1)
         gr.spread(5)
         gr.relay(3, 2)
         gr.relay(4, 1)
@@ -1604,21 +1626,28 @@
         rs.drain()
         for m in range(streams):
             ag.finish(0, m)
+        out_copy.start()
         gr.collect(6, grad_acc)
         for k in range(4):
             gr.finish(k)
+            filter_copy(k).start()
             gr.drain(k)
         for j in range(2 * seq_count):
             pl.when(me != j)(lambda: far_copy(j, j).wait_recv())
         gain_out[...] = functools.reduce(jnp.add, [gain_far[j] for j in range(2 * seq_count)])
         for k in range(4, chunks):
             gr.finish(k)
+            if k < count:
+                filter_copy(k).start()
             gr.drain(k)
         for j in range(4):
             pl.when(t != j)(lambda: near_copy(j, t).wait_send())
         for j in range(2 * seq_count):
             pl.when(me != j)(lambda: far_copy(j, me).wait_send())
         ag.drain()
+        out_copy.wait()
+        for k in range(count):
+            filter_copy(k).wait()
 
     anywhere = pl.BlockSpec(memory_space=pl.ANY)
     return pl.pallas_call(
@@ -1631,8 +1660,12 @@
             jax.ShapeDtypeStruct((gain_rows, rows), F32),
         ),
         in_specs=[anywhere if i in (1, 3, 6, 7) else spec for i, spec in enumerate(in_vmem(11))],
-        out_specs=tuple(in_vmem(4)),
+        out_specs=(anywhere, anywhere) + tuple(in_vmem(2)),
         scratch_shapes=[
+            pltpu.VMEM((1, streams, 4, quarter, width), BF),
+            pltpu.VMEM((count, rows, width), BF),
+            pltpu.SemaphoreType.DMA,
+            pltpu.SemaphoreType.DMA((count,)),
             pltpu.VMEM(conv.shape, BF),
             pltpu.VMEM(filter_proj.shape, BF),
             pltpu.VMEM(strip_back.shape, BF),

time: 249 us -> 246 us (0.988)
  Pallas kernels: 248 us -> 245 us
where the time goes in v9:
time: 246 us; the launch traced here: 245 us
  Pallas kernels  245 us (100%)
    pallas_call x1, Pallas kernels, head(): pl.pallas_call(kernel, name='head', out_shape=(jax.ShapeDtypeStruct(gathe...  166 us
    pallas_call x1, Pallas kernels, tail(): pl.pallas_call(kernel, name='tail', out_shape=(jax.ShapeDtypeStruct((1, s...  74.1 us

profile of v9, /device:TPU:0, one launch (start us, length us, event | category | flops | bytes accessed | tf_op | source)
XLA Modules:
  0.0 245.4 jit_solution(13042666528944104427)
XLA Ops:
  0.6 166.2 %head.1 = (bf16[1,2,4,128,512]{4,3,2,1,0:T(8,128)(2,1)}, bf16[1,2,4,128,512]{4,3,2,1,0:T(8,128)(2,1)}, f32[2,128,512]{2,1,0:T(8,128)}, f32[2,512]{1,0:T(2,128)},...) custom-call(bf16[2,4,128,512]{3,2,1,0:T(8,128)(2,1)} %bitcast.10, ...), custom_call_target="tpu_custom_call" | custom-call | tf_op jit(solution)/shard_map/head/pallas_call | solution.py:1374
  166.8 74.1 %tail.1 = (bf16[1,2,4,128,512]{4,3,2,1,0:T(8,128)(2,1)}, bf16[6,128,512]{2,1,0:T(8,128)(2,1)}, bf16[128,512]{1,0:T(8,128)(2,1)}, f32[8,128]{1,0:T(8,128)}) custom-call(bf16[1024,512]{1,0:T(8,128)(2,1)} %bitcast.13, bf16[6,512,512]{2,1,0:T(8,128)(2,1)} %fp_hbm.3, bf16[3,128,512]{2,1,0:T(8,128)(2,1)} %lp_ref.3, ...), custom_call_target="tpu_custom_call" | custom-call | tf_op jit(solution)/shard_map/tail/pallas_call | solution.py:1653
  240.9 4.3 %write_out.1 = (bf16[2,1,512,512]{3,2,1,0:T(8,128)(2,1)}, bf16[2,1,512,512]{3,2,1,0:T(8,128)(2,1)}, f32[1,128]{1,0:T(1,128)}, f32[6,128,512]{2,1,0:T(8,128)}, f3...) custom-call(bf16[1,2,4,128,512]{4,3,2,1,0:T(8,128)(2,1)} %get-tuple-, ...), custom_call_target="tpu_custom_call" | custom-call | tf_op jit(solution)/shard_map/write_out/pallas_call | solution.py:1747
